TPU v7x, 32 devices: a whole 2x2x4 slice. The times are simulated.
32 devices in a mesh: dp: 16 (over z, y, x), tensor: 2 (over core).
Axes of the slice: x: 2, y: 2, z: 4, core: 2. Of those that a mesh axis runs over, the one named last changes fastest.
Arguments:
- tokens: bfloat16 [16384, 768], P(('dp', 'tensor')), may hold values from -6 to 6
- lengths: int32 [16], P('dp'), may hold values from 256 to 1024, as said below
- qkv_weight: bfloat16 [3, 768, 768], P(None, 'dp', 'tensor'), may hold values from -0.21875 to 0.21875
- qv_bias: bfloat16 [2, 768], P(None, ('tensor', 'dp')), may hold values from -3 to 3
- out_weight: bfloat16 [768, 768], P('tensor', 'dp'), may hold values from -0.4375 to 0.4375
- in_weight: bfloat16 [2, 768, 3072], P(None, 'dp', 'tensor'), may hold values from -0.21875 to 0.21875
- in_bias: bfloat16 [2, 3072], P(None, ('tensor', 'dp')), may hold values from -3 to 3
- down_weight: bfloat16 [3072, 768], P('tensor', 'dp'), may hold values from -0.21875 to 0.21875
- norm_gains: float32 [2, 768], P(None, ('dp', 'tensor')), may hold values from 0.1 to 1.9
- offsets: float32 [4, 768], P(None, ('dp', 'tensor')), may hold values from -3 to 3
- cotangent: bfloat16 [16384, 768], P(('dp', 'tensor')), may hold values from -6 to 6
Outputs:
- output: bfloat16 [16384, 768], P(('dp', 'tensor'))
- grad_tokens: float32 [16384, 768], P(('dp', 'tensor'))
- grad_qkv_weight: float32 [3, 768, 768], P(None, 'dp', 'tensor')
- grad_qv_bias: float32 [2, 768], P(None, ('tensor', 'dp'))
- grad_out_weight: float32 [768, 768], P('tensor', 'dp')
- grad_in_weight: float32 [2, 768, 3072], P(None, 'dp', 'tensor')
- grad_in_bias: float32 [2, 3072], P(None, ('tensor', 'dp'))
- grad_down_weight: float32 [3072, 768], P('tensor', 'dp')
- grad_norm_gains: float32 [2, 768], P(None, ('dp', 'tensor'))
- grad_offsets: float32 [4, 768], P(None, ('dp', 'tensor'))
Inputs may be any that keep to these rules, and one draw needn't show every extreme that they name: `lengths`: the number of valid leading slots of each sequence; some sequence is full and some holds exactly 256.
All inputs are finite; a program needn't handle non-finite values.
Results may differ from a plain program's by a relative error of at most 0.02.
Values may be sent and summed in bfloat16 or wider, within the bound.
A program may use at most 128 MiB of HBM per device.

v0:
```python
import jax
import jax.numpy as jnp
from jax import lax
from jax.sharding import PartitionSpec as P

HEAD = 64


norm_epsilon = 1e-06


def norm_forward(values, gain_row, shift_row):
    centred = values - jnp.mean(values, axis=-1, keepdims=True)
    variance = jnp.mean(centred * centred, axis=-1, keepdims=True)
    inv_scale = lax.rsqrt(variance + norm_epsilon)
    unit_vals = centred * inv_scale
    return (unit_vals * gain_row + shift_row, unit_vals, inv_scale)


def norm_backward(grad_out, unit_vals, inv_scale, gain_row):
    grad_unit = grad_out * gain_row
    inner_term = (
        grad_unit
        - jnp.mean(grad_unit, axis=-1, keepdims=True)
        - unit_vals * jnp.mean(grad_unit * unit_vals, axis=-1, keepdims=True)
    )
    return (
        inner_term * inv_scale,
        jnp.sum(grad_out * unit_vals, axis=0),
        jnp.sum(grad_out, axis=0),
    )


def score_block(query_block, first_row, key_heads, slopes, key_valid):
    block_size = query_block.shape[0]
    heads_here = slopes.shape[0]
    query_heads = query_block.reshape(block_size, heads_here, HEAD)
    raw_scores = jnp.einsum(
        "qhc,khc->hqk", query_heads, key_heads, preferred_element_type=jnp.float32
    )
    query_pos = first_row + lax.iota(jnp.int32, block_size)
    key_pos = lax.iota(jnp.int32, key_heads.shape[0])
    distance = jnp.abs(query_pos[:, None] - key_pos[None, :]).astype(jnp.float32)
    scores = 0.125 * raw_scores - slopes[:, None, None] * distance[None, :, :]
    return (jnp.where(key_valid[None, None, :], scores, -1e30), query_heads)


def attend(queries, key_rows, value_rows, slopes, key_valid):
    slot_count, width_here = queries.shape
    heads_here = width_here // HEAD
    block_size = min(512, slot_count)
    key_heads = key_rows.reshape(slot_count, heads_here, HEAD)
    value_heads = value_rows.reshape(slot_count, heads_here, HEAD)

    def one_block(first_row):
        query_block = lax.dynamic_slice_in_dim(queries, first_row, block_size, 0)
        scores, query_heads = score_block(query_block, first_row, key_heads, slopes, key_valid)
        row_max = jnp.max(scores, axis=-1, keepdims=True)
        exp_scores = jnp.exp(scores - row_max)
        row_total = jnp.sum(exp_scores, axis=-1, keepdims=True)
        weights = (exp_scores / row_total).astype(jnp.bfloat16)
        mixed_block = jnp.einsum(
            "hqk,khc->qhc", weights, value_heads, preferred_element_type=jnp.float32
        )
        return (
            mixed_block.reshape(block_size, width_here).astype(jnp.bfloat16),
            (row_max + jnp.log(row_total))[..., 0],
        )

    first_rows = lax.iota(jnp.int32, slot_count // block_size) * block_size
    mixed_heads, logsum = lax.map(one_block, first_rows)
    return (mixed_heads.reshape(slot_count, width_here), logsum)


def attend_back(queries, key_rows, value_rows, grad_mixed, logsum, slopes, key_valid):
    slot_count, width_here = queries.shape
    heads_here = width_here // HEAD
    block_size = min(512, slot_count)
    key_heads = key_rows.reshape(slot_count, heads_here, HEAD)
    value_heads = value_rows.reshape(slot_count, heads_here, HEAD)

    def one_block(running, block_item):
        grad_keys, grad_values = running
        first_row, block_lse = block_item
        query_block = lax.dynamic_slice_in_dim(queries, first_row, block_size, 0)
        grad_block = lax.dynamic_slice_in_dim(grad_mixed, first_row, block_size, 0)
        scores, query_heads = score_block(query_block, first_row, key_heads, slopes, key_valid)
        probs = jnp.exp(scores - block_lse[..., None])
        grad_heads = grad_block.reshape(block_size, heads_here, HEAD)
        grad_probs = jnp.einsum(
            "qhc,khc->hqk", grad_heads, value_heads, preferred_element_type=jnp.float32
        )
        row_dot = jnp.sum(probs * grad_probs, axis=-1, keepdims=True)
        grad_scores = (probs * (grad_probs - row_dot)).astype(jnp.bfloat16)
        grad_query = 0.125 * jnp.einsum(
            "hqk,khc->qhc", grad_scores, key_heads, preferred_element_type=jnp.float32
        )
        grad_keys = grad_keys + 0.125 * jnp.einsum(
            "hqk,qhc->khc", grad_scores, query_heads, preferred_element_type=jnp.float32
        )
        grad_values = grad_values + jnp.einsum(
            "hqk,qhc->khc",
            probs.astype(jnp.bfloat16),
            grad_heads,
            preferred_element_type=jnp.float32,
        )
        return ((grad_keys, grad_values), grad_query.reshape(block_size, width_here))

    first_rows = lax.iota(jnp.int32, slot_count // block_size) * block_size
    zero_grads = jnp.zeros((slot_count, heads_here, HEAD), jnp.float32)
    (grad_keys, grad_values), grad_queries = lax.scan(
        one_block, (zero_grads, zero_grads), (first_rows, logsum)
    )
    return (
        grad_queries.reshape(slot_count, width_here),
        grad_keys.reshape(slot_count, width_here),
        grad_values.reshape(slot_count, width_here),
    )


def per_device(
    tokens,
    lengths,
    qkv_weight,
    qv_bias,
    out_weight,
    in_weight,
    in_bias,
    down_weight,
    norm_gains,
    offsets,
    cotangent,
):
    row_count = tokens.shape[0]
    pieces = lax.axis_size("tensor")
    piece_index = lax.axis_index("tensor")
    slot_count = row_count * pieces
    length = lengths[0]
    heads_here = qkv_weight.shape[2] // HEAD
    head_ids = (piece_index * heads_here + lax.iota(jnp.int32, heads_here)).astype(jnp.float32)
    slopes = jnp.exp2(-8.0 * (head_ids + 1.0) / (heads_here * pieces))
    key_valid = lax.iota(jnp.int32, slot_count) < length
    row_valid = (piece_index * row_count + lax.iota(jnp.int32, row_count) < length).astype(
        jnp.float32
    )[:, None]
    gains, shift_rows = (
        lax.all_gather(norm_gains, ("dp", "tensor"), axis=1, tiled=True),
        lax.all_gather(offsets, ("dp", "tensor"), axis=1, tiled=True),
    )

    def fetch_weights():
        return (
            lax.all_gather(qkv_weight, "dp", axis=1, tiled=True),
            lax.all_gather(qv_bias, "dp", axis=1, tiled=True),
            lax.all_gather(out_weight, "dp", axis=1, tiled=True),
            lax.all_gather(in_weight, "dp", axis=1, tiled=True),
            lax.all_gather(in_bias, "dp", axis=1, tiled=True),
            lax.all_gather(down_weight, "dp", axis=1, tiled=True),
        )

    def attention_inputs(whole_qkv, whole_bqv):
        gathered = lax.all_gather(tokens, "tensor", axis=0, tiled=True)
        projected = jnp.einsum(
            "sd,kdc->ksc", gathered, whole_qkv, preferred_element_type=jnp.float32
        )
        queries = (projected[0] + whole_bqv[0].astype(jnp.float32)).astype(jnp.bfloat16)
        key_rows = projected[1].astype(jnp.bfloat16)
        value_rows = (projected[2] + whole_bqv[1].astype(jnp.float32)).astype(jnp.bfloat16)
        mixed_heads, logsum = attend(queries, key_rows, value_rows, slopes, key_valid)
        return (gathered, queries, key_rows, value_rows, mixed_heads, logsum)

    def feed_inputs(whole_in, whole_bin, attended_low):
        gathered_ff = lax.all_gather(attended_low, "tensor", axis=0, tiled=True)
        pre_acts = jnp.einsum(
            "sd,kdc->ksc", gathered_ff, whole_in, preferred_element_type=jnp.float32
        )
        pre_acts = pre_acts + whole_bin.astype(jnp.float32)[:, None, :]
        hidden = (jax.nn.gelu(pre_acts[0], approximate=False) * pre_acts[1]).astype(jnp.bfloat16)
        return (gathered_ff, pre_acts, hidden)

    whole_qkv, whole_bqv, whole_out, whole_in, whole_bin, whole_down = fetch_weights()
    gathered, queries, key_rows, value_rows, mixed_heads, logsum = attention_inputs(
        whole_qkv, whole_bqv
    )
    attn_part = jnp.dot(mixed_heads, whole_out, preferred_element_type=jnp.float32)
    attn_total = lax.psum_scatter(
        attn_part.astype(jnp.bfloat16), "tensor", scatter_dimension=0, tiled=True
    ).astype(jnp.float32)
    first_in = tokens.astype(jnp.float32) + attn_total + shift_rows[0]
    attended, unit_one, scale_one = norm_forward(first_in, gains[0], shift_rows[1])
    attended_low = attended.astype(jnp.bfloat16)
    gathered_ff, pre_acts, hidden = feed_inputs(whole_in, whole_bin, attended_low)
    ff_part = jnp.dot(hidden, whole_down, preferred_element_type=jnp.float32)
    ff_total = lax.psum_scatter(
        ff_part.astype(jnp.bfloat16), "tensor", scatter_dimension=0, tiled=True
    ).astype(jnp.float32)
    second_in = attended + ff_total + shift_rows[2]
    final_norm, unit_two, scale_two = norm_forward(second_in, gains[1], shift_rows[3])
    output = (final_norm * row_valid).astype(jnp.bfloat16)
    grad_final = cotangent.astype(jnp.float32) * row_valid
    grad_second, grad_gain_two, grad_shift_two = norm_backward(
        grad_final, unit_two, scale_two, gains[1]
    )
    grad_bdown = jnp.sum(grad_second, axis=0)
    whole_qkv, whole_bqv, whole_out, whole_in, whole_bin, whole_down = fetch_weights()
    gathered_ff, pre_acts, hidden = feed_inputs(whole_in, whole_bin, attended_low)
    grad_ff_rows = lax.all_gather(grad_second.astype(jnp.bfloat16), "tensor", axis=0, tiled=True)
    grad_down = jnp.einsum("sf,sd->fd", hidden, grad_ff_rows, preferred_element_type=jnp.float32)
    grad_hidden = jnp.einsum(
        "sd,fd->sf", grad_ff_rows, whole_down, preferred_element_type=jnp.float32
    )
    pullback = jax.vjp(
        lambda gate_pre, up_pre: jax.nn.gelu(gate_pre, approximate=False) * up_pre,
        pre_acts[0],
        pre_acts[1],
    )[1]
    grad_gate, grad_up = pullback(grad_hidden)
    grad_pre = jnp.stack([grad_gate, grad_up]).astype(jnp.bfloat16)
    grad_bin = jnp.sum(grad_pre, axis=1, dtype=jnp.float32)
    grad_in = jnp.einsum("sd,ksc->kdc", gathered_ff, grad_pre, preferred_element_type=jnp.float32)
    ff_back = jnp.einsum("ksc,kdc->sd", grad_pre, whole_in, preferred_element_type=jnp.float32)
    grad_attended = grad_second + lax.psum_scatter(
        ff_back.astype(jnp.bfloat16), "tensor", scatter_dimension=0, tiled=True
    ).astype(jnp.float32)
    grad_first, grad_gain_one, grad_shift_one = norm_backward(
        grad_attended, unit_one, scale_one, gains[0]
    )
    grad_bout = jnp.sum(grad_first, axis=0)
    gathered, queries, key_rows, value_rows, mixed_heads, logsum = attention_inputs(
        whole_qkv, whole_bqv
    )
    grad_attn_rows = lax.all_gather(grad_first.astype(jnp.bfloat16), "tensor", axis=0, tiled=True)
    grad_out = jnp.einsum(
        "sc,sd->cd", mixed_heads, grad_attn_rows, preferred_element_type=jnp.float32
    )
    grad_mixed = jnp.einsum(
        "sd,cd->sc", grad_attn_rows, whole_out, preferred_element_type=jnp.float32
    ).astype(jnp.bfloat16)
    grad_queries, grad_keys, grad_values = attend_back(
        queries, key_rows, value_rows, grad_mixed, logsum, slopes, key_valid
    )
    grad_qkv = jnp.stack([grad_queries, grad_keys, grad_values]).astype(jnp.bfloat16)
    grad_wqkv = jnp.einsum("sd,ksc->kdc", gathered, grad_qkv, preferred_element_type=jnp.float32)
    grad_bqv = jnp.stack(
        [
            jnp.sum(grad_qkv[0], axis=0, dtype=jnp.float32),
            jnp.sum(grad_qkv[2], axis=0, dtype=jnp.float32),
        ]
    )
    input_back = jnp.einsum("ksc,kdc->sd", grad_qkv, whole_qkv, preferred_element_type=jnp.float32)
    grad_tokens = grad_first + lax.psum_scatter(
        input_back.astype(jnp.bfloat16), "tensor", scatter_dimension=0, tiled=True
    ).astype(jnp.float32)
    shard_wqkv, shard_bqv, shard_out, shard_in, shard_bin, shard_down = (
        lax.psum_scatter(grad_wqkv, "dp", scatter_dimension=1, tiled=True),
        lax.psum_scatter(grad_bqv, "dp", scatter_dimension=1, tiled=True),
        lax.psum_scatter(grad_out, "dp", scatter_dimension=1, tiled=True),
        lax.psum_scatter(grad_in, "dp", scatter_dimension=1, tiled=True),
        lax.psum_scatter(grad_bin, "dp", scatter_dimension=1, tiled=True),
        lax.psum_scatter(grad_down, "dp", scatter_dimension=1, tiled=True),
    )
    gain_grads = jnp.stack([grad_gain_one, grad_gain_two])
    offset_grads = jnp.stack([grad_bout, grad_shift_one, grad_bdown, grad_shift_two])
    shard_gains, shard_offsets = (
        lax.psum_scatter(gain_grads, ("dp", "tensor"), scatter_dimension=1, tiled=True),
        lax.psum_scatter(offset_grads, ("dp", "tensor"), scatter_dimension=1, tiled=True),
    )
    return (
        output,
        grad_tokens,
        shard_wqkv,
        shard_bqv,
        shard_out,
        shard_in,
        shard_bin,
        shard_down,
        shard_gains,
        shard_offsets,
    )


def solution(mesh):
    placed = (
        P(("dp", "tensor"), None),
        P("dp"),
        P(None, "dp", "tensor"),
        P(None, ("tensor", "dp")),
        P("tensor", "dp"),
        P(None, "dp", "tensor"),
        P(None, ("tensor", "dp")),
        P("tensor", "dp"),
        P(None, ("dp", "tensor")),
        P(None, ("dp", "tensor")),
        P(("dp", "tensor"), None),
    )
    return jax.shard_map(
        per_device,
        mesh=mesh,
        in_specs=placed,
        out_specs=(
            P(("dp", "tensor"), None),
            P(("dp", "tensor"), None),
            P(None, "dp", "tensor"),
            P(None, ("tensor", "dp")),
            P("tensor", "dp"),
            P(None, "dp", "tensor"),
            P(None, ("tensor", "dp")),
            P("tensor", "dp"),
            P(None, ("dp", "tensor")),
            P(None, ("dp", "tensor")),
        ),
        check_vma=False,
    )
```

profile of v0, /device:TPU:0, one launch (start us, length us, event | category | flops | bytes accessed | tf_op | source)
XLA Modules:
  0.0 1312.7 jit_solution(11390183064277286681)
XLA Ops:
  8.7 42.6 %all-gather = bf16[16,24,2]{1,2,0:T(2,128)(2,1)S(1)} all-gather(bf16[1,24,2]{1,2,0:T(2,128)(2,1)} %bitcast.307), channel_id=1, replica_groups=mesh['dp'=16,'tensor'=2] {'dp'}, dimensions={0}, use_global_device_ids=true | all-gather | bytes 1632 | tf_op jit(solution)/shard_map/all_gather | solution.py:154
  51.5 42.9 %all_gather.47 = bf16[384,768]{0,1:T(8,128)(2,1)} all-gather(bf16[384,48]{0,1:T(8,128)(2,1)} %param.21), channel_id=1, replica_groups=mesh['dp'=16,'tensor'=2] {'dp'}, dimensions={1}, use_global_device_ids=true | all-gather | bytes 626688 | tf_op jit(solution)/shard_map/all_gather | solution.py:155
  101.8 45.8 %while.39 = (s32[]{:T(128)}, bf16[2,512,384]{2,1,0:T(8,128)(2,1)}, s32[2]{0:T(128)S(1)}, bf16[1024,384]{0,1:T(8,128)(2,1)S(1)}, bf16[1024,6,64]{0,2,1:T(8,128)(2...) while((s32[]{:T(128)}, bf16[2,512,384]{2,1,0:T(8,128)(2,1)}, ...), condition=%wide.region_3.4_spmd.clone, body=%wide.region_0.3_spmd.clone.sunk | while | flops 832244224 | bytes 40401184 | solution.py:71
  106.3 10.3 fusion.142
  116.6 6.9 fusion.143
  129.2 10.3 fusion.142
  139.4 6.9 fusion.143
  151.1 39.1 %all-gather.2 = f32[32,24,2]{1,2,0:T(2,128)S(1)} all-gather(f32[1,24,2]{1,2,0:T(2,128)S(1)} %bitcast.306), channel_id=1, replica_groups=mesh['dp'=16,'tensor'=2] {'dp','tensor'}, dimensions={0}, use_global_device_ids=true | all-gather | bytes 6336 | tf_op jit(solution)/shard_map/all_gather | solution.py:147
  190.3 37.3 %all-gather.1 = f32[32,24,4]{1,2,0:T(4,128)S(1)} all-gather(f32[1,24,4]{1,2,0:T(4,128)S(1)} %bitcast.305), channel_id=1, replica_groups=mesh['dp'=16,'tensor'=2] {'dp','tensor'}, dimensions={0}, use_global_device_ids=true | all-gather | bytes 12672 | tf_op jit(solution)/shard_map/all_gather | solution.py:148
  233.6 37.3 %all-gather.3 = bf16[16,96,2]{1,2,0:T(2,128)(2,1)S(1)} all-gather(bf16[1,96,2]{1,2,0:T(2,128)(2,1)S(1)} %bitcast.308), channel_id=1, replica_groups=mesh['dp'=16,'tensor'=2] {'dp'}, dimensions={0}, use_global_device_ids=true | all-gather | bytes 6528 | tf_op jit(solution)/shard_map/all_gather | solution.py:157
  271.0 52.2 %all-gather.18.cloned.1.call-done = bf16[2,768,1536]{2,1,0:T(8,128)(2,1)} async-done(((bf16[2,48,1536]{2,1,0:T(8,128)(2,1)}), bf16[2,768,1536]{2,1,0:T(8,128)(2,1)}) %all-gather.18.cloned.1.call-update) | async-done | bytes 4718608 | tf_op jit(solution)/shard_map/all_gather | solution.py:156
  323.2 7.4 add_bitcast_fusion
  335.1 14.8 %multiply_convert_fusion.2 = (bf16[1024,1536]{1,0:T(8,128)(2,1)}, f32[1024,1536]{1,0:T(8,128)}) fusion(f32[2,1024,1536]{2,1,0:T(8,128)S(1)} %add_bitcast_fusion), kind=kLoop, calls=%fused_computation.79 | loop fusion | flops 103809024 | bytes 22020096 | tf_op jit(solution)/shard_map/convert_element_type | solution.py:178
  349.9 36.8 %all-gather.20.cloned.1.call-done = bf16[1536,768]{0,1:T(8,128)(2,1)} async-done(((bf16[1536,48]{0,1:T(8,128)(2,1)}), bf16[1536,768]{0,1:T(8,128)(2,1)}) %all-gather.20.cloned.1.call-update) | async-done | bytes 2359312 | tf_op jit(solution)/shard_map/all_gather | solution.py:158
  393.9 6.8 reduce-scatter.15.cloned.1.call-done
  407.1 11.0 all-gather.22.cloned.1.call-done
  418.1 10.4 fusion.56
  431.1 8.6 bitcast_convert_fusion.1
  439.8 10.3 reduce-scatter.17.cloned.1.call-done
  458.2 34.3 %while.40 = (s32[]{:T(128)}, bf16[2,512,384]{2,1,0:T(8,128)(2,1)}, f32[2,6,512]{2,1,0:T(8,128)S(1)}, s32[2]{0:T(128)S(1)}, bf16[1024,384]{0,1:T(8,128)(2,1)S(1)}...) while((s32[]{:T(128)}, bf16[2,512,384]{2,1,0:T(8,128)(2,1)}, ...), condition=%wide.region_18.19_spmd.clone, body=%wide.region_15.18_spmd.clone.sunk | while | flops 863697408 | bytes 50975008 | solution.py:71
  501.3 68.6 %while.41 = (s32[]{:T(128)}, f32[1024,6,64]{0,2,1:T(8,128)S(1)}, f32[1024,6,64]{0,2,1:T(8,128)}, bf16[2,512,384]{1,2,0:T(8,128)(2,1)}, s32[2]{0:T(128)S(1)}, /*i...) while((s32[]{:T(128)}, f32[1024,6,64]{0,2,1:T(8,128)S(1)}, ...), condition=%wide.region_21.22_spmd.clone, body=%wide.region_19.21_spmd.clone.sunk | while | flops 2051799552 | bytes 137763632 | solution.py:111
  509.5 6.4 fusion.160
  515.9 8.1 multiply_reduce_fusion.9
  543.8 6.4 fusion.160
  550.2 8.0 multiply_reduce_fusion.9
  579.9 10.1 convolution_bitcast_fusion
  590.0 15.0 %copy.72 = f32[2,768,1536]{2,0,1:T(2,128)} copy(f32[2,768,1536]{1,2,0:T(8,128)} %convolution_bitcast_fusion) | data formatting | bytes 18874368 | tf_op jit(solution)/shard_map/sd,ksc->kdc/transpose | solution.py:220
  627.2 43.2 %all-reduce.5 = (f32[2,768]{1,0:T(2,128)S(1)}, f32[4,768]{1,0:T(4,128)S(1)}) all-reduce(f32[2,768]{1,0:T(2,128)S(1)} %pad_maximum_fusion.7, f32[4,768]{1,0:T(4,128)S(1)} %pad_maximum_fusion.6), channel_id=12, replica_groups=mesh['dp'=16,'tensor'=2] {'dp','tensor'}, use_global_device_ids=true, to_apply=%region_34.35.clone | all-reduce | flops 4608 | bytes 36864
  671.9 42.8 %all-reduce.1 = f32[2,384]{1,0:T(2,128)S(1)} all-reduce(f32[2,384]{1,0:T(2,128)S(1)} %pad_maximum_fusion.8), channel_id=7, replica_groups=mesh['dp'=16,'tensor'=2] {'dp'}, use_global_device_ids=true, to_apply=%region_26.27.clone | all-reduce | flops 768 | bytes 6144
  717.8 315.9 %all-reduce.9.cloned.1.call-done = (f32[3,768,384]{2,0,1:T(4,128)}, f32[2,768,1536]{2,0,1:T(2,128)}) async-done(((f32[3,768,384]{2,0,1:T(4,128)}, f32[2,768,1536]{2,0,1:T(2,128)}), (f32[3,768,384]{2,0,1:T(4,128)}, f32[2,768,1536]{2,0,1:T(2,128)})) %all-reduce.9.cloned.1.call-update) | async-done | bytes 12976144
  1037.5 125.4 %reduce-scatter.21.cloned.1.call-done = f32[384,48]{0,1:T(8,128)} async-done(((f32[384,768]{0,1:T(8,128)}), f32[384,48]{0,1:T(8,128)}) %reduce-scatter.21.cloned.1.call-update) | async-done | bytes 73744 | tf_op jit(solution)/shard_map/reduce_scatter | solution.py:257
  1162.9 143.1 %reduce-scatter.23.cloned.1.call-done = f32[1536,48]{0,1:T(8,128)} async-done(((f32[1536,768]{0,1:T(8,128)}), f32[1536,48]{0,1:T(8,128)}) %reduce-scatter.23.cloned.1.call-update) | async-done | bytes 294928 | tf_op jit(solution)/shard_map/reduce_scatter | solution.py:260
  (298 shorter events, 167.5 us)
Async XLA Ops:
  7.2 87.3 %all-gather.14.cloned.1.call-start = ((), (), s32[]{:S(2)}) async-start(), calls=%async_computation.8 | async-start | bytes 2359296 | tf_op jit(solution)/shard_map/all_gather | solution.py:162
  7.9 86.6 %all-gather.12.cloned.1.call-start = ((), (), s32[]{:S(2)}) async-start(), calls=%async_computation.7 | async-start | bytes 1880064 | tf_op jit(solution)/shard_map/all_gather | solution.py:153
  8.7 219.1 %reduce-scatter.13.cloned.1.call-start = ((), (), s32[]{:S(2)}) async-start(), calls=%async_computation.9 | async-start | bytes 2359296 | tf_op jit(solution)/shard_map/reduce_scatter | solution.py:186
  116.6 7.1 copy-start.24
  139.4 7.1 copy-start.24
  147.5 42.8 %copy-start.37 = (f32[4,24]{1,0:T(4,128)S(1)}, f32[4,24]{1,0:T(4,128)}, u32[]{:S(2)}) copy-start(f32[4,24]{1,0:T(4,128)} %param.26) | copy-start | bytes 1156
  147.5 80.3 %copy-start.3 = (bf16[512,768]{1,0:T(8,128)(2,1)S(1)}, bf16[512,768]{1,0:T(8,128)(2,1)}, u32[]{:S(2)}) copy-start(bf16[512,768]{1,0:T(8,128)(2,1)} %param.17) | copy-start | bytes 2359300
  151.1 119.9 %all-gather.16.cloned.1.call-start = ((), (), s32[]{:S(2)}) async-start(), calls=%async_computation.10 | async-start | bytes 2359296 | tf_op jit(solution)/shard_map/all_gather | solution.py:173
  232.3 90.8 %all-gather.18.cloned.1.call-start = ((), (), s32[]{:S(2)}) async-start(), calls=%async_computation.11 | async-start | bytes 5013504 | tf_op jit(solution)/shard_map/all_gather | solution.py:156
  232.9 153.8 %all-gather.20.cloned.1.call-start = ((), (), s32[]{:S(2)}) async-start(), calls=%async_computation.12 | async-start | bytes 2506752 | tf_op jit(solution)/shard_map/all_gather | solution.py:158
  233.5 167.2 %reduce-scatter.15.cloned.1.call-start = ((), (), s32[]{:S(2)}) async-start(), calls=%async_computation.13 | async-start | bytes 2359296 | tf_op jit(solution)/shard_map/reduce_scatter | solution.py:194
  393.1 9.8 copy-start.13
  393.1 24.9 %all-gather.22.cloned.1.call-start = ((), (), s32[]{:S(2)}) async-start(), calls=%async_computation.14 | async-start | bytes 2359296 | tf_op jit(solution)/shard_map/all_gather | solution.py:207
  406.8 43.2 %reduce-scatter.17.cloned.1.call-start = ((), (), s32[]{:S(2)}) async-start(), calls=%async_computation.15 | async-start | bytes 2359296 | tf_op jit(solution)/shard_map/reduce_scatter | solution.py:222
  439.7 58.3 %all-gather.24.cloned.1.call-start = ((), (), s32[]{:S(2)}) async-start(), calls=%async_computation.16 | async-start | bytes 2359296 | tf_op jit(solution)/shard_map/all_gather | solution.py:232
  457.0 168.7 %reduce-scatter.25.cloned.1.call-start = ((), (), s32[]{:S(2)}) async-start(), calls=%async_computation.20 | async-start | bytes 835584
  497.7 217.7 %reduce-scatter.19.cloned.1.call-start = ((), (), s32[]{:S(2)}) async-start(), calls=%async_computation.17 | async-start | bytes 2359296 | tf_op jit(solution)/shard_map/reduce_scatter | solution.py:251
  501.3 6.6 copy-start.27
  501.3 6.6 copy-start.41
  509.5 6.4 copy-start.6
  509.5 6.4 copy-start.29
  535.6 6.6 copy-start.27
  535.6 6.6 copy-start.41
  543.8 6.4 copy-start.6
  543.8 6.4 copy-start.29
  543.8 6.4 copy-start.36
  571.9 7.5 copy-start.22
  579.4 454.3 %all-reduce.9.cloned.1.call-start = ((), (), s32[]{:S(2)}) async-start(), calls=%async_computation.21 | async-start | bytes 28311552
  613.2 549.7 %reduce-scatter.21.cloned.1.call-start = ((), (), s32[]{:S(2)}) async-start(), calls=%async_computation.18 | async-start | bytes 1253376 | tf_op jit(solution)/shard_map/reduce_scatter | solution.py:257
  617.2 688.8 %reduce-scatter.23.cloned.1.call-start = ((), (), s32[]{:S(2)}) async-start(), calls=%async_computation.19 | async-start | bytes 5013504 | tf_op jit(solution)/shard_map/reduce_scatter | solution.py:260
  623.1 48.6 %copy-start.15 = (bf16[2,512,384]{2,1,0:T(8,128)(2,1)S(1)}, bf16[2,512,384]{2,1,0:T(8,128)(2,1)}, u32[]{:S(2)}) copy-start(bf16[2,512,384]{2,1,0:T(8,128)(2,1)} %copy-done.14) | copy-start | bytes 2359300
  623.1 92.3 %copy-start.10 = (f32[512,768]{1,0:T(8,128)S(1)}, f32[512,768]{1,0:T(8,128)}, u32[]{:S(2)}) copy-start(f32[512,768]{1,0:T(8,128)} %copy-done.9) | copy-start | bytes 4718596
  (40 other events, 120.7 us)
Sparse Core Ops, SparseCore 0:
  9.5 12.5 all-gather.13
  24.8 62.7 all-gather.11
  151.2 7.5 reduce-scatter.12
  232.5 7.2 all-gather.15
  242.3 80.8 all-gather.17
  325.8 60.8 all-gather.19
  393.2 7.3 reduce-scatter.14
  407.0 11.0 all-gather.21
  439.8 10.2 reduce-scatter.16
  457.1 11.0 all-gather.23
  497.8 125.2 reduce-scatter.24
  625.2 8.0 reduce-scatter.18
  639.7 393.9 all-reduce.8
  1038.9 123.9 reduce-scatter.20
  1168.5 137.4 reduce-scatter.22
where the time goes:
time: 1320 us; the launch traced here: 1310 us
  waiting for transfers between devices  704 us (53%)
  blocking collectives  285 us (22%)
  matrix products  161 us (12%)
  other arithmetic  75.2 us (6%)
  local copies, waits for them, and re-layouts  56.4 us (4%)
  between operations  16.6 us (1%)
    unnamed x17, waiting for transfers between devices  319 us
    reduce_scatter x1, waiting for transfers between devices, per_device(): lax.psum_scatter(grad_down, 'dp', scatter_dimension=1, tiled=True)  143 us
    reduce_scatter x1, waiting for transfers between devices, per_device(): lax.psum_scatter(grad_out, 'dp', scatter_dimension=1, tiled=True)  125 us
    unnamed x2, blocking collectives  86 us
    all_gather x1, waiting for transfers between devices, fetch_weights(): lax.all_gather(in_weight, 'dp', axis=1, tiled=True)  52.2 us
    all_gather x1, blocking collectives, fetch_weights(): lax.all_gather(out_weight, 'dp', axis=1, tiled=True)  42.9 us
    all_gather x1, blocking collectives, fetch_weights(): lax.all_gather(qv_bias, 'dp', axis=1, tiled=True)  42.6 us
    all_gather x1, blocking collectives, per_device(): lax.all_gather(norm_gains, ('dp', 'tensor'), axis=1, tiled=True)  39.1 us
  transfers between devices with their start and end apart: 15, of which 8 were waited for; matrix products, arithmetic and copies ran while one was open for 14% of the time, Pallas kernels for 0%

commit v1 on v0

--- a/solution.py
+++ b/solution.py
@@ -1,9 +1,404 @@
+import functools
+
 import jax
 import jax.numpy as jnp
 from jax import lax
+from jax.experimental import pallas as pl
+from jax.experimental.pallas import tpu as pltpu
 from jax.sharding import PartitionSpec as P
 
 HEAD = 64
+MESH = pl.DeviceIdType.MESH
+VMEM_LIMIT = 64 * 1024 * 1024 - 65536
+
+
+class Grid3:
+    def __init__(self, dp):
+        self.nx, self.ny = 2, 2
+        self.nz = dp // 4
+
+    def here(self):
+        me = lax.axis_index("dp")
+        return me // 4, (me // 2) % 2, me % 2
+
+    def at(self, z, y, x):
+        return (z * 2 + y) * 2 + x
+
+    def up(self, z, k):
+        return (z + k) % self.nz
+
+
+def remote(src, dst, send_sem, recv_sem, **device):
+    return pltpu.make_async_remote_copy(
+        src_ref=src, dst_ref=dst, send_sem=send_sem, recv_sem=recv_sem, device_id=device, device_id_type=MESH
+    )
+
+
+def greet(grid, z, y, x, partner):
+    barrier = pltpu.get_barrier_semaphore()
+    peers = [grid.at(grid.up(z, k), y, x) for k in range(1, grid.nz)]
+    peers += [grid.at(z, 1 - y, x), grid.at(z, y, 1 - x)]
+    for peer in peers:
+        pl.semaphore_signal(barrier, inc=1, device_id={"dp": peer}, device_id_type=MESH)
+    if partner is not None:
+        pl.semaphore_signal(barrier, inc=1, device_id={"tensor": partner}, device_id_type=MESH)
+    pl.semaphore_wait(barrier, len(peers) + (partner is not None))
+
+
+class SmallSum:
+    def __init__(self, grid, place, value, out, box, send, recv):
+        self.grid, self.place = grid, place
+        self.value, self.out, self.box, self.send, self.recv = value, out, box, send, recv
+        self.copies = []
+
+    def _post(self, slot, **device):
+        copy = remote(self.out, self.box.at[slot], self.send.at[slot], self.recv.at[slot], **device)
+        copy.start()
+        self.copies.append(copy)
+
+    def stage(self, number):
+        z, y, x = self.place
+        grid = self.grid
+        if number == 0:
+            self.out[...] = self.value[...]
+            self._post(0, tensor=1 - lax.axis_index("tensor"))
+            return
+        for copy in self.copies:
+            copy.wait()
+        self.copies = []
+        if number == 1:
+            self.out[...] = self.out[...] + self.box[0]
+            self._post(1, dp=grid.at(z, y, 1 - x))
+        elif number == 2:
+            self.out[...] = self.out[...] + self.box[1]
+            self._post(2, dp=grid.at(z, 1 - y, x))
+        elif number == 3:
+            self.out[...] = self.out[...] + self.box[2]
+            for k in range(1, grid.nz):
+                self._post(2 + k, dp=grid.at(grid.up(z, k), y, x))
+        else:
+            total = self.out[...]
+            for k in range(1, grid.nz):
+                total = total + self.box[2 + k]
+            self.out[...] = total
+
+
+def small_slots(grid):
+    return 2 + grid.nz
+
+
+class Gather:
+    def __init__(self, grid, place, rows, chunks, send, recv):
+        self.grid, self.place, self.rows, self.chunks = grid, place, rows, chunks
+        self.send_sem, self.recv_sem = send, recv
+        self.copies = []
+
+    def _dst(self, chunk, shard):
+        return chunk[1](pl.ds(pl.multiple_of(shard * self.rows, self.rows), self.rows))
+
+    def _send(self, number, shard, peer, slot, first=False):
+        chunk = self.chunks[number]
+        dst = self._dst(chunk, shard)
+        copy = remote(
+            chunk[0] if first else dst, dst, self.send_sem.at[number, slot], self.recv_sem.at[number, slot], dp=peer
+        )
+        copy.start()
+        self.copies.append(copy)
+
+    def _arrive(self, number, shard, slot):
+        dst = self._dst(self.chunks[number], shard)
+        remote(dst, dst, self.send_sem.at[number, slot], self.recv_sem.at[number, slot], dp=shard).wait_recv()
+
+    def peer(self, colour, order):
+        z, y, x = self.place
+        along_y = (colour == 0) == (order == 0)
+        return self.grid.at(z, 1 - y, x) if along_y else self.grid.at(z, y, 1 - x)
+
+    def shard(self, k, colour, order):
+        z, y, x = self.place
+        low = (z - k) % self.grid.nz
+        if order is None:
+            return self.grid.at(low, y, x)
+        if order == 2:
+            return self.grid.at(low, 1 - y, 1 - x)
+        along_y = (colour == 0) == (order == 0)
+        return self.grid.at(low, 1 - y, x) if along_y else self.grid.at(low, y, 1 - x)
+
+    def begin(self, number):
+        nz = self.grid.nz
+        colour = self.chunks[number][2]
+        z, y, x = self.place
+        me = self.grid.at(z, y, x)
+        for k in range(1, nz):
+            self._send(number, me, self.grid.at(self.grid.up(z, k), y, x), k - 1, True)
+        self._send(number, me, self.peer(colour, 0), nz - 1, True)
+        self._send(number, me, self.peer(colour, 1), 2 * nz - 1, True)
+
+    def from_line(self, number, k):
+        nz = self.grid.nz
+        colour = self.chunks[number][2]
+        shard = self.shard(k, colour, None)
+        self._arrive(number, shard, k - 1)
+        self._send(number, shard, self.peer(colour, 0), nz - 1 + k)
+        self._send(number, shard, self.peer(colour, 1), 2 * nz - 1 + k)
+
+    def from_first(self, number, k):
+        nz = self.grid.nz
+        colour = self.chunks[number][2]
+        shard = self.shard(k, colour, 0)
+        self._arrive(number, shard, nz - 1 + k)
+        self._send(number, shard, self.peer(colour, 1), 3 * nz - 1 + k)
+
+    def finish(self, number):
+        nz = self.grid.nz
+        colour = self.chunks[number][2]
+        for k in range(nz):
+            self._arrive(number, self.shard(k, colour, 1), 2 * nz - 1 + k)
+            self._arrive(number, self.shard(k, colour, 2), 3 * nz - 1 + k)
+
+    def drain(self):
+        for copy in self.copies:
+            copy.wait_send()
+        self.copies = []
+
+
+def gather_slots(grid):
+    return 4 * grid.nz - 1
+
+
+class Scatter:
+    def __init__(self, grid, place, rows, chunks, send, recv):
+        self.grid, self.place, self.rows, self.chunks = grid, place, rows, chunks
+        self.send_sem, self.recv_sem = send, recv
+        self.copies = []
+
+    def peer(self, colour, order):
+        z, y, x = self.place
+        along_x = (colour == 0) == (order == 0)
+        return self.grid.at(z, y, 1 - x) if along_x else self.grid.at(z, 1 - y, x)
+
+    def _part(self, number, shard):
+        return self.chunks[number][0](pl.ds(pl.multiple_of(shard * self.rows, self.rows), self.rows))
+
+    def shard(self, k, colour, mine0, mine1):
+        z, y, x = self.place
+        high = self.grid.up(z, k)
+        xs, ys = (mine0, mine1) if colour == 0 else (mine1, mine0)
+        return self.grid.at(high, y if ys else 1 - y, x if xs else 1 - x)
+
+    def _send(self, number, source, slot, peer):
+        box = self.chunks[number][3]
+        copy = remote(
+            source, box.at[slot], self.send_sem.at[number, slot], self.recv_sem.at[number, slot], dp=peer
+        )
+        copy.start()
+        self.copies.append(copy)
+
+    def _arrive(self, number, slot):
+        box = self.chunks[number][3].at[slot]
+        remote(box, box, self.send_sem.at[number, slot], self.recv_sem.at[number, slot], dp=0).wait_recv()
+
+    def begin(self, number):
+        nz = self.grid.nz
+        colour = self.chunks[number][2]
+        peer = self.peer(colour, 0)
+        for k in list(range(1, nz)) + [0]:
+            self._send(number, self._part(number, self.shard(k, colour, False, False)), k, peer)
+        for k in list(range(1, nz)) + [0]:
+            self._send(number, self._part(number, self.shard(k, colour, False, True)), nz + k, peer)
+
+    def second(self, number, k):
+        nz = self.grid.nz
+        colour, box = self.chunks[number][2:4]
+        self._arrive(number, k)
+        shard = self.shard(k, colour, True, False)
+        part = self._part(number, shard)
+        box[k] = (part[...].astype(jnp.float32) + box[k].astype(jnp.float32)).astype(jnp.bfloat16)
+        self._send(number, box.at[k], 2 * nz + k, self.peer(colour, 1))
+
+    def third(self, number, k):
+        nz = self.grid.nz
+        colour, box = self.chunks[number][2:4]
+        z, y, x = self.place
+        self._arrive(number, nz + k)
+        self._arrive(number, 2 * nz + k)
+        shard = self.shard(k, colour, True, True)
+        part = self._part(number, shard)
+        total = part[...].astype(jnp.float32) + box[nz + k].astype(jnp.float32) + box[2 * nz + k].astype(jnp.float32)
+        box[nz + k] = total.astype(jnp.bfloat16)
+        self._send(number, box.at[nz + k], 3 * nz - 1 + k, self.grid.at(self.grid.up(z, k), y, x))
+
+    def last(self, number):
+        nz = self.grid.nz
+        colour, box = self.chunks[number][2:4]
+        self._arrive(number, nz)
+        self._arrive(number, 2 * nz)
+        part = self._part(number, self.shard(0, colour, True, True))
+        total = part[...].astype(jnp.float32) + box[nz].astype(jnp.float32) + box[2 * nz].astype(jnp.float32)
+        for k in range(1, nz):
+            self._arrive(number, 3 * nz - 1 + k)
+            total = total + box[3 * nz - 1 + k].astype(jnp.float32)
+        self.chunks[number][1][...] = total
+
+    def drain(self):
+        for copy in self.copies:
+            copy.wait_send()
+        self.copies = []
+
+
+def scatter_slots(grid):
+    return 4 * grid.nz - 1
+
+
+def gather_chunks(qkv, outw, inw, down, to_qkv, to_out, to_in, to_down):
+    half = down.shape[1] // 2
+    first, second = pl.ds(0, half), pl.ds(half, half)
+    return [
+        (qkv.at[0], lambda rows: to_qkv.at[0, rows], 0),
+        (qkv.at[1], lambda rows: to_qkv.at[1, rows], 1),
+        (qkv.at[2], lambda rows: to_qkv.at[2, rows], 0),
+        (outw, lambda rows: to_out.at[rows], 1),
+        (inw.at[0], lambda rows: to_in.at[0, rows], 0),
+        (inw.at[1], lambda rows: to_in.at[1, rows], 1),
+        (down.at[:, first], lambda rows: to_down.at[rows, first], 0),
+        (down.at[:, second], lambda rows: to_down.at[rows, second], 1),
+    ]
+
+
+def gather_body(grid, rows, qkv, outw, inw, down, small, to_qkv, to_out, to_in, to_down, to_small, box, send, recv, ssend, srecv, own):
+    place = grid.here()
+    z, y, x = place
+    me = grid.at(z, y, x)
+    greet(grid, z, y, x, 1 - lax.axis_index("tensor"))
+    chunks = gather_chunks(qkv, outw, inw, down, to_qkv, to_out, to_in, to_down)
+    gather = Gather(grid, place, rows, chunks, send, recv)
+    sums = SmallSum(grid, place, small, to_small, box, ssend, srecv)
+    sums.stage(0)
+    for number in range(len(chunks)):
+        gather.begin(number)
+    mine = pl.ds(pl.multiple_of(me * rows, rows), rows)
+    copies = [pltpu.make_async_copy(c[0], c[1](mine), own.at[n]) for n, c in enumerate(chunks)]
+    for copy in copies:
+        copy.start()
+    for number in range(len(chunks)):
+        for k in range(1, grid.nz):
+            gather.from_line(number, k)
+        for k in range(grid.nz):
+            gather.from_first(number, k)
+        if number < 4:
+            sums.stage(number + 1)
+    for number in range(len(chunks)):
+        gather.finish(number)
+    gather.drain()
+    for copy in copies:
+        copy.wait()
+
+
+def gather_call(grid, qkv, outw, inw, down, small):
+    rows = qkv.shape[1]
+    count = rows * grid.nz * 4
+    chunks = 8
+    shapes = [
+        jax.ShapeDtypeStruct((3, count, qkv.shape[2]), qkv.dtype),
+        jax.ShapeDtypeStruct((count, outw.shape[1]), outw.dtype),
+        jax.ShapeDtypeStruct((2, count, inw.shape[2]), inw.dtype),
+        jax.ShapeDtypeStruct((count, down.shape[1]), down.dtype),
+        jax.ShapeDtypeStruct(small.shape, small.dtype),
+    ]
+    vmem = pl.BlockSpec(memory_space=pltpu.VMEM)
+    slots = gather_slots(grid)
+    return pl.pallas_call(
+        functools.partial(gather_body, grid, rows),
+        out_shape=shapes,
+        in_specs=[vmem] * 5,
+        out_specs=[vmem] * 5,
+        scratch_shapes=[
+            pltpu.VMEM((small_slots(grid), *small.shape), small.dtype),
+            pltpu.SemaphoreType.DMA((chunks, slots)),
+            pltpu.SemaphoreType.DMA((chunks, slots)),
+            pltpu.SemaphoreType.DMA((small_slots(grid),)),
+            pltpu.SemaphoreType.DMA((small_slots(grid),)),
+            pltpu.SemaphoreType.DMA((chunks,)),
+        ],
+        compiler_params=pltpu.CompilerParams(collective_id=0, has_side_effects=True, vmem_limit_bytes=VMEM_LIMIT),
+        name="gather",
+    )(qkv, outw, inw, down, small)
+
+
+def scatter_chunks(qkv, outw, inw, down, to_qkv, to_out, to_in, to_down, box_a, box_b, box_c):
+    half = down.shape[1] // 2
+    first, second = pl.ds(0, half), pl.ds(half, half)
+    return [
+        (lambda rows: inw.at[0, rows], to_in.at[0], 0, box_a.at[0]),
+        (lambda rows: inw.at[1, rows], to_in.at[1], 1, box_a.at[1]),
+        (lambda rows: down.at[rows, first], to_down.at[:, first], 0, box_b.at[0]),
+        (lambda rows: down.at[rows, second], to_down.at[:, second], 1, box_b.at[1]),
+        (lambda rows: outw.at[rows], to_out, 1, box_c.at[3]),
+        (lambda rows: qkv.at[0, rows], to_qkv.at[0], 0, box_c.at[0]),
+        (lambda rows: qkv.at[1, rows], to_qkv.at[1], 1, box_c.at[1]),
+        (lambda rows: qkv.at[2, rows], to_qkv.at[2], 0, box_c.at[2]),
+    ]
+
+
+def scatter_body(grid, rows, qkv, outw, inw, down, small, to_qkv, to_out, to_in, to_down, to_small,
+                 box_a, box_b, box_c, box, send, recv, ssend, srecv):
+    place = grid.here()
+    greet(grid, *place, 1 - lax.axis_index("tensor"))
+    chunks = scatter_chunks(qkv, outw, inw, down, to_qkv, to_out, to_in, to_down, box_a, box_b, box_c)
+    scatter = Scatter(grid, place, rows, chunks, send, recv)
+    sums = SmallSum(grid, place, small, to_small, box, ssend, srecv)
+    sums.stage(0)
+    for number in range(len(chunks)):
+        scatter.begin(number)
+    for number in range(len(chunks)):
+        for k in list(range(1, grid.nz)) + [0]:
+            scatter.second(number, k)
+        if number < 4:
+            sums.stage(number + 1)
+        if number >= 2:
+            for k in range(1, grid.nz):
+                scatter.third(number - 2, k)
+    for number in range(len(chunks) - 2, len(chunks)):
+        for k in range(1, grid.nz):
+            scatter.third(number, k)
+    for number in range(len(chunks)):
+        scatter.last(number)
+    scatter.drain()
+
+
+def scatter_call(grid, qkv, outw, inw, down, small):
+    count = qkv.shape[1]
+    rows = count // (grid.nz * 4)
+    chunks = 8
+    slots = scatter_slots(grid)
+    f32 = jnp.float32
+    shapes = [
+        jax.ShapeDtypeStruct((3, rows, qkv.shape[2]), f32),
+        jax.ShapeDtypeStruct((rows, outw.shape[1]), f32),
+        jax.ShapeDtypeStruct((2, rows, inw.shape[2]), f32),
+        jax.ShapeDtypeStruct((rows, down.shape[1]), f32),
+        jax.ShapeDtypeStruct(small.shape, small.dtype),
+    ]
+    vmem = pl.BlockSpec(memory_space=pltpu.VMEM)
+    return pl.pallas_call(
+        functools.partial(scatter_body, grid, rows),
+        out_shape=shapes,
+        in_specs=[vmem] * 5,
+        out_specs=[vmem] * 5,
+        scratch_shapes=[
+            pltpu.VMEM((2, slots, rows, inw.shape[2]), jnp.bfloat16),
+            pltpu.VMEM((2, slots, rows, down.shape[1] // 2), jnp.bfloat16),
+            pltpu.VMEM((4, slots, rows, qkv.shape[2]), jnp.bfloat16),
+            pltpu.VMEM((small_slots(grid), *small.shape), small.dtype),
+            pltpu.SemaphoreType.DMA((chunks, slots)),
+            pltpu.SemaphoreType.DMA((chunks, slots)),
+            pltpu.SemaphoreType.DMA((small_slots(grid),)),
+            pltpu.SemaphoreType.DMA((small_slots(grid),)),
+        ],
+        input_output_aliases={},
+        compiler_params=pltpu.CompilerParams(collective_id=1, has_side_effects=True, vmem_limit_bytes=VMEM_LIMIT),
+        name="scatter",
+    )(qkv, outw, inw, down, small)
 
 
 norm_epsilon = 1e-06
@@ -118,7 +513,36 @@
     )
 
 
+def spread(part, index, count):
+    wide = jnp.tile(part, (1, count))
+    owner = lax.broadcasted_iota(jnp.int32, wide.shape, 1) // part.shape[1]
+    return jnp.where(owner == index, wide.astype(jnp.float32), 0.0)
+
+
+def pick(whole, index, count):
+    size = whole.shape[1] // count
+    return lax.dynamic_slice_in_dim(whole, index * size, size, 1)
+
+
+def pack_small(biases_qv, biases_in, rows_all, piece, pieces):
+    width = rows_all.shape[1]
+    halves = [b if pieces == 1 else spread(b, piece, pieces) for b in (biases_qv, biases_in)]
+    rows = [rows_all] + [h.reshape(-1, width) for h in halves]
+    packed = jnp.concatenate(rows, axis=0)
+    return jnp.pad(packed, ((0, -packed.shape[0] % 8), (0, 0)))
+
+
+def unpack_small(packed, width_qv, width_in, piece, pieces):
+    width = packed.shape[1]
+    count_qv = 2 * width_qv * pieces // width
+    count_in = 2 * width_in * pieces // width
+    whole_qv = packed[6 : 6 + count_qv].reshape(2, -1)
+    whole_in = packed[6 + count_qv : 6 + count_qv + count_in].reshape(2, -1)
+    return packed[:6], pick(whole_qv, piece, pieces), pick(whole_in, piece, pieces)
+
+
 def per_device(
+    direct,
     tokens,
     lengths,
     qkv_weight,
@@ -132,8 +556,12 @@
     cotangent,
 ):
     row_count = tokens.shape[0]
+    dp = lax.axis_size("dp")
     pieces = lax.axis_size("tensor")
     piece_index = lax.axis_index("tensor")
+    dp_index = lax.axis_index("dp")
+    flat_index = dp_index * pieces + piece_index
+    grid = Grid3(dp)
     slot_count = row_count * pieces
     length = lengths[0]
     heads_here = qkv_weight.shape[2] // HEAD
@@ -143,54 +571,44 @@
     row_valid = (piece_index * row_count + lax.iota(jnp.int32, row_count) < length).astype(
         jnp.float32
     )[:, None]
-    gains, shift_rows = (
-        lax.all_gather(norm_gains, ("dp", "tensor"), axis=1, tiled=True),
-        lax.all_gather(offsets, ("dp", "tensor"), axis=1, tiled=True),
-    )
-
-    def fetch_weights():
-        return (
-            lax.all_gather(qkv_weight, "dp", axis=1, tiled=True),
-            lax.all_gather(qv_bias, "dp", axis=1, tiled=True),
-            lax.all_gather(out_weight, "dp", axis=1, tiled=True),
-            lax.all_gather(in_weight, "dp", axis=1, tiled=True),
-            lax.all_gather(in_bias, "dp", axis=1, tiled=True),
-            lax.all_gather(down_weight, "dp", axis=1, tiled=True),
-        )
-
-    def attention_inputs(whole_qkv, whole_bqv):
-        gathered = lax.all_gather(tokens, "tensor", axis=0, tiled=True)
-        projected = jnp.einsum(
-            "sd,kdc->ksc", gathered, whole_qkv, preferred_element_type=jnp.float32
-        )
-        queries = (projected[0] + whole_bqv[0].astype(jnp.float32)).astype(jnp.bfloat16)
-        key_rows = projected[1].astype(jnp.bfloat16)
-        value_rows = (projected[2] + whole_bqv[1].astype(jnp.float32)).astype(jnp.bfloat16)
-        mixed_heads, logsum = attend(queries, key_rows, value_rows, slopes, key_valid)
-        return (gathered, queries, key_rows, value_rows, mixed_heads, logsum)
-
-    def feed_inputs(whole_in, whole_bin, attended_low):
-        gathered_ff = lax.all_gather(attended_low, "tensor", axis=0, tiled=True)
-        pre_acts = jnp.einsum(
-            "sd,kdc->ksc", gathered_ff, whole_in, preferred_element_type=jnp.float32
-        )
-        pre_acts = pre_acts + whole_bin.astype(jnp.float32)[:, None, :]
-        hidden = (jax.nn.gelu(pre_acts[0], approximate=False) * pre_acts[1]).astype(jnp.bfloat16)
-        return (gathered_ff, pre_acts, hidden)
-
-    whole_qkv, whole_bqv, whole_out, whole_in, whole_bin, whole_down = fetch_weights()
-    gathered, queries, key_rows, value_rows, mixed_heads, logsum = attention_inputs(
-        whole_qkv, whole_bqv
-    )
-    attn_part = jnp.dot(mixed_heads, whole_out, preferred_element_type=jnp.float32)
+
+    width_qv, width_in = qkv_weight.shape[2], in_weight.shape[2]
+    small = pack_small(
+        spread(qv_bias, dp_index, dp),
+        spread(in_bias, dp_index, dp),
+        jnp.concatenate([spread(norm_gains, flat_index, dp * pieces), spread(offsets, flat_index, dp * pieces)]),
+        piece_index,
+        pieces,
+    )
+    parts = (qkv_weight, out_weight.T, in_weight, down_weight.T)
+    if direct:
+        whole_qkv, whole_out_t, whole_in, whole_down_t, small = gather_call(grid, *parts, small)
+    else:
+        whole_qkv, whole_out_t, whole_in, whole_down_t = (
+            lax.all_gather(p, "dp", axis=p.ndim - 2, tiled=True) for p in parts
+        )
+        small = lax.psum(small, ("dp", "tensor"))
+    rows_all, whole_bqv, whole_bin = unpack_small(small, width_qv, width_in, piece_index, pieces)
+    gains, shift_rows = rows_all[:2], rows_all[2:6]
+
+    gathered = lax.all_gather(tokens, "tensor", axis=0, tiled=True)
+    projected = jnp.einsum("sd,kdc->ksc", gathered, whole_qkv, preferred_element_type=jnp.float32)
+    queries = (projected[0] + whole_bqv[0]).astype(jnp.bfloat16)
+    key_rows = projected[1].astype(jnp.bfloat16)
+    value_rows = (projected[2] + whole_bqv[1]).astype(jnp.bfloat16)
+    mixed_heads, logsum = attend(queries, key_rows, value_rows, slopes, key_valid)
+    attn_part = jnp.einsum("sc,dc->sd", mixed_heads, whole_out_t, preferred_element_type=jnp.float32)
     attn_total = lax.psum_scatter(
         attn_part.astype(jnp.bfloat16), "tensor", scatter_dimension=0, tiled=True
     ).astype(jnp.float32)
     first_in = tokens.astype(jnp.float32) + attn_total + shift_rows[0]
     attended, unit_one, scale_one = norm_forward(first_in, gains[0], shift_rows[1])
     attended_low = attended.astype(jnp.bfloat16)
-    gathered_ff, pre_acts, hidden = feed_inputs(whole_in, whole_bin, attended_low)
-    ff_part = jnp.dot(hidden, whole_down, preferred_element_type=jnp.float32)
+    gathered_ff = lax.all_gather(attended_low, "tensor", axis=0, tiled=True)
+    pre_acts = jnp.einsum("sd,kdc->ksc", gathered_ff, whole_in, preferred_element_type=jnp.float32)
+    pre_acts = pre_acts + whole_bin[:, None, :]
+    hidden = (jax.nn.gelu(pre_acts[0], approximate=False) * pre_acts[1]).astype(jnp.bfloat16)
+    ff_part = jnp.einsum("sf,df->sd", hidden, whole_down_t, preferred_element_type=jnp.float32)
     ff_total = lax.psum_scatter(
         ff_part.astype(jnp.bfloat16), "tensor", scatter_dimension=0, tiled=True
     ).astype(jnp.float32)
@@ -202,13 +620,9 @@
         grad_final, unit_two, scale_two, gains[1]
     )
     grad_bdown = jnp.sum(grad_second, axis=0)
-    whole_qkv, whole_bqv, whole_out, whole_in, whole_bin, whole_down = fetch_weights()
-    gathered_ff, pre_acts, hidden = feed_inputs(whole_in, whole_bin, attended_low)
     grad_ff_rows = lax.all_gather(grad_second.astype(jnp.bfloat16), "tensor", axis=0, tiled=True)
-    grad_down = jnp.einsum("sf,sd->fd", hidden, grad_ff_rows, preferred_element_type=jnp.float32)
-    grad_hidden = jnp.einsum(
-        "sd,fd->sf", grad_ff_rows, whole_down, preferred_element_type=jnp.float32
-    )
+    grad_down_t = jnp.einsum("sd,sf->df", grad_ff_rows, hidden, preferred_element_type=jnp.float32)
+    grad_hidden = jnp.einsum("sd,df->sf", grad_ff_rows, whole_down_t, preferred_element_type=jnp.float32)
     pullback = jax.vjp(
         lambda gate_pre, up_pre: jax.nn.gelu(gate_pre, approximate=False) * up_pre,
         pre_acts[0],
@@ -226,15 +640,10 @@
         grad_attended, unit_one, scale_one, gains[0]
     )
     grad_bout = jnp.sum(grad_first, axis=0)
-    gathered, queries, key_rows, value_rows, mixed_heads, logsum = attention_inputs(
-        whole_qkv, whole_bqv
-    )
     grad_attn_rows = lax.all_gather(grad_first.astype(jnp.bfloat16), "tensor", axis=0, tiled=True)
-    grad_out = jnp.einsum(
-        "sc,sd->cd", mixed_heads, grad_attn_rows, preferred_element_type=jnp.float32
-    )
+    grad_out_t = jnp.einsum("sd,sc->dc", grad_attn_rows, mixed_heads, preferred_element_type=jnp.float32)
     grad_mixed = jnp.einsum(
-        "sd,cd->sc", grad_attn_rows, whole_out, preferred_element_type=jnp.float32
+        "sd,dc->sc", grad_attn_rows, whole_out_t, preferred_element_type=jnp.float32
     ).astype(jnp.bfloat16)
     grad_queries, grad_keys, grad_values = attend_back(
         queries, key_rows, value_rows, grad_mixed, logsum, slopes, key_valid
@@ -251,31 +660,35 @@
     grad_tokens = grad_first + lax.psum_scatter(
         input_back.astype(jnp.bfloat16), "tensor", scatter_dimension=0, tiled=True
     ).astype(jnp.float32)
-    shard_wqkv, shard_bqv, shard_out, shard_in, shard_bin, shard_down = (
-        lax.psum_scatter(grad_wqkv, "dp", scatter_dimension=1, tiled=True),
-        lax.psum_scatter(grad_bqv, "dp", scatter_dimension=1, tiled=True),
-        lax.psum_scatter(grad_out, "dp", scatter_dimension=1, tiled=True),
-        lax.psum_scatter(grad_in, "dp", scatter_dimension=1, tiled=True),
-        lax.psum_scatter(grad_bin, "dp", scatter_dimension=1, tiled=True),
-        lax.psum_scatter(grad_down, "dp", scatter_dimension=1, tiled=True),
-    )
-    gain_grads = jnp.stack([grad_gain_one, grad_gain_two])
-    offset_grads = jnp.stack([grad_bout, grad_shift_one, grad_bdown, grad_shift_two])
-    shard_gains, shard_offsets = (
-        lax.psum_scatter(gain_grads, ("dp", "tensor"), scatter_dimension=1, tiled=True),
-        lax.psum_scatter(offset_grads, ("dp", "tensor"), scatter_dimension=1, tiled=True),
-    )
+
+    small_grads = pack_small(
+        grad_bqv,
+        grad_bin,
+        jnp.stack([grad_gain_one, grad_gain_two, grad_bout, grad_shift_one, grad_bdown, grad_shift_two]),
+        piece_index,
+        pieces,
+    )
+    grads = tuple(g.astype(jnp.bfloat16) for g in (grad_wqkv, grad_out_t, grad_in, grad_down_t))
+    if direct:
+        shard_wqkv, shard_out_t, shard_in, shard_down_t, small_grads = scatter_call(grid, *grads, small_grads)
+    else:
+        shard_wqkv, shard_out_t, shard_in, shard_down_t = (
+            lax.psum_scatter(g.astype(jnp.float32), "dp", scatter_dimension=g.ndim - 2, tiled=True) for g in grads
+        )
+        small_grads = lax.psum(small_grads, ("dp", "tensor"))
+    row_grads, bqv_grads, bin_grads = unpack_small(small_grads, width_qv, width_in, piece_index, pieces)
+    own_rows = pick(row_grads, flat_index, dp * pieces)
     return (
         output,
         grad_tokens,
         shard_wqkv,
-        shard_bqv,
-        shard_out,
+        pick(bqv_grads, dp_index, dp),
+        shard_out_t.T,
         shard_in,
-        shard_bin,
-        shard_down,
-        shard_gains,
-        shard_offsets,
+        pick(bin_grads, dp_index, dp),
+        shard_down_t.T,
+        own_rows[:2],
+        own_rows[2:],
     )
 
 
@@ -293,21 +706,27 @@
         P(None, ("dp", "tensor")),
         P(("dp", "tensor"), None),
     )
-    return jax.shard_map(
-        per_device,
-        mesh=mesh,
-        in_specs=placed,
-        out_specs=(
-            P(("dp", "tensor"), None),
-            P(("dp", "tensor"), None),
-            P(None, "dp", "tensor"),
-            P(None, ("tensor", "dp")),
-            P("tensor", "dp"),
-            P(None, "dp", "tensor"),
-            P(None, ("tensor", "dp")),
-            P("tensor", "dp"),
-            P(None, ("dp", "tensor")),
-            P(None, ("dp", "tensor")),
-        ),
-        check_vma=False,
-    )
+
+    def run(*args):
+        dp = mesh.shape["dp"]
+        direct = dp % 4 == 0 and (args[2].shape[1] // dp) % 16 == 0 and mesh.shape["tensor"] == 2
+        return jax.shard_map(
+            functools.partial(per_device, direct),
+            mesh=mesh,
+            in_specs=placed,
+            out_specs=(
+                P(("dp", "tensor"), None),
+                P(("dp", "tensor"), None),
+                P(None, "dp", "tensor"),
+                P(None, ("tensor", "dp")),
+                P("tensor", "dp"),
+                P(None, "dp", "tensor"),
+                P(None, ("tensor", "dp")),
+                P("tensor", "dp"),
+                P(None, ("dp", "tensor")),
+                P(None, ("dp", "tensor")),
+            ),
+            check_vma=False,
+        )(*args)
+
+    return run

time: 1320 us -> 597 us (0.45)
  waiting for transfers between devices: 704 us -> 51.2 us
  blocking collectives: 285 us -> 0 us
  Pallas kernels: 0 us -> 255 us
  matrix products: 161 us -> 131 us
    unnamed x17 -> x8, waiting for transfers between devices: 319 us -> 0.8 us
    reduce_scatter x2 -> x0, waiting for transfers between devices: 269 us -> none  [the longest x1 143 us: per_device(): lax.psum_scatter(grad_down, 'dp', scatter_dimension=1, tiled=True)]
    pallas_call x0 -> x2, Pallas kernels: none -> 255 us  [the longest x1 133 us: scatter_call(): pl.pallas_call(functools.partial(scatter_body, grid, rows), out_shape=sha...]
    all_gather x5 -> x0, blocking collectives: 199 us -> none  [the longest x1 42.9 us: fetch_weights(): lax.all_gather(out_weight, 'dp', axis=1, tiled=True)]
    unnamed x2 -> x0, blocking collectives: 86 us -> none
    all_gather x5 -> x2, waiting for transfers between devices: 89 us -> 11.1 us  [the longest x1 11.1 us: per_device(): gathered_ff = lax.all_gather(attended_low, 'tensor', axis=0, tiled=True)]
    sub x2 -> x0, matrix products: 20.6 us -> none  [one_block(): exp_scores = jnp.exp(scores - row_max)]
    transpose x2 -> x0, local copies, waits for them, and re-layouts: 19 us -> none  [the longest x1 15 us: per_device(): jnp.einsum('sd,ksc->kdc', gathered_ff, grad_pre, preferred_element_type=j...]
  transfers between devices with their start and end apart: 15 -> 8, of which waited for: 8 -> 5; matrix products, arithmetic and copies ran while one was open for 14% -> 7% of each run, Pallas kernels for 0% -> 43%
where the time goes in v1:
time: 597 us; the launch traced here: 587 us
  Pallas kernels  255 us (43%)
  matrix products  131 us (22%)
  other arithmetic  72.6 us (12%)
  waiting for transfers between devices  51.2 us (9%)
  local copies, waits for them, and re-layouts  43.7 us (7%)
  between operations  16.1 us (3%)
  starting transfers between devices  9.12 us (2%)
  loops' own time  8.35 us (1%)
    pallas_call x1, Pallas kernels, scatter_call(): pl.pallas_call(functools.partial(scatter_body, grid, rows), out_shape=sha...  133 us
    pallas_call x1, Pallas kernels, gather_call(): pl.pallas_call(functools.partial(gather_body, grid, rows), out_shape=shap...  122 us
    dot_general x4, matrix products, score_block(): jnp.einsum('qhc,khc->hqk', query_heads, key_heads, preferred_element_type...  25.7 us
    dot_general x2, matrix products, one_block(): jnp.einsum('qhc,khc->hqk', grad_heads, value_heads, preferred_element_typ...  15.1 us
    convert_element_type x1, other arithmetic, per_device(): (jax.nn.gelu(pre_acts[0], approximate=False) * pre_acts[1]).astype(jnp.bf...  15 us
  transfers between devices with their start and end apart: 8, of which 5 were waited for; matrix products, arithmetic and copies ran while one was open for 7% of the time, Pallas kernels for 43%

profile of v1, /device:TPU:0, one launch (start us, length us, event | category | flops | bytes accessed | tf_op | source)
XLA Modules:
  0.0 587.2 jit_solution(9388117612273919156)
XLA Ops:
  12.7 122.1 %gather.1 = (bf16[3,768,384]{2,1,0:T(8,128)(2,1)}, bf16[768,384]{1,0:T(8,128)(2,1)}, bf16[2,768,1536]{2,1,0:T(8,128)(2,1)}, bf16[768,1536]{1,0:T(8,128)(2,1)}, f32[16,768]{1,0:T(8,128)}) custom-call(bf16[3,48,384]{2,1,0:T(8,128)(2,1)} %qkv.1, bf16[48,384]{1,0:T(8,128)(2,1)} %bitcast.251, bf16[2,48,1536]{2,1,0:T(8,128)(2,1)} %inw.1, ...), custom_call_target="tpu_custom_call" | custom-call | tf_op jit(solution)/shard_map/gather/pallas_call | solution.py:310
  135.7 4.0 convolution_bitcast_fusion
  142.9 40.8 %while.28 = (s32[]{:T(128)}, bf16[2,512,384]{2,1,0:T(8,128)(2,1)S(1)}, f32[2,6,512]{2,1,0:T(8,128)}, s32[2]{0:T(128)S(1)}, bf16[1024,384]{0,1:T(8,128)(2,1)}, /*...) while((s32[]{:T(128)}, ...), condition=%wide.region_3.4_spmd.clone, body=%wide.region_0.3_spmd.clone.sunk | while | flops 863697408 | bytes 50966816 | solution.py:466
  148.4 4.5 fusion.126
  152.9 4.0 fusion.127
  156.9 5.4 fusion.128
  168.7 4.5 fusion.126
  173.2 4.0 fusion.127
  177.3 5.4 fusion.128
  186.3 8.2 %reduce-scatter.5.cloned.1.call-done = bf16[512,768]{1,0:T(8,128)(2,1)} async-done(((bf16[1024,768]{1,0:T(8,128)(2,1)}), bf16[512,768]{1,0:T(8,128)(2,1)}) %reduce-scatter.5.cloned.1.call-update) | async-done | bytes 786448 | tf_op jit(solution)/shard_map/reduce_scatter | solution.py:601
  199.0 11.1 %all-gather.7.cloned.1.call-done = bf16[1024,768]{1,0:T(8,128)(2,1)} async-done(((bf16[512,768]{1,0:T(8,128)(2,1)}), bf16[1024,768]{1,0:T(8,128)(2,1)}) %all-gather.7.cloned.1.call-update) | async-done | bytes 1572880 | tf_op jit(solution)/shard_map/all_gather | solution.py:607
  210.1 7.4 %add_bitcast_fusion = f32[2,1024,1536]{2,1,0:T(8,128)S(1)} fusion(f32[2,1536]{1,0:T(2,128)S(1)} %constant_dynamic-slice_fusion.6, bf16[2,768,1536]{2,1,0:T(8,128)(2,1)} %get-tuple-element.136, bf16[1024,768]{1,0:T(8,128)(2,1)} %all-gather.7.cloned.1.call-done), kind=kOutput, calls=%fused_computation.37 | convolution fusion | flops 4834983936 | bytes 18886656 | tf_op jit(solution)/shard_map/sd,kdc->ksc/dot_general | solution.py:608
  217.5 15.0 %multiply_convert_fusion.2 = (bf16[1024,1536]{1,0:T(8,128)(2,1)S(1)}, f32[1024,1536]{1,0:T(8,128)}) fusion(f32[2,1024,1536]{2,1,0:T(8,128)S(1)} %add_bitcast_fusion), kind=kLoop, calls=%fused_computation.56 | loop fusion | flops 103809024 | bytes 22020096 | tf_op jit(solution)/shard_map/convert_element_type | solution.py:610
  234.3 3.7 convolution_convert_fusion.2
  238.8 9.6 %reduce-scatter.7.cloned.1.call-done = bf16[512,768]{1,0:T(8,128)(2,1)} async-done(((bf16[1024,768]{1,0:T(8,128)(2,1)}), bf16[512,768]{1,0:T(8,128)(2,1)}) %reduce-scatter.7.cloned.1.call-update) | async-done | bytes 786448 | tf_op jit(solution)/shard_map/reduce_scatter | solution.py:612
  253.6 11.2 %all-gather.9.cloned.1.call-done = bf16[1024,768]{1,0:T(8,128)(2,1)} async-done(((bf16[512,768]{1,0:T(8,128)(2,1)}), bf16[1024,768]{1,0:T(8,128)(2,1)}) %all-gather.9.cloned.1.call-update) | async-done | bytes 1572880 | tf_op jit(solution)/shard_map/all_gather | solution.py:623
  264.8 10.4 %fusion.39 = (bf16[1,1024,1536]{2,1,0:T(8,128)(2,1)S(1)}, bf16[1,1024,1536]{2,1,0:T(8,128)(2,1)S(1)}) fusion(f32[1024,1536]{1,0:T(8,128)} %get-tuple-element.307, f32[2,1024,1536]{2,1,0:T(8,128)} %copy-done.3, bf16[1024,768]{1,0:T(8,128)(2,1)} %all-gather.9.cloned.1.call-done, bf16[768,1536]{1,0:T(8,128)(2,1)} %get-tuple-element.137), kind=kOutput, calls=%fused_computation.76 | convolution fusion | flops 2444230656 | bytes 29097984 | tf_op jit(solution)/shard_map/sd,df->sf/dot_general | solution.py:625
  277.9 8.6 %bitcast_convert_fusion.1 = bf16[1024,768]{1,0:T(8,128)(2,1)} fusion(bf16[2,768,1536]{2,1,0:T(8,128)(2,1)} %get-tuple-element.136, bf16[1,1024,1536]{2,1,0:T(8,128)(2,1)S(1)} %get-tuple-element.313, bf16[1,1024,1536]{2,1,0:T(8,128)(2,1)S(1)} %get-tuple-element.312), kind=kOutput, calls=%fused_computation.75 | convolution fusion | flops 4835770368 | bytes 12582912 | tf_op jit(solution)/shard_map/ksc,kdc->sd/dot_general | solution.py:635
  286.5 10.3 %reduce-scatter.9.cloned.1.call-done = bf16[512,768]{1,0:T(8,128)(2,1)} async-done(((bf16[1024,768]{1,0:T(8,128)(2,1)}), bf16[512,768]{1,0:T(8,128)(2,1)}) %reduce-scatter.9.cloned.1.call-update) | async-done | bytes 786448 | tf_op jit(solution)/shard_map/reduce_scatter | solution.py:636
  303.2 8.6 %reduce-scatter.11.cloned.1.call-start = ((), (), s32[]{:S(2)}) async-start(), calls=%async_computation.11 | async-start | bytes 2359296 | tf_op jit(solution)/shard_map/reduce_scatter | solution.py:660
  313.0 6.4 %convolution_convert_fusion.down = bf16[768,1536]{1,0:T(8,128)(2,1)} fusion(bf16[1024,768]{1,0:T(8,128)(2,1)} %all-gather.9.cloned.1.call-done, bf16[1024,1536]{1,0:T(8,128)(2,1)} %copy-done.10), kind=kOutput, calls=%fused_computation.72 | convolution fusion | flops 2417098752 | bytes 7077888 | tf_op jit(solution)/shard_map/sd,sf->df/dot_general | solution.py:624
  322.8 80.3 %while.29 = (s32[]{:T(128)}, f32[1024,6,64]{0,2,1:T(8,128)S(1)}, f32[1024,6,64]{0,2,1:T(8,128)S(1)}, bf16[2,512,384]{1,2,0:T(8,128)(2,1)}, s32[2]{0:T(128)S(1)},...) while((s32[]{:T(128)}, f32[1024,6,64]{0,2,1:T(8,128)S(1)}, ...), condition=%wide.region_17.18_spmd.clone, body=%wide.region_15.17_spmd.clone.sunk | while | flops 2051799552 | bytes 118692448 | solution.py:506
  334.4 7.5 %fusion.139 = f32[6,512,1024]{2,1,0:T(8,128)} fusion(bf16[512,6,64]{0,2,1:T(8,128)(2,1)S(1)} %bitcast.237, bf16[1024,6,64]{0,2,1:T(8,128)(2,1)} %get-tuple-element.536), kind=kOutput, calls=%fused_computation.196.clone.1 | convolution fusion | flops 402653184 | bytes 13762560 | tf_op jit(solution)/shard_map/while/body/eval_jaxpr/qhc,khc->hqk/dot_general | solution.py:485
  341.9 8.4 %multiply_reduce_fusion.9 = (f32[6,512]{1,0:T(8,128)S(1)}, f32[6,512,1024]{2,1,0:T(8,128)S(1)}) fusion(f32[6,512,1024]{2,1,0:T(8,128)} %fusion.139, f32[6,512]{1,0:T(8,128)S(1)} %dynamic-slice_bitcast_fusion.2, f32[512,1024]{1,0:T(8,128)S(1)} %abs_convert_fusion.5, f32[6]{0:T(128)S(1)} %copy-done.30, bf16[512,6,64]{0,2,1:T(8,128)(2,1)S(1)} %bitcast.235, ...), kind=kOutput, calls=%fused_computation.21.clone.1 | convolution fusion | flops 424670208 | bytes 28468248 | tf_op jit(solution)/shard_map/while/body/eval_jaxpr/qhc,khc->hqk/dot_general | solution.py:433
  350.3 5.5 multiply_convert_fusion.5
  374.4 7.5 %fusion.139 = f32[6,512,1024]{2,1,0:T(8,128)} fusion(bf16[512,6,64]{0,2,1:T(8,128)(2,1)S(1)} %bitcast.237, bf16[1024,6,64]{0,2,1:T(8,128)(2,1)} %get-tuple-element.536), kind=kOutput, calls=%fused_computation.196.clone.1 | convolution fusion | flops 402653184 | bytes 13762560 | tf_op jit(solution)/shard_map/while/body/eval_jaxpr/qhc,khc->hqk/dot_general | solution.py:485
  381.9 8.4 %multiply_reduce_fusion.9 = (f32[6,512]{1,0:T(8,128)S(1)}, f32[6,512,1024]{2,1,0:T(8,128)S(1)}) fusion(f32[6,512,1024]{2,1,0:T(8,128)} %fusion.139, f32[6,512]{1,0:T(8,128)S(1)} %dynamic-slice_bitcast_fusion.2, f32[512,1024]{1,0:T(8,128)S(1)} %abs_convert_fusion.5, f32[6]{0:T(128)S(1)} %copy-done.30, bf16[512,6,64]{0,2,1:T(8,128)(2,1)S(1)} %bitcast.235, ...), kind=kOutput, calls=%fused_computation.21.clone.1 | convolution fusion | flops 424670208 | bytes 28468248 | tf_op jit(solution)/shard_map/while/body/eval_jaxpr/qhc,khc->hqk/dot_general | solution.py:433
  390.3 5.5 multiply_convert_fusion.5
  409.4 5.1 bitcast_convert_fusion
  414.5 3.8 convert_reduce_fusion
  418.5 9.4 %convert_bitcast_fusion.inw = bf16[2,768,1536]{2,1,0:T(8,128)(2,1)} fusion(bf16[1,1024,1536]{2,1,0:T(8,128)(2,1)} %copy-done.9, bf16[1,1024,1536]{2,1,0:T(8,128)(2,1)} %copy-done.8, bf16[1024,768]{1,0:T(8,128)(2,1)} %all-gather.7.cloned.1.call-done), kind=kOutput, calls=%fused_computation.71 | convolution fusion | flops 4837343232 | bytes 12582912 | tf_op jit(solution)/shard_map/sd,ksc->kdc/dot_general | solution.py:634
  436.7 132.7 %scatter.1 = (f32[3,48,384]{2,1,0:T(8,128)}, f32[48,384]{1,0:T(8,128)}, f32[2,48,1536]{2,1,0:T(8,128)}, f32[48,1536]{1,0:T(8,128)}, f32[16,768]{1,0:T(8,128)}) custom-call(bf16[3,768,384]{2,1,0:T(8,128)(2,1)} %convert_bitcast_fusion.1.qkv, bf16[768,384]{1,0:T(8,128)(2,1)} %convolution_convert_fusion.4.outw, bf16[2,768,1536]{2,1,0:T(8,128)(2,1)} %convert_bitcast_fusion.inw, ...), custom_call_target="tpu_custom_call" | custom-call | tf_op jit(solution)/shard_map/scatter/pallas_call | solution.py:383
  (265 shorter events, 104.6 us)
Async XLA Ops:
  7.2 128.5 %all-gather.5.cloned.1.call-start = ((), (), s32[]{:S(2)}) async-start(), calls=%async_computation.4 | async-start | bytes 2359296 | tf_op jit(solution)/shard_map/all_gather | solution.py:594
  7.9 186.5 %reduce-scatter.5.cloned.1.call-start = ((), (), s32[]{:S(2)}) async-start(), calls=%async_computation.5 | async-start | bytes 2359296 | tf_op jit(solution)/shard_map/reduce_scatter | solution.py:601
  142.9 40.8 %copy-start.39 = (bf16[768,384]{1,0:T(8,128)(2,1)S(1)}, bf16[768,384]{1,0:T(8,128)(2,1)}, u32[]{:S(2)}) copy-start(bf16[768,384]{1,0:T(8,128)(2,1)} %get-tuple-element.135) | copy-start | bytes 1769476
  183.7 10.7 %copy-start = (bf16[512,768]{1,0:T(8,128)(2,1)S(1)}, bf16[512,768]{1,0:T(8,128)(2,1)}, u32[]{:S(2)}) copy-start(bf16[512,768]{1,0:T(8,128)(2,1)} %param.15) | copy-start | bytes 2359300
  185.9 24.3 %all-gather.7.cloned.1.call-start = ((), (), s32[]{:S(2)}) async-start(), calls=%async_computation.6 | async-start | bytes 2359296 | tf_op jit(solution)/shard_map/all_gather | solution.py:607
  198.9 49.5 %reduce-scatter.7.cloned.1.call-start = ((), (), s32[]{:S(2)}) async-start(), calls=%async_computation.7 | async-start | bytes 2359296 | tf_op jit(solution)/shard_map/reduce_scatter | solution.py:612
  217.5 15.0 %copy-start.3 = (f32[2,1024,1536]{2,1,0:T(8,128)}, f32[2,1024,1536]{2,1,0:T(8,128)S(1)}, u32[]{:S(2)}) copy-start(f32[2,1024,1536]{2,1,0:T(8,128)S(1)} %add_bitcast_fusion) | copy-start | bytes 37748740
  217.5 16.7 %copy-start.35 = (bf16[768,1536]{1,0:T(8,128)(2,1)S(1)}, bf16[768,1536]{1,0:T(8,128)(2,1)}, u32[]{:S(2)}) copy-start(bf16[768,1536]{1,0:T(8,128)(2,1)} %get-tuple-element.137) | copy-start | bytes 7077892
  238.0 12.7 %copy-start.4 = (bf16[512,768]{1,0:T(8,128)(2,1)S(1)}, bf16[512,768]{1,0:T(8,128)(2,1)}, u32[]{:S(2)}) copy-start(bf16[512,768]{1,0:T(8,128)(2,1)} %param.25) | copy-start | bytes 2359300
  238.0 26.7 %all-gather.9.cloned.1.call-start = ((), (), s32[]{:S(2)}) async-start(), calls=%async_computation.8 | async-start | bytes 2359296 | tf_op jit(solution)/shard_map/all_gather | solution.py:623
  253.5 43.3 %reduce-scatter.9.cloned.1.call-start = ((), (), s32[]{:S(2)}) async-start(), calls=%async_computation.9 | async-start | bytes 2359296 | tf_op jit(solution)/shard_map/reduce_scatter | solution.py:636
  286.5 32.9 %all-gather.11.cloned.1.call-start = ((), (), s32[]{:S(2)}) async-start(), calls=%async_computation.10 | async-start | bytes 2359296 | tf_op jit(solution)/shard_map/all_gather | solution.py:643
  303.2 271.0 %reduce-scatter.11.cloned.1.call-start = ((), (), s32[]{:S(2)}) async-start(), calls=%async_computation.11 | async-start | bytes 2359296 | tf_op jit(solution)/shard_map/reduce_scatter | solution.py:660
  322.8 6.2 %copy-start.40 = (s32[2]{0:T(128)}, s32[2]{0:T(128)S(1)}, u32[]{:S(2)}) copy-start(s32[2]{0:T(128)S(1)} %get-tuple-element.531) | copy-start | bytes 28 | tf_op jit(solution)/shard_map/while
  334.4 7.6 %copy-start.25 = (pred[1024]{0:T(1024)(128)(4,1)S(1)}, pred[1024]{0:T(1024)(128)(4,1)}, u32[]{:S(2)}) copy-start(pred[1024]{0:T(1024)(128)(4,1)} %iota_compare_fusion.5) | copy-start | bytes 3076 | tf_op jit(solution)/shard_map/while
  334.4 7.6 %copy-start.30 = (f32[6]{0:T(128)S(1)}, f32[6]{0:T(128)}, u32[]{:S(2)}) copy-start(f32[6]{0:T(128)} %multiply_exponential_fusion.5) | copy-start | bytes 76 | tf_op jit(solution)/shard_map/while
  362.9 6.2 %copy-start.40 = (s32[2]{0:T(128)}, s32[2]{0:T(128)S(1)}, u32[]{:S(2)}) copy-start(s32[2]{0:T(128)S(1)} %get-tuple-element.531) | copy-start | bytes 28 | tf_op jit(solution)/shard_map/while
  374.4 7.6 %copy-start.25 = (pred[1024]{0:T(1024)(128)(4,1)S(1)}, pred[1024]{0:T(1024)(128)(4,1)}, u32[]{:S(2)}) copy-start(pred[1024]{0:T(1024)(128)(4,1)} %iota_compare_fusion.5) | copy-start | bytes 3076 | tf_op jit(solution)/shard_map/while
  374.4 7.5 %copy-start.30 = (f32[6]{0:T(128)S(1)}, f32[6]{0:T(128)}, u32[]{:S(2)}) copy-start(f32[6]{0:T(128)} %multiply_exponential_fusion.5) | copy-start | bytes 76 | tf_op jit(solution)/shard_map/while
  418.4 9.5 %copy-start.28 = (f32[768]{0:T(1024)S(1)}, f32[768]{0:T(1024)}, u32[]{:S(2)}) copy-start(f32[768]{0:T(1024)} %get-tuple-element.239) | copy-start | bytes 9220
  418.4 9.5 %copy-start.29 = (f32[768]{0:T(1024)S(1)}, f32[768]{0:T(1024)}, u32[]{:S(2)}) copy-start(f32[768]{0:T(1024)} %get-tuple-element.300) | copy-start | bytes 9220
  418.5 9.6 %copy-start.27 = (f32[768]{0:T(1024)S(1)}, f32[768]{0:T(1024)}, u32[]{:S(2)}) copy-start(f32[768]{0:T(1024)} %get-tuple-element.244) | copy-start | bytes 9220
  418.5 9.6 %copy-start.26 = (f32[768]{0:T(1024)S(1)}, f32[768]{0:T(1024)}, u32[]{:S(2)}) copy-start(f32[768]{0:T(1024)} %get-tuple-element.245) | copy-start | bytes 9220
  418.5 9.8 %copy-start.22 = (s32[768]{0:T(1024)S(1)}, s32[768]{0:T(1024)}, u32[]{:S(2)}) copy-start(s32[768]{0:T(1024)} %copy-done.21) | copy-start | bytes 9220
  418.5 9.8 %copy-start.24 = (s32[768]{0:T(1024)S(1)}, s32[768]{0:T(1024)}, u32[]{:S(2)}) copy-start(s32[768]{0:T(1024)} %copy-done.23) | copy-start | bytes 9220
  418.5 9.8 %copy-start.34 = (pred[768]{0:T(1024)(128)(4,1)S(1)}, pred[768]{0:T(1024)(128)(4,1)}, u32[]{:S(2)}) copy-start(pred[768]{0:T(1024)(128)(4,1)} %copy-done.33) | copy-start | bytes 2308
  418.5 9.8 %copy-start.31 = (f32[1,768]{1,0:T(1,128)S(1)}, f32[1,768]{1,0:T(1,128)}, u32[]{:S(2)}) copy-start(f32[1,768]{1,0:T(1,128)} %stack.48) | copy-start | bytes 9220
  418.5 9.8 %copy-start.32 = (f32[1,768]{1,0:T(1,128)S(1)}, f32[1,768]{1,0:T(1,128)}, u32[]{:S(2)}) copy-start(f32[1,768]{1,0:T(1,128)} %stack.52) | copy-start | bytes 9220
  569.3 7.8 %copy-start.16 = (f32[3,48,384]{2,1,0:T(8,128)S(1)}, f32[3,48,384]{2,1,0:T(8,128)}, u32[]{:S(2)}) copy-start(f32[3,48,384]{2,1,0:T(8,128)} %get-tuple-element.554) | copy-start | bytes 663556
  569.4 8.4 %copy-start.17 = (f32[48,384]{1,0:T(8,128)S(1)}, f32[48,384]{1,0:T(8,128)}, u32[]{:S(2)}) copy-start(f32[48,384]{1,0:T(8,128)} %get-tuple-element.144) | copy-start | bytes 221188
  569.4 9.1 %copy-start.14 = (f32[2,48,1536]{2,1,0:T(8,128)S(1)}, f32[2,48,1536]{2,1,0:T(8,128)}, u32[]{:S(2)}) copy-start(f32[2,48,1536]{2,1,0:T(8,128)} %get-tuple-element.557) | copy-start | bytes 1769476
  569.4 9.9 %copy-start.15 = (f32[48,1536]{1,0:T(8,128)S(1)}, f32[48,1536]{1,0:T(8,128)}, u32[]{:S(2)}) copy-start(f32[48,1536]{1,0:T(8,128)} %get-tuple-element.146) | copy-start | bytes 884740
  (24 other events, 53.1 us)
Sparse Core Ops, SparseCore 0:
  9.5 12.5 all-gather.4
  186.0 8.3 reduce-scatter.4
  199.0 11.0 all-gather.6
  238.1 10.2 reduce-scatter.6
  253.7 11.0 all-gather.8
  286.6 10.2 reduce-scatter.8
  303.3 11.0 all-gather.10
  414.6 10.3 reduce-scatter.10

commit v2 on v0

--- a/solution.py
+++ b/solution.py
@@ -1,9 +1,938 @@
+import functools
+import itertools
+
 import jax
 import jax.numpy as jnp
 from jax import lax
+from jax.experimental import pallas as pl
+from jax.experimental.pallas import tpu as pltpu
 from jax.sharding import PartitionSpec as P
 
 HEAD = 64
+MESH = pl.DeviceIdType.MESH
+VMEM_LIMIT = 64 * 1024 * 1024 - 65536
+
+
+class Grid3:
+    def __init__(self, dp):
+        self.nz = dp // 4
+        self.slots = dp
+
+    def here(self):
+        me = lax.axis_index("dp")
+        self.z, self.y, self.x = me // 4, (me // 2) % 2, me % 2
+        z, nz = self.z, self.nz
+        self.low, self.high = z > 0, z < nz - 1
+        near = [sorted(range(1, nz), key=lambda k: (abs((p + k) % nz - p), k)) for p in range(nz)]
+        self.by_distance = [(sum(jnp.where(z == p, near[p][j], 0) for p in range(nz)), 0, 0) for j in range(nz - 1)]
+        self.line = []
+        for d in self.by_distance:
+            above = (z + d[0]) % nz > z
+            self.line.append((above, jnp.where(above, z, nz - 1 - z) > 0))
+
+    def at(self, dz, dy, dx):
+        y = 1 - self.y if dy else self.y
+        x = 1 - self.x if dx else self.x
+        return (((self.z + dz) % self.nz) * 2 + y) * 2 + x
+
+    def slot(self, d):
+        return (d[0] % self.nz) * 4 + d[1] * 2 + d[2]
+
+    def steps(self, axis):
+        if axis == "z":
+            return [(k, 0, 0) for k in range(1, self.nz)]
+        return [(0, 1, 0)] if axis == "y" else [(0, 0, 1)]
+
+    def seen_from(self, d, move):
+        return ((d[0] - move[0] + self.nz) % self.nz, d[1] ^ move[1], d[2] ^ move[2])
+
+    def span(self, axis):
+        if axis == "z":
+            return [(k, 0, 0) for k in range(self.nz)]
+        return [(0, 0, 0), (0, 1, 0)] if axis == "y" else [(0, 0, 0), (0, 0, 1)]
+
+
+def joined(*ds):
+    return tuple(sum(part) for part in zip(*ds))
+
+
+def remote(src, dst, send_sem, recv_sem, **device):
+    return pltpu.make_async_remote_copy(
+        src_ref=src, dst_ref=dst, send_sem=send_sem, recv_sem=recv_sem, device_id=device, device_id_type=MESH
+    )
+
+
+def greet(grid, partner):
+    barrier = pltpu.get_barrier_semaphore()
+    moves = [m for axis in "zyx" for m in grid.steps(axis)]
+    for move in moves:
+        pl.semaphore_signal(barrier, inc=1, device_id={"dp": grid.at(*move)}, device_id_type=MESH)
+    pl.semaphore_signal(barrier, inc=1, device_id={"tensor": partner}, device_id_type=MESH)
+    pl.semaphore_wait(barrier, len(moves) + 1)
+
+
+class SmallSum:
+    def __init__(self, grid, value, out, box, send, recv):
+        self.grid = grid
+        self.value, self.out, self.box, self.send, self.recv = value, out, box, send, recv
+        self.copies = []
+
+    def _post(self, slot, **device):
+        copy = remote(self.out, self.box.at[slot], self.send.at[slot], self.recv.at[slot], **device)
+        copy.start()
+        self.copies.append(copy)
+
+    def stage(self, number):
+        grid = self.grid
+        if number == 0:
+            self.out[...] = self.value[...]
+            self._post(0, tensor=1 - lax.axis_index("tensor"))
+            return
+        for copy in self.copies:
+            copy.wait()
+        self.copies = []
+        if number == 1:
+            self.out[...] = self.out[...] + self.box[0]
+            self._post(1, dp=grid.at(0, 0, 1))
+        elif number == 2:
+            self.out[...] = self.out[...] + self.box[1]
+            self._post(2, dp=grid.at(0, 1, 0))
+        elif number == 3:
+            self.out[...] = self.out[...] + self.box[2]
+            for k in range(1, grid.nz):
+                self._post(2 + k, dp=grid.at(k, 0, 0))
+        else:
+            total = self.out[...]
+            for k in range(1, grid.nz):
+                total = total + self.box[2 + k]
+            self.out[...] = total
+
+
+def small_slots(grid):
+    return 2 + grid.nz
+
+
+class Gather:
+    def __init__(self, grid, chunks, send, recv):
+        self.grid, self.chunks = grid, chunks
+        self.send_sem, self.recv_sem = send, recv
+        self.sent = []
+
+    def _dst(self, number, d):
+        rows = self.chunks[number][0].shape[0]
+        return self.chunks[number][1].at[pl.ds(pl.multiple_of(self.grid.at(*d) * rows, rows), rows)]
+
+    def _copy(self, number, d, move):
+        dst = self._dst(number, d)
+        if isinstance(move, int):
+            move = (jnp.where(self.grid.line[move][0], -1, 1), 0, 0)
+        source = self.chunks[number][0] if isinstance(d[0], int) and d == (0, 0, 0) else dst
+        slot = self.grid.slot(self.grid.seen_from(d, move))
+        return remote(source, dst, self.send_sem.at[number, slot], self.recv_sem.at[number, slot], dp=self.grid.at(*move))
+
+    def _start(self, allowed, *args):
+        if allowed is None:
+            self._copy(*args).start()
+        else:
+            pl.when(allowed)(lambda: self._copy(*args).start())
+        self.sent.append((allowed, args))
+
+    def send(self, number, d, axis):
+        if axis == "z":
+            self._start(self.grid.low, number, d, (-1, 0, 0))
+            self._start(self.grid.high, number, d, (1, 0, 0))
+        else:
+            self._start(None, number, d, self.grid.steps(axis)[0])
+
+    def relay(self, number, d, j):
+        self._start(self.grid.line[j][1], number, d, j)
+
+    def arrive(self, number, d):
+        dst, slot = self._dst(number, d), self.grid.slot(d)
+        remote(dst, dst, self.send_sem.at[number, slot], self.recv_sem.at[number, slot], dp=self.grid.at(*d)).wait_recv()
+
+    def moved(self, axis):
+        return self.grid.by_distance if axis == "z" else self.grid.steps(axis)
+
+    def first(self, number):
+        return [(self.pass_first, number, d, j) for j, d in enumerate(self.moved(self.chunks[number][2][0]))]
+
+    def second(self, number):
+        one, two = self.chunks[number][2][:2]
+        return [
+            (self.pass_second, number, joined(a, b), j) for j, b in enumerate(self.moved(two)) for a in self.grid.span(one)
+        ]
+
+    def third(self, number):
+        one, two, three = self.chunks[number][2]
+        return [joined(a, b, c) for a in self.grid.span(one) for b in self.grid.span(two) for c in self.grid.steps(three)]
+
+    def pass_first(self, number, d, j):
+        order = self.chunks[number][2]
+        self.arrive(number, d)
+        if order[0] == "z":
+            self.relay(number, d, j)
+        for axis in order[1:]:
+            self.send(number, d, axis)
+
+    def pass_second(self, number, d, j):
+        order = self.chunks[number][2]
+        self.arrive(number, d)
+        if order[1] == "z":
+            self.relay(number, d, j)
+        self.send(number, d, order[2])
+
+    def finish(self, number):
+        for d in self.third(number):
+            self.arrive(number, d)
+
+    def drain(self):
+        for allowed, args in self.sent:
+            if allowed is None:
+                self._copy(*args).wait_send()
+            else:
+                pl.when(allowed)(lambda args=args: self._copy(*args).wait_send())
+        self.sent = []
+
+
+class Scatter:
+    def __init__(self, grid, rows, chunks, send, recv):
+        self.grid, self.rows, self.chunks = grid, rows, chunks
+        self.send_sem, self.recv_sem = send, recv
+        self.sent = []
+        self.far_first = [2, 1, 3] if grid.nz == 4 else list(range(1, grid.nz))
+        self.second, self.line = 2 * grid.nz, 3 * grid.nz - 1
+
+    def part(self, number, d):
+        return self.chunks[number][0].at[pl.ds(pl.multiple_of(self.grid.at(*d) * self.rows, self.rows), self.rows)]
+
+    def box(self, number, slot):
+        return self.chunks[number][3].at[slot]
+
+    def other(self, number):
+        return "y" if self.chunks[number][2] == "x" else "x"
+
+    def place(self, number, dz, e):
+        return (dz, e, 0) if self.other(number) == "y" else (dz, 0, e)
+
+    def _copy(self, number, kind, dz, e=0):
+        grid = self.grid
+        if kind == "own":
+            move = grid.steps(self.chunks[number][2])[0]
+            source, slot = self.part(number, joined(self.place(number, dz, e), move)), dz * 2 + e
+        elif kind == "side":
+            move = grid.steps(self.other(number))[0]
+            source, slot = self.box(number, dz * 2 + 1), self.second + dz
+        else:
+            move = (dz, 0, 0)
+            source, slot = self.box(number, dz * 2), self.line + dz
+        return remote(
+            source, self.box(number, slot), self.send_sem.at[number, slot], self.recv_sem.at[number, slot], dp=grid.at(*move)
+        )
+
+    def _send(self, *args):
+        self._copy(*args).start()
+        self.sent.append(args)
+
+    def _arrive(self, number, slot):
+        box = self.box(number, slot)
+        remote(box, box, self.send_sem.at[number, slot], self.recv_sem.at[number, slot], dp=0).wait_recv()
+
+    def begin(self, number, *halves):
+        for e in halves or (1, 0):
+            for dz in self.far_first + [0]:
+                self._send(number, "own", dz, e)
+
+    def held(self, number, dz, e):
+        slot = dz * 2 + e
+        self._arrive(number, slot)
+        return self.part(number, self.place(number, dz, e))[...].astype(jnp.float32) + self.box(number, slot)[...].astype(jnp.float32)
+
+    def side(self, number, dz):
+        self.box(number, dz * 2 + 1)[...] = self.held(number, dz, 1).astype(jnp.bfloat16)
+        self._send(number, "side", dz)
+
+    def both(self, number, dz):
+        value = self.held(number, dz, 0)
+        self._arrive(number, self.second + dz)
+        return value + self.box(number, self.second + dz)[...].astype(jnp.float32)
+
+    def along(self, number, dz):
+        self.box(number, dz * 2)[...] = self.both(number, dz).astype(jnp.bfloat16)
+        self._send(number, "line", dz)
+
+    def sides(self, *numbers):
+        return [(self.side, n, dz) for dz in self.far_first + [0] for n in numbers]
+
+    def lines(self, *numbers):
+        return [(self.along, n, dz) for dz in self.far_first for n in numbers]
+
+    def lasts(self, *numbers):
+        return [(self.last, n) for n in numbers]
+
+    def last(self, number):
+        total = self.both(number, 0)
+        for dz in self.far_first:
+            self._arrive(number, self.line + dz)
+            total = total + self.box(number, self.line + dz)[...].astype(jnp.float32)
+        self.chunks[number][1][...] = total
+
+    def drain(self):
+        for args in self.sent:
+            self._copy(*args).wait_send()
+        self.sent = []
+
+
+def scatter_slots(grid):
+    return 4 * grid.nz - 1
+bf16, f32 = jnp.bfloat16, jnp.float32
+NORM_EPSILON = 1e-06
+EARLY = 4
+AFTER_PROJECTION = 4
+GATHER_STEPS = 4
+AFTER_OUT = 4
+AFTER_NORM = 4
+ROOT_HALF = 0.7071067811865476
+PHI_SCALE = 0.3989422804014327
+
+
+def nn(a, b):
+    return jnp.dot(a, b, preferred_element_type=f32)
+
+
+def nt(a, b):
+    return lax.dot_general(a, b, (((1,), (1,)), ((), ())), preferred_element_type=f32)
+
+
+def aligned(start, size):
+    return pl.ds(pl.multiple_of(start, size), size)
+
+
+def unit_rows(values):
+    centred = values - jnp.mean(values, axis=-1, keepdims=True)
+    variance = jnp.mean(centred * centred, axis=-1, keepdims=True)
+    scale = lax.rsqrt(variance + NORM_EPSILON)
+    return centred * scale, scale
+
+
+def unit_back(grad_unit, unit, scale):
+    inner = (
+        grad_unit
+        - jnp.mean(grad_unit, axis=-1, keepdims=True)
+        - unit * jnp.mean(grad_unit * unit, axis=-1, keepdims=True)
+    )
+    return inner * scale
+
+
+def fold(rows):
+    return jnp.sum(rows.reshape(rows.shape[0] // 8, 8, rows.shape[1]), axis=0)
+
+
+def merged(*lists):
+    return [entry for row in itertools.zip_longest(*lists) for entry in row if entry is not None]
+
+
+class Pump:
+    def __init__(self, steps=()):
+        self.steps = list(steps)
+
+    def take(self, count=None):
+        count = len(self.steps) if count is None else min(count, len(self.steps))
+        taken, self.steps = self.steps[:count], self.steps[count:]
+        return taken
+
+    def run(self, count=None):
+        for function, *args in self.take(count):
+            function(*args)
+
+
+def at_trips(*shares):
+    def run(index):
+        for trip, share in enumerate(shares):
+
+            @pl.when(index == trip)
+            def _(share=share):
+                Pump(share).run()
+
+    return run
+
+
+def layer_body(
+    grid, rows,
+    tokens, cotangent, length, slopes, qv_part, ko_part, in_part, low_part, high_part, small,
+    output, grad_tokens, to_qv, to_ko, to_in, to_low, to_high, small_grads, probs_far,
+    w_qv, w_ko, w_gate, w_up, w_low, w_high, small_pair, small_tiles, every_small, small_box,
+    x, qkv, inverse, mixed, work, key_aug, value_aug, query_aug,
+    rows_f32, attended_low, branch_rows, outgoing, incoming, cot, turned,
+    grad_t, pair_b, grad_value_t, grad_key_t,
+    g_qv, g_ko, g_gate, g_up, g_low, g_high, box_qv, box_ko, box_gate, box_up, box_low, box_high,
+    gather_send, gather_recv, scatter_send, scatter_recv, small_send, small_recv, own_sem, swap_send, swap_recv, local_sem, prob_sem,
+):
+    grid.here()
+    side = lax.axis_index("tensor")
+    other = 1 - side
+    half = tokens.shape[0]
+    slots = 2 * half
+    width = tokens.shape[1]
+    heads_wide = mixed.shape[1]
+    units = w_gate.shape[1]
+    mine = aligned(side * half, half)
+    count = length[0]
+    attended, unit_one = rows_f32.at[:, pl.ds(0, width)], rows_f32.at[:, pl.ds(width, width)]
+    scale_one = rows_f32.at[:, pl.ds(2 * width, 128)]
+    block = 256
+    span = 2 * slots - block
+    bias = rows_f32.at[pl.ds(0, block), pl.ds(0, span)]
+
+    greet(grid, other)
+
+    gather = Gather(grid, [
+        (qv_part, w_qv, "zyx"),
+        (ko_part, w_ko, "zxy"),
+        (in_part.at[0], w_gate, "yzx"),
+        (in_part.at[1], w_up, "xzy"),
+        (low_part, w_low, "zyx"),
+        (high_part, w_high, "zxy"),
+        (small_pair, small_tiles, "zyx"),
+    ], gather_send, gather_recv)
+    scatter = Scatter(grid, rows, [
+        (g_qv, to_qv, "x", box_qv),
+        (g_ko, to_ko, "y", box_ko),
+        (g_gate, to_in.at[0], "x", box_gate),
+        (g_up, to_in.at[1], "y", box_up),
+        (g_low, to_low, "x", box_low),
+        (g_high, to_high, "y", box_high),
+    ], scatter_send, scatter_recv)
+    QV, KO, GATE, UP, LOW, HIGH, SMALL = range(7)
+
+    def swap(source, target, slot):
+        copy = remote(source, target, swap_send.at[slot], swap_recv.at[slot], tensor=other)
+        copy.start()
+        return copy
+
+    token_swap = swap(tokens, x.at[mine], 0)
+    token_copy = pltpu.make_async_copy(tokens, x.at[mine], local_sem.at[0])
+    token_copy.start()
+    cot_copy = pltpu.make_async_copy(cotangent, cot, local_sem.at[1])
+    cot_copy.start()
+    my_small = small_pair.at[:, pl.ds(pl.multiple_of(side * 128, 128), 128)]
+    small_copy = pltpu.make_async_copy(small, my_small, local_sem.at[4])
+    small_copy.start()
+    small_swap = swap(small, my_small, 8)
+    own_copies = []
+    for n, (source, target, _) in enumerate(gather.chunks[:SMALL]):
+        copy = pltpu.make_async_copy(source, target.at[aligned(grid.at(0, 0, 0) * rows, rows)], own_sem.at[n])
+        copy.start()
+        own_copies.append(copy)
+        for axis in gather.chunks[n][2]:
+            gather.send(n, (0, 0, 0), axis)
+        if n == KO:
+            small_copy.wait()
+            small_swap.wait()
+            for axis in gather.chunks[SMALL][2]:
+                gather.send(SMALL, (0, 0, 0), axis)
+            small_tiles[aligned(grid.at(0, 0, 0) * 16, 16), :] = small_pair[...]
+    near_units = merged(gather.second(GATE), gather.second(UP))
+    ends_first = merged(gather.first(LOW), gather.first(HIGH))
+    ends_second = merged(gather.second(LOW), gather.second(HIGH))
+    early = (
+        merged(gather.first(QV), gather.first(SMALL), gather.first(KO))
+        + merged(gather.first(GATE), gather.first(UP))
+        + merged(merged(gather.second(QV), gather.second(SMALL), gather.second(KO)), near_units[:EARLY])
+    )
+    pump = Pump(early)
+    pump.run()
+    pump = Pump(merged(near_units[EARLY:], ends_first) + ends_second)
+    for copy in own_copies:
+        copy.wait()
+    token_copy.wait()
+    token_swap.wait()
+    for number in (SMALL, QV, KO):
+        gather.finish(number)
+
+    norm_rows = jnp.zeros((8, width), f32)
+    head_rows = jnp.zeros((8, heads_wide), f32)
+    unit_rows_in = jnp.zeros((8, units), f32)
+
+    def at_lanes(tile, lanes, start):
+        wide = jnp.concatenate([tile, jnp.zeros((8, lanes - 128), f32)], axis=1)
+        return pltpu.roll(wide, start, 1) if start else wide
+
+    for i in range(grid.slots):
+        pair_tile = [small_tiles[16 * i : 16 * i + 8, 128 * s : 128 * s + 128] for s in range(2)]
+        unit_tile = [small_tiles[16 * i + 8 : 16 * i + 16, 128 * s : 128 * s + 128] for s in range(2)]
+        for s in range(2):
+            norm_rows = norm_rows + at_lanes(pair_tile[s], width, (2 * i + s) * (rows // 2))
+        units_here = jnp.where(side == 0, unit_tile[0], unit_tile[1])
+        unit_rows_in = unit_rows_in + at_lanes(units_here, units, i * (units // grid.slots))
+        head_rows = head_rows + at_lanes(pltpu.roll(units_here, 6, 0), heads_wide, i * (heads_wide // grid.slots))
+    every_small[0:8, :] = norm_rows
+    every_small[8:9, pl.ds(0, heads_wide)] = head_rows[0:1, :]
+    every_small[8:9, pl.ds(heads_wide, heads_wide)] = head_rows[1:2, :]
+    turned[0:8, :] = unit_rows_in
+
+    q_cols, v_cols, k_cols = (pl.ds(i * heads_wide, heads_wide) for i in range(3))
+    side_cols = pl.ds(pl.multiple_of(side * heads_wide, 128), heads_wide)
+    row_bias = every_small[8:9, :]
+    row_scale = jnp.where(lax.broadcasted_iota(jnp.int32, (1, 2 * heads_wide), 1) < heads_wide, 0.125, 1.0)
+
+    @pl.loop(0, slots // 256)
+    def _(i):
+        r = aligned(i * 256, 256)
+        raw = (nn(x[r, :], w_qv[...]) + row_bias).astype(bf16)
+        qkv[r, pl.ds(0, 2 * heads_wide)] = (raw.astype(f32) * row_scale).astype(bf16)
+        qkv[r, k_cols] = nn(x[r, :], w_ko[:, pl.ds(0, heads_wide)]).astype(bf16)
+
+    pump.run(AFTER_PROJECTION)
+
+    lane = lax.broadcasted_iota(jnp.int32, (slots, 128), 1)
+    slot = lax.broadcasted_iota(jnp.int32, (slots, 128), 0)
+    key_mask = jnp.where(slot < count, 0.0, -1e30).astype(bf16)
+    zero, one = jnp.zeros((), bf16), jnp.ones((), bf16)
+    block_lane = lax.broadcasted_iota(jnp.int32, (block, 128), 1)
+    pairs = heads_wide // 128
+
+    def prob_slot(upper):
+        return work.at[:, pl.ds(upper * slots, slots)]
+
+    def prob_out(pair, upper):
+        return pltpu.make_async_copy(prob_slot(upper), probs_far.at[2 * pair + upper], prob_sem.at[upper])
+
+    def prob_in(pair, upper):
+        return pltpu.make_async_copy(probs_far.at[2 * pair + upper], prob_slot(upper), prob_sem.at[upper])
+
+    def pair_cols(pair, start=0):
+        return pl.ds(pl.multiple_of(start + pair * 128, 128), 128)
+
+    def attend_pair(pair):
+        cols = pair_cols(pair)
+        for upper in (0, 1):
+            own = (lane >= 64) == (upper == 1)
+            spare = 0 if upper else 64
+            gap = jnp.abs(
+                lax.broadcasted_iota(jnp.int32, (block, span), 0)
+                - (lax.broadcasted_iota(jnp.int32, (block, span), 1) - (span - slots))
+            )
+            bias[...] = gap.astype(f32) * slopes[2 * pair + upper]
+            key_aug[...] = jnp.where(own, qkv[:, pair_cols(pair, 2 * heads_wide)], jnp.where(lane == spare, key_mask, zero))
+            value_aug[...] = jnp.where(own, qkv[:, pair_cols(pair, heads_wide)], one)
+            query_aug[...] = jnp.where(own, qkv[:, cols], jnp.where(lane == spare, one, zero))
+
+            @pl.when(pair > 0)
+            def _(upper=upper):
+                prob_out(pair - 1, upper).wait()
+
+            def attend(i, inner_carry, upper=upper):
+                r = aligned(i * block, block)
+                scores = nt(query_aug[r, :], key_aug[...]) - bias[:, pl.ds(pl.multiple_of(span - slots - i * block, block), slots)]
+                top = jnp.max(scores, axis=1, keepdims=True)
+                weights = jnp.exp(scores - top).astype(bf16)
+                work[r, pl.ds(upper * slots, slots)] = weights
+                product = nn(weights, value_aug[...])
+                scale = 1.0 / (product[:, 0:1] if upper else product[:, 64:65])
+                result = (product * scale).astype(bf16)
+                inverse[r, :] = jnp.where(block_lane == 2 * pair + upper, scale, inverse[r, :])
+                mixed[r, cols] = jnp.where(block_lane < 64, mixed[r, cols], result) if upper else result
+                return inner_carry
+
+            lax.fori_loop(0, slots // block, attend, 0, unroll=2)
+            prob_out(pair, upper).start()
+        between_pairs(pair)
+
+    inverse[...] = jnp.zeros_like(inverse)
+    between_pairs = at_trips(*(pump.take(GATHER_STEPS) for _ in range(pairs)))
+    pl.loop(0, pairs)(attend_pair)
+
+    def project(source, weights, target_rows, sink):
+        @pl.loop(0, half // 256)
+        def _(i):
+            r = aligned(target_rows * half + i * 256, 256)
+            sink(i, nt(source[r, :], weights[...]))
+
+    def to_outgoing(i, value):
+        outgoing[aligned(i * 256, 256), :] = value.astype(bf16)
+
+    def to_attended(i, value):
+        attended[aligned(i * 256, 256), :] = value
+
+    w_out = w_ko.at[:, pl.ds(heads_wide, heads_wide)]
+    project(mixed, w_out, other, to_outgoing)
+    first_swap = swap(outgoing, incoming.at[0], 1)
+    pump.run(AFTER_OUT)
+    project(mixed, w_out, side, to_attended)
+    first_swap.wait()
+    gain_one, gain_two = every_small[0:1, :], every_small[1:2, :]
+    step = 64
+
+    @pl.loop(0, half // step)
+    def _(i):
+        r = aligned(i * step, step)
+        own = pl.ds(pl.multiple_of(side * half + i * step, step), step)
+        total = x[own, :].astype(f32) + attended[r, :] + incoming[0, r, :].astype(f32) + every_small[2:3, :]
+        unit, scale = unit_rows(total)
+        result = unit * gain_one + every_small[3:4, :]
+        unit_one[r, :] = unit
+        scale_one[r, :] = jnp.broadcast_to(scale, (step, 128))
+        attended[r, :] = result
+        attended_low[own, :] = result.astype(bf16)
+
+    low_swap = swap(attended_low.at[mine], attended_low.at[mine], 2)
+    for upper in (0, 1):
+        prob_out(pairs - 1, upper).wait()
+    pump.run(AFTER_NORM)
+    gather.finish(GATE)
+    gather.finish(UP)
+
+    def feed(rows_side):
+        r = aligned(rows_side * half, half)
+
+        @pl.loop(0, units // 256)
+        def _(j):
+            c = aligned(j * 256, 256)
+            c_up = pl.ds(pl.multiple_of(units + j * 256, 256), 256)
+            c_hidden = pl.ds(pl.multiple_of(2 * units + j * 256, 256), 256)
+            gate = nn(attended_low[r, :], w_gate[:, c]) + turned[0:1, c]
+            up = nn(attended_low[r, :], w_up[:, c]) + turned[1:2, c]
+            below = 0.5 * (1.0 + lax.erf(gate * ROOT_HALF))
+            density = PHI_SCALE * jnp.exp(-0.5 * gate * gate)
+            bent = gate * below
+            work[r, c_hidden] = (bent * up).astype(bf16)
+            work[r, c] = (up * (below + gate * density)).astype(bf16)
+            work[r, c_up] = bent.astype(bf16)
+
+    feed(side)
+    pump.run()
+    low_swap.wait()
+    feed(other)
+    pump.run()
+    gather.finish(LOW)
+    gather.finish(HIGH)
+
+    hidden_low, hidden_high = pl.ds(2 * units, units // 2), pl.ds(2 * units + units // 2, units // 2)
+
+    def down(rows_side, sink):
+        @pl.loop(0, half // 256)
+        def _(i):
+            r = aligned(rows_side * half + i * 256, 256)
+            sink(i, nt(work[r, hidden_low], w_low[...]) + nt(work[r, hidden_high], w_high[...]))
+
+    def add_attended(i, value):
+        r = aligned(i * 256, 256)
+        attended[r, :] = attended[r, :] + value
+
+    down(other, to_outgoing)
+    second_swap = swap(outgoing, incoming.at[1], 3)
+    down(side, add_attended)
+    cot_copy.wait()
+    second_swap.wait()
+    nothing = jnp.zeros((8, width), f32)
+
+    def second_norm(i, carry):
+        sum_gain, sum_shift, sum_branch = carry
+        r = aligned(i * step, step)
+        own = pl.ds(pl.multiple_of(side * half + i * step, step), step)
+        position = side * half + i * step + lax.broadcasted_iota(jnp.int32, (step, 1), 0)
+        valid = jnp.where(position < count, 1.0, 0.0)
+        unit, scale = unit_rows(attended[r, :] + incoming[1, r, :].astype(f32) + every_small[4:5, :])
+        grad = cot[r, :].astype(f32) * valid
+        cot[r, :] = ((unit * gain_two + every_small[5:6, :]) * valid).astype(bf16)
+        back = unit_back(grad * gain_two, unit, scale)
+        attended[r, :] = back
+        branch_rows[own, :] = back.astype(bf16)
+        return sum_gain + fold(grad * unit), sum_shift + fold(grad), sum_branch + fold(back)
+
+    gain_two_sum, shift_two_sum, down_bias_sum = lax.fori_loop(0, half // step, second_norm, (nothing,) * 3)
+    branch_swap = swap(branch_rows.at[mine], branch_rows.at[mine], 4)
+    output_copy = pltpu.make_async_copy(cot, output, local_sem.at[2])
+    output_copy.start()
+    small_grads[...] = jnp.zeros_like(small_grads)
+    small_grads[1:2, :] = jnp.sum(gain_two_sum, axis=0, keepdims=True)
+    small_grads[5:6, :] = jnp.sum(shift_two_sum, axis=0, keepdims=True)
+    small_grads[4:5, :] = jnp.sum(down_bias_sum, axis=0, keepdims=True)
+    branch_swap.wait()
+
+    def turn(source):
+        @pl.loop(0, slots // 256)
+        def _(i):
+            r = aligned(i * 256, 256)
+            grad_t[:, r] = source[r, :].T
+
+    def weight_grad(sink, source, source_start, tile):
+        @pl.loop(0, sink.shape[1] // tile)
+        def _(j):
+            sink[:, aligned(j * tile, tile)] = nn(
+                grad_t[...], source[:, pl.ds(pl.multiple_of(source_start + j * tile, tile), tile)]
+            ).astype(bf16)
+
+    turn(branch_rows)
+    weight_grad(g_low, work, 2 * units, 256)
+    scatter.begin(LOW)
+    weight_grad(g_high, work, 2 * units + units // 2, 256)
+    scatter.begin(HIGH)
+
+    turned[8:24, :] = jnp.zeros((16, units), f32)
+    for index, weights in enumerate((w_low, w_high)):
+        @pl.loop(0, units // 2 // 256)
+        def _(j, index=index, weights=weights):
+            c = pl.ds(pl.multiple_of(index * (units // 2) + j * 256, 256), 256)
+            c_up = pl.ds(pl.multiple_of(units + index * (units // 2) + j * 256, 256), 256)
+            for part in range(2):
+                r = pl.ds(part * half, half)
+                grad = nn(branch_rows[r, :], weights[:, aligned(j * 256, 256)])
+                gate_grad = (grad * work[r, c].astype(f32)).astype(bf16)
+                up_grad = (grad * work[r, c_up].astype(f32)).astype(bf16)
+                work[r, c] = gate_grad
+                work[r, c_up] = up_grad
+                turned[8:16, c] = turned[8:16, c] + fold(gate_grad.astype(f32))
+                turned[16:24, c] = turned[16:24, c] + fold(up_grad.astype(f32))
+
+    for index in range(2):
+        total = jnp.sum(turned[8 + 8 * index : 16 + 8 * index, :], axis=0, keepdims=True)
+        for j in range(units // width):
+            small_grads[pl.ds(8 + 4 * index + 2 * side + j, 1), :] = total[:, j * width : (j + 1) * width]
+
+    Pump(scatter.sides(LOW, HIGH)).run()
+    turn(attended_low)
+    weight_grad(g_gate, work, 0, 512)
+    scatter.begin(GATE, 1)
+    weight_grad(g_up, work, units, 512)
+    scatter.begin(UP, 1)
+    scatter.begin(GATE, 0)
+
+    gate_cols, up_cols = pl.ds(0, units), pl.ds(units, units)
+
+    def units_back(rows_side, sink):
+        @pl.loop(0, half // 256)
+        def _(i):
+            r = aligned(rows_side * half + i * 256, 256)
+            sink(i, nt(work[r, gate_cols], w_gate[...]) + nt(work[r, up_cols], w_up[...]))
+
+    units_back(other, to_outgoing)
+    third_swap = swap(outgoing, incoming.at[0], 5)
+    units_back(side, add_attended)
+    Pump(scatter.lines(LOW, HIGH)).run()
+    third_swap.wait()
+
+    def first_norm_back(i, carry):
+        sum_gain, sum_shift, sum_branch = carry
+        r = aligned(i * step, step)
+        own = pl.ds(pl.multiple_of(side * half + i * step, step), step)
+        grad = attended[r, :] + incoming[0, r, :].astype(f32)
+        unit = unit_one[r, :]
+        back = unit_back(grad * gain_one, unit, scale_one[r, 0:1])
+        attended[r, :] = back
+        branch_rows[own, :] = back.astype(bf16)
+        return sum_gain + fold(grad * unit), sum_shift + fold(grad), sum_branch + fold(back)
+
+    prob_in(0, 0).start()
+    prob_in(0, 1).start()
+    gain_one_sum, shift_one_sum, out_bias_sum = lax.fori_loop(0, half // step, first_norm_back, (nothing,) * 3)
+    attn_swap = swap(branch_rows.at[mine], branch_rows.at[mine], 6)
+    small_grads[0:1, :] = jnp.sum(gain_one_sum, axis=0, keepdims=True)
+    small_grads[3:4, :] = jnp.sum(shift_one_sum, axis=0, keepdims=True)
+    small_grads[2:3, :] = jnp.sum(out_bias_sum, axis=0, keepdims=True)
+    attn_swap.wait()
+
+    grad_mixed = attended_low.at[:, pl.ds(0, heads_wide)]
+    turn(branch_rows)
+    g_ko[:, pl.ds(heads_wide, heads_wide)] = nn(grad_t[...], mixed[...]).astype(bf16)
+    sides_gate = Pump(scatter.sides(GATE))
+    sides_gate.run(2)
+
+    @pl.loop(0, slots // 256)
+    def _(i):
+        r = aligned(i * 256, 256)
+        grad_mixed[r, :] = nn(branch_rows[r, :], w_out[...]).astype(bf16)
+
+    sides_gate.run()
+    scatter.begin(UP, 0)
+
+    mixed_t, query_t = pair_b.at[0], pair_b.at[1]
+
+    def pair_back(pair):
+        cols, key_cols, value_cols = pair_cols(pair), pair_cols(pair, 2 * heads_wide), pair_cols(pair, heads_wide)
+        scales = inverse[...]
+        shrink = jnp.where(
+            lane < 64,
+            jnp.sum(jnp.where(lane == 2 * pair, scales, 0.0), axis=1, keepdims=True),
+            jnp.sum(jnp.where(lane == 2 * pair + 1, scales, 0.0), axis=1, keepdims=True),
+        )
+        scaled = (grad_mixed[:, cols].astype(f32) * shrink).astype(bf16)
+        mixed_t[...] = scaled.T
+        query_t[...] = qkv[:, cols].T
+        outgoing_pair[...] = scaled
+        for upper in (0, 1):
+            own = (lane >= 64) == (upper == 1)
+            spare = 0 if upper else 64
+            scaled = outgoing_pair[...]
+            dots = jnp.sum(jnp.where(own, scaled.astype(f32) * mixed[:, cols].astype(f32), 0.0), axis=1, keepdims=True)
+            dots_high = dots.astype(bf16)
+            dots_low = (dots - dots_high.astype(f32)).astype(bf16)
+            ones = (lane == spare) | (lane == spare + 1)
+            value_aug[...] = jnp.where(own, qkv[:, value_cols], jnp.where(ones, one, zero))
+            query_aug[...] = jnp.where(
+                own, scaled, jnp.where(lane == spare, -dots_high, jnp.where(lane == spare + 1, -dots_low, zero))
+            )
+            part = pl.ds(64 * upper, 64)
+            base = upper * slots
+            prob_in(pair, upper).wait()
+            for j in range(slots // 512):
+                c = pl.ds(j * 512, 512)
+                grad_value_t[part, c] = nn(mixed_t[part, :], work[:, pl.ds(base + j * 512, 512)]).astype(bf16)
+
+            def attend_back(i, inner_carry, upper=upper, base=base):
+                r = aligned(i * block, block)
+                inner = nt(query_aug[r, :], value_aug[...])
+                grads = (work[r, pl.ds(base, slots)].astype(f32) * inner).astype(bf16)
+                work[r, pl.ds(base, slots)] = grads
+                result = (nn(grads, qkv[:, key_cols]) * 0.125).astype(bf16)
+                qkv[r, cols] = jnp.where(block_lane < 64, qkv[r, cols], result) if upper else result
+                return inner_carry
+
+            lax.fori_loop(0, slots // block, attend_back, 0, unroll=2)
+            for j in range(slots // 512):
+                c = pl.ds(j * 512, 512)
+                grad_key_t[part, c] = nn(query_t[part, :], work[:, pl.ds(base + j * 512, 512)]).astype(bf16)
+
+            @pl.when(pair + 1 < pairs)
+            def _(upper=upper):
+                prob_in(pair + 1, upper).start()
+
+        qkv[:, value_cols] = grad_value_t[...].T
+        qkv[:, key_cols] = grad_key_t[...].T
+        between_pairs(pair)
+
+    outgoing_pair = key_aug
+    between_pairs = at_trips(scatter.sides(UP), scatter.lasts(LOW, HIGH), scatter.lines(GATE))
+    pl.loop(0, pairs)(pair_back)
+
+    turn(x)
+    g_qv[...] = nn(grad_t[...], qkv[:, pl.ds(0, 2 * heads_wide)]).astype(bf16)
+    scatter.begin(QV)
+    g_ko[:, pl.ds(0, heads_wide)] = nn(grad_t[...], qkv[:, k_cols]).astype(bf16)
+    scatter.begin(KO)
+    def column_sum(cols):
+        def add(i, carry):
+            return carry + fold(qkv[aligned(i * 128, 128), cols].astype(f32))
+
+        return jnp.sum(lax.fori_loop(0, slots // 128, add, jnp.zeros((8, heads_wide), f32)), axis=0, keepdims=True)
+
+    small_grads[6:7, side_cols] = column_sum(q_cols)
+    small_grads[7:8, side_cols] = column_sum(v_cols)
+    sums = SmallSum(grid, small_grads, small_grads, small_box, small_send, small_recv)
+    sums.stage(0)
+
+    def inputs_back(rows_side, sink):
+        @pl.loop(0, half // 256)
+        def _(i):
+            r = aligned(rows_side * half + i * 256, 256)
+            sink(
+                i,
+                nt(qkv[r, pl.ds(0, 2 * heads_wide)], w_qv[...]) + nt(qkv[r, k_cols], w_ko[:, pl.ds(0, heads_wide)]),
+            )
+
+    inputs_back(other, to_outgoing)
+    fourth_swap = swap(outgoing, incoming.at[1], 7)
+    sums.stage(1)
+    inputs_back(side, add_attended)
+    fourth_swap.wait()
+
+    @pl.loop(0, half // step)
+    def _(i):
+        r = aligned(i * step, step)
+        attended[r, :] = attended[r, :] + incoming[1, r, :].astype(f32)
+
+    tokens_copy = pltpu.make_async_copy(attended, grad_tokens, local_sem.at[3])
+    tokens_copy.start()
+    sums.stage(2)
+    Pump(scatter.lines(UP) + scatter.sides(QV, KO)).run()
+    sums.stage(3)
+    Pump(scatter.lasts(GATE, UP) + scatter.lines(QV, KO) + scatter.lasts(QV, KO)).run()
+    sums.stage(4)
+    output_copy.wait()
+    tokens_copy.wait()
+    gather.drain()
+    scatter.drain()
+
+
+def layer_call(grid, tokens, cotangent, lengths, slopes, qv_part, ko_part, in_part, low_part, high_part, small):
+    rows, wide = qv_part.shape
+    width = rows * grid.nz * 4
+    half = tokens.shape[0]
+    slots = 2 * half
+    heads_wide = wide // 2
+    units = in_part.shape[2]
+    heads = heads_wide // HEAD
+    shapes = [
+        jax.ShapeDtypeStruct((half, width), bf16),
+        jax.ShapeDtypeStruct((half, width), f32),
+        jax.ShapeDtypeStruct(qv_part.shape, f32),
+        jax.ShapeDtypeStruct(ko_part.shape, f32),
+        jax.ShapeDtypeStruct(in_part.shape, f32),
+        jax.ShapeDtypeStruct(low_part.shape, f32),
+        jax.ShapeDtypeStruct(high_part.shape, f32),
+        jax.ShapeDtypeStruct((16, width), f32),
+        jax.ShapeDtypeStruct((heads, slots, slots), bf16),
+    ]
+    vmem = pl.BlockSpec(memory_space=pltpu.VMEM)
+    smem = pl.BlockSpec(memory_space=pltpu.SMEM)
+    anywhere = pl.BlockSpec(memory_space=pl.ANY)
+    smalls = small_slots(grid)
+    dma = pltpu.SemaphoreType.DMA
+    wides = (wide, wide, units, units, units // 2, units // 2)
+    scratch = (
+        [pltpu.VMEM((width, w), bf16) for w in wides]
+        + [
+            pltpu.VMEM((16, 256), f32),
+            pltpu.VMEM((16 * grid.slots, 256), f32),
+            pltpu.VMEM((16, width), f32),
+            pltpu.VMEM((smalls, 16, width), f32),
+            pltpu.VMEM((slots, width), bf16),
+            pltpu.VMEM((slots, 3 * heads_wide), bf16),
+            pltpu.VMEM((slots, 128), f32),
+            pltpu.VMEM((slots, heads_wide), bf16),
+            pltpu.VMEM((slots, 3 * units), bf16),
+            pltpu.VMEM((slots, 128), bf16),
+            pltpu.VMEM((slots, 128), bf16),
+            pltpu.VMEM((slots, 128), bf16),
+            pltpu.VMEM((half, max(2 * slots - 256, 2 * width + 128)), f32),
+            pltpu.VMEM((slots, width), bf16),
+            pltpu.VMEM((slots, width), bf16),
+            pltpu.VMEM((half, width), bf16),
+            pltpu.VMEM((2, half, width), bf16),
+            pltpu.VMEM((half, width), bf16),
+            pltpu.VMEM((24, units), f32),
+            pltpu.VMEM((width, slots), bf16),
+            pltpu.VMEM((2, 128, slots), bf16),
+            pltpu.VMEM((128, slots), bf16),
+            pltpu.VMEM((128, slots), bf16),
+        ]
+        + [pltpu.VMEM((width, w), bf16) for w in wides]
+        + [pltpu.VMEM((scatter_slots(grid), rows, w), bf16) for w in wides]
+        + [
+            dma((7, grid.slots)),
+            dma((7, grid.slots)),
+            dma((6, scatter_slots(grid))),
+            dma((6, scatter_slots(grid))),
+            dma((smalls,)),
+            dma((smalls,)),
+            dma((6,)),
+            dma((9,)),
+            dma((9,)),
+            dma((5,)),
+            dma((2,)),
+        ]
+    )
+    results = pl.pallas_call(
+        functools.partial(layer_body, grid, rows),
+        out_shape=shapes,
+        in_specs=[anywhere, anywhere, smem, smem] + [anywhere] * 6,
+        out_specs=[anywhere] * 2 + [vmem] * 6 + [anywhere],
+        scratch_shapes=scratch,
+        compiler_params=pltpu.CompilerParams(collective_id=0, has_side_effects=True, vmem_limit_bytes=VMEM_LIMIT),
+        name="layer",
+    )(tokens, cotangent, lengths, slopes, qv_part, ko_part, in_part, low_part, high_part, small)
+    return results[:8]
 
 
 norm_epsilon = 1e-06
@@ -118,7 +1047,45 @@
     )
 
 
+def spread(part, index, count):
+    wide = jnp.tile(part, (1, count))
+    owner = lax.broadcasted_iota(jnp.int32, wide.shape, 1) // part.shape[1]
+    return jnp.where(owner == index, wide.astype(jnp.float32), 0.0)
+
+
+def pick(whole, index, count):
+    size = whole.shape[1] // count
+    return lax.dynamic_slice_in_dim(whole, index * size, size, 1)
+
+
+def pack_small(biases_qv, biases_in, rows_all, piece, pieces):
+    width = rows_all.shape[1]
+    halves = [b if pieces == 1 else spread(b, piece, pieces) for b in (biases_qv, biases_in)]
+    rows = [rows_all] + [h.reshape(-1, width) for h in halves]
+    packed = jnp.concatenate(rows, axis=0)
+    return jnp.pad(packed, ((0, -packed.shape[0] % 8), (0, 0)))
+
+
+def small_tile(norm_gains, offsets, qv_bias, in_bias):
+    def rows(part, count):
+        return jnp.pad(part.astype(f32), ((0, count - part.shape[0]), (0, 128 - part.shape[1])))
+
+    return jnp.concatenate(
+        [rows(norm_gains, 2), rows(offsets, 6), rows(in_bias, 2), rows(qv_bias, 6)], axis=0
+    )
+
+
+def unpack_small(packed, width_qv, width_in, piece, pieces):
+    width = packed.shape[1]
+    count_qv = 2 * width_qv * pieces // width
+    count_in = 2 * width_in * pieces // width
+    whole_qv = packed[6 : 6 + count_qv].reshape(2, -1)
+    whole_in = packed[6 + count_qv : 6 + count_qv + count_in].reshape(2, -1)
+    return packed[:6], pick(whole_qv, piece, pieces), pick(whole_in, piece, pieces)
+
+
 def per_device(
+    direct,
     tokens,
     lengths,
     qkv_weight,
@@ -132,8 +1099,12 @@
     cotangent,
 ):
     row_count = tokens.shape[0]
+    dp = lax.axis_size("dp")
     pieces = lax.axis_size("tensor")
     piece_index = lax.axis_index("tensor")
+    dp_index = lax.axis_index("dp")
+    flat_index = dp_index * pieces + piece_index
+    grid = Grid3(dp)
     slot_count = row_count * pieces
     length = lengths[0]
     heads_here = qkv_weight.shape[2] // HEAD
@@ -143,54 +1114,73 @@
     row_valid = (piece_index * row_count + lax.iota(jnp.int32, row_count) < length).astype(
         jnp.float32
     )[:, None]
-    gains, shift_rows = (
-        lax.all_gather(norm_gains, ("dp", "tensor"), axis=1, tiled=True),
-        lax.all_gather(offsets, ("dp", "tensor"), axis=1, tiled=True),
-    )
-
-    def fetch_weights():
+
+    width_qv, width_in = qkv_weight.shape[2], in_weight.shape[2]
+    if direct:
+        middle = down_weight.shape[0] // 2
+        output, grad_tokens, shard_qv, shard_ko, shard_in, shard_low, shard_high, small_grads = layer_call(
+            grid,
+            tokens,
+            cotangent,
+            lengths,
+            slopes,
+            jnp.concatenate([qkv_weight[0], qkv_weight[2]], axis=1),
+            jnp.concatenate([qkv_weight[1], out_weight.T], axis=1),
+            in_weight,
+            down_weight[:middle].T,
+            down_weight[middle:].T,
+            small_tile(norm_gains, offsets, qv_bias, in_bias),
+        )
+        shard_wqkv = jnp.stack([shard_qv[:, :width_qv], shard_ko[:, :width_qv], shard_qv[:, width_qv:]])
+        shard_out_t = shard_ko[:, width_qv:]
+        shard_down_t = jnp.concatenate([shard_low, shard_high], axis=1)
+        row_grads, bqv_grads, bin_grads = unpack_small(small_grads, width_qv, width_in, piece_index, pieces)
+        own_rows = pick(row_grads, flat_index, dp * pieces)
         return (
-            lax.all_gather(qkv_weight, "dp", axis=1, tiled=True),
-            lax.all_gather(qv_bias, "dp", axis=1, tiled=True),
-            lax.all_gather(out_weight, "dp", axis=1, tiled=True),
-            lax.all_gather(in_weight, "dp", axis=1, tiled=True),
-            lax.all_gather(in_bias, "dp", axis=1, tiled=True),
-            lax.all_gather(down_weight, "dp", axis=1, tiled=True),
+            output,
+            grad_tokens,
+            shard_wqkv,
+            pick(bqv_grads, dp_index, dp),
+            shard_out_t.T,
+            shard_in,
+            pick(bin_grads, dp_index, dp),
+            shard_down_t.T,
+            own_rows[:2],
+            own_rows[2:],
         )
-
-    def attention_inputs(whole_qkv, whole_bqv):
-        gathered = lax.all_gather(tokens, "tensor", axis=0, tiled=True)
-        projected = jnp.einsum(
-            "sd,kdc->ksc", gathered, whole_qkv, preferred_element_type=jnp.float32
-        )
-        queries = (projected[0] + whole_bqv[0].astype(jnp.float32)).astype(jnp.bfloat16)
-        key_rows = projected[1].astype(jnp.bfloat16)
-        value_rows = (projected[2] + whole_bqv[1].astype(jnp.float32)).astype(jnp.bfloat16)
-        mixed_heads, logsum = attend(queries, key_rows, value_rows, slopes, key_valid)
-        return (gathered, queries, key_rows, value_rows, mixed_heads, logsum)
-
-    def feed_inputs(whole_in, whole_bin, attended_low):
-        gathered_ff = lax.all_gather(attended_low, "tensor", axis=0, tiled=True)
-        pre_acts = jnp.einsum(
-            "sd,kdc->ksc", gathered_ff, whole_in, preferred_element_type=jnp.float32
-        )
-        pre_acts = pre_acts + whole_bin.astype(jnp.float32)[:, None, :]
-        hidden = (jax.nn.gelu(pre_acts[0], approximate=False) * pre_acts[1]).astype(jnp.bfloat16)
-        return (gathered_ff, pre_acts, hidden)
-
-    whole_qkv, whole_bqv, whole_out, whole_in, whole_bin, whole_down = fetch_weights()
-    gathered, queries, key_rows, value_rows, mixed_heads, logsum = attention_inputs(
-        whole_qkv, whole_bqv
-    )
-    attn_part = jnp.dot(mixed_heads, whole_out, preferred_element_type=jnp.float32)
+    parts = (qkv_weight, out_weight.T, in_weight, down_weight.T)
+    small = pack_small(
+        spread(qv_bias, dp_index, dp),
+        spread(in_bias, dp_index, dp),
+        jnp.concatenate([spread(norm_gains, flat_index, dp * pieces), spread(offsets, flat_index, dp * pieces)]),
+        piece_index,
+        pieces,
+    )
+    whole_qkv, whole_out_t, whole_in, whole_down_t = (
+        lax.all_gather(p, "dp", axis=p.ndim - 2, tiled=True) for p in parts
+    )
+    small = lax.psum(small, ("dp", "tensor"))
+    rows_all, whole_bqv, whole_bin = unpack_small(small, width_qv, width_in, piece_index, pieces)
+    gains, shift_rows = rows_all[:2], rows_all[2:6]
+
+    gathered = lax.all_gather(tokens, "tensor", axis=0, tiled=True)
+    projected = jnp.einsum("sd,kdc->ksc", gathered, whole_qkv, preferred_element_type=jnp.float32)
+    queries = (projected[0] + whole_bqv[0]).astype(jnp.bfloat16)
+    key_rows = projected[1].astype(jnp.bfloat16)
+    value_rows = (projected[2] + whole_bqv[1]).astype(jnp.bfloat16)
+    mixed_heads, logsum = attend(queries, key_rows, value_rows, slopes, key_valid)
+    attn_part = jnp.einsum("sc,dc->sd", mixed_heads, whole_out_t, preferred_element_type=jnp.float32)
     attn_total = lax.psum_scatter(
         attn_part.astype(jnp.bfloat16), "tensor", scatter_dimension=0, tiled=True
     ).astype(jnp.float32)
     first_in = tokens.astype(jnp.float32) + attn_total + shift_rows[0]
     attended, unit_one, scale_one = norm_forward(first_in, gains[0], shift_rows[1])
     attended_low = attended.astype(jnp.bfloat16)
-    gathered_ff, pre_acts, hidden = feed_inputs(whole_in, whole_bin, attended_low)
-    ff_part = jnp.dot(hidden, whole_down, preferred_element_type=jnp.float32)
+    gathered_ff = lax.all_gather(attended_low, "tensor", axis=0, tiled=True)
+    pre_acts = jnp.einsum("sd,kdc->ksc", gathered_ff, whole_in, preferred_element_type=jnp.float32)
+    pre_acts = pre_acts + whole_bin[:, None, :]
+    hidden = (jax.nn.gelu(pre_acts[0], approximate=False) * pre_acts[1]).astype(jnp.bfloat16)
+    ff_part = jnp.einsum("sf,df->sd", hidden, whole_down_t, preferred_element_type=jnp.float32)
     ff_total = lax.psum_scatter(
         ff_part.astype(jnp.bfloat16), "tensor", scatter_dimension=0, tiled=True
     ).astype(jnp.float32)
@@ -202,13 +1192,9 @@
         grad_final, unit_two, scale_two, gains[1]
     )
     grad_bdown = jnp.sum(grad_second, axis=0)
-    whole_qkv, whole_bqv, whole_out, whole_in, whole_bin, whole_down = fetch_weights()
-    gathered_ff, pre_acts, hidden = feed_inputs(whole_in, whole_bin, attended_low)
     grad_ff_rows = lax.all_gather(grad_second.astype(jnp.bfloat16), "tensor", axis=0, tiled=True)
-    grad_down = jnp.einsum("sf,sd->fd", hidden, grad_ff_rows, preferred_element_type=jnp.float32)
-    grad_hidden = jnp.einsum(
-        "sd,fd->sf", grad_ff_rows, whole_down, preferred_element_type=jnp.float32
-    )
+    grad_down_t = jnp.einsum("sd,sf->df", grad_ff_rows, hidden, preferred_element_type=jnp.float32)
+    grad_hidden = jnp.einsum("sd,df->sf", grad_ff_rows, whole_down_t, preferred_element_type=jnp.float32)
     pullback = jax.vjp(
         lambda gate_pre, up_pre: jax.nn.gelu(gate_pre, approximate=False) * up_pre,
         pre_acts[0],
@@ -226,15 +1212,10 @@
         grad_attended, unit_one, scale_one, gains[0]
     )
     grad_bout = jnp.sum(grad_first, axis=0)
-    gathered, queries, key_rows, value_rows, mixed_heads, logsum = attention_inputs(
-        whole_qkv, whole_bqv
-    )
     grad_attn_rows = lax.all_gather(grad_first.astype(jnp.bfloat16), "tensor", axis=0, tiled=True)
-    grad_out = jnp.einsum(
-        "sc,sd->cd", mixed_heads, grad_attn_rows, preferred_element_type=jnp.float32
-    )
+    grad_out_t = jnp.einsum("sd,sc->dc", grad_attn_rows, mixed_heads, preferred_element_type=jnp.float32)
     grad_mixed = jnp.einsum(
-        "sd,cd->sc", grad_attn_rows, whole_out, preferred_element_type=jnp.float32
+        "sd,dc->sc", grad_attn_rows, whole_out_t, preferred_element_type=jnp.float32
     ).astype(jnp.bfloat16)
     grad_queries, grad_keys, grad_values = attend_back(
         queries, key_rows, value_rows, grad_mixed, logsum, slopes, key_valid
@@ -251,31 +1232,32 @@
     grad_tokens = grad_first + lax.psum_scatter(
         input_back.astype(jnp.bfloat16), "tensor", scatter_dimension=0, tiled=True
     ).astype(jnp.float32)
-    shard_wqkv, shard_bqv, shard_out, shard_in, shard_bin, shard_down = (
-        lax.psum_scatter(grad_wqkv, "dp", scatter_dimension=1, tiled=True),
-        lax.psum_scatter(grad_bqv, "dp", scatter_dimension=1, tiled=True),
-        lax.psum_scatter(grad_out, "dp", scatter_dimension=1, tiled=True),
-        lax.psum_scatter(grad_in, "dp", scatter_dimension=1, tiled=True),
-        lax.psum_scatter(grad_bin, "dp", scatter_dimension=1, tiled=True),
-        lax.psum_scatter(grad_down, "dp", scatter_dimension=1, tiled=True),
-    )
-    gain_grads = jnp.stack([grad_gain_one, grad_gain_two])
-    offset_grads = jnp.stack([grad_bout, grad_shift_one, grad_bdown, grad_shift_two])
-    shard_gains, shard_offsets = (
-        lax.psum_scatter(gain_grads, ("dp", "tensor"), scatter_dimension=1, tiled=True),
-        lax.psum_scatter(offset_grads, ("dp", "tensor"), scatter_dimension=1, tiled=True),
-    )
+
+    small_grads = pack_small(
+        grad_bqv,
+        grad_bin,
+        jnp.stack([grad_gain_one, grad_gain_two, grad_bout, grad_shift_one, grad_bdown, grad_shift_two]),
+        piece_index,
+        pieces,
+    )
+    grads = tuple(g.astype(jnp.bfloat16) for g in (grad_wqkv, grad_out_t, grad_in, grad_down_t))
+    shard_wqkv, shard_out_t, shard_in, shard_down_t = (
+        lax.psum_scatter(g.astype(jnp.float32), "dp", scatter_dimension=g.ndim - 2, tiled=True) for g in grads
+    )
+    small_grads = lax.psum(small_grads, ("dp", "tensor"))
+    row_grads, bqv_grads, bin_grads = unpack_small(small_grads, width_qv, width_in, piece_index, pieces)
+    own_rows = pick(row_grads, flat_index, dp * pieces)
     return (
         output,
         grad_tokens,
         shard_wqkv,
-        shard_bqv,
-        shard_out,
+        pick(bqv_grads, dp_index, dp),
+        shard_out_t.T,
         shard_in,
-        shard_bin,
-        shard_down,
-        shard_gains,
-        shard_offsets,
+        pick(bin_grads, dp_index, dp),
+        shard_down_t.T,
+        own_rows[:2],
+        own_rows[2:],
     )
 
 
@@ -293,21 +1275,27 @@
         P(None, ("dp", "tensor")),
         P(("dp", "tensor"), None),
     )
-    return jax.shard_map(
-        per_device,
-        mesh=mesh,
-        in_specs=placed,
-        out_specs=(
-            P(("dp", "tensor"), None),
-            P(("dp", "tensor"), None),
-            P(None, "dp", "tensor"),
-            P(None, ("tensor", "dp")),
-            P("tensor", "dp"),
-            P(None, "dp", "tensor"),
-            P(None, ("tensor", "dp")),
-            P("tensor", "dp"),
-            P(None, ("dp", "tensor")),
-            P(None, ("dp", "tensor")),
-        ),
-        check_vma=False,
-    )
+
+    def run(*args):
+        dp = mesh.shape["dp"]
+        direct = dp % 4 == 0 and (args[2].shape[1] // dp) % 16 == 0 and mesh.shape["tensor"] == 2
+        return jax.shard_map(
+            functools.partial(per_device, direct),
+            mesh=mesh,
+            in_specs=placed,
+            out_specs=(
+                P(("dp", "tensor"), None),
+                P(("dp", "tensor"), None),
+                P(None, "dp", "tensor"),
+                P(None, ("tensor", "dp")),
+                P("tensor", "dp"),
+                P(None, "dp", "tensor"),
+                P(None, ("tensor", "dp")),
+                P("tensor", "dp"),
+                P(None, ("dp", "tensor")),
+                P(None, ("dp", "tensor")),
+            ),
+            check_vma=False,
+        )(*args)
+
+    return run

time: 1320 us -> 234 us (0.18)
  waiting for transfers between devices: 704 us -> 0 us
  blocking collectives: 285 us -> 0 us
  Pallas kernels: 0 us -> 212 us
  matrix products: 161 us -> 0 us
  other arithmetic: 75.2 us -> 6.99 us
  local copies, waits for them, and re-layouts: 56.4 us -> 13 us
  between operations: 16.6 us -> 1.33 us
    unnamed x17 -> x0, waiting for transfers between devices: 319 us -> none
    reduce_scatter x6 -> x0, waiting for transfers between devices: 286 us -> none  [the longest x1 143 us: per_device(): lax.psum_scatter(grad_down, 'dp', scatter_dimension=1, tiled=True)]
    pallas_call x0 -> x1, Pallas kernels: none -> 212 us  [layer_call(): pl.pallas_call(functools.partial(layer_body, grid, rows), out_shape=shape...]
    all_gather x5 -> x0, blocking collectives: 199 us -> none  [the longest x1 42.9 us: fetch_weights(): lax.all_gather(out_weight, 'dp', axis=1, tiled=True)]
    dot_general x28 -> x0, matrix products: 140 us -> none  [the longest x4 22.5 us: score_block(): jnp.einsum('qhc,khc->hqk', query_heads, key_heads, preferred_element_type...]
    all_gather x7 -> x0, waiting for transfers between devices: 100 us -> none  [the longest x1 52.2 us: fetch_weights(): lax.all_gather(in_weight, 'dp', axis=1, tiled=True)]
    unnamed x2 -> x0, blocking collectives: 86 us -> none
    convert_element_type x16 -> x0, other arithmetic: 35.8 us -> none  [the longest x1 14.8 us: feed_inputs(): (jax.nn.gelu(pre_acts[0], approximate=False) * pre_acts[1]).astype(jnp.bf...]
  transfers between devices with their start and end apart: 15 -> 0, of which waited for: 8 -> 0; matrix products, arithmetic and copies ran while one was open for 14% -> 0% of each run, Pallas kernels for 0% -> 0%
where the time goes in v2:
time: 234 us; the launch traced here: 233 us
  Pallas kernels  212 us (91%)
  local copies, waits for them, and re-layouts  13 us (6%)
  other arithmetic  6.99 us (3%)
    pallas_call x1, Pallas kernels, layer_call(): pl.pallas_call(functools.partial(layer_body, grid, rows), out_shape=shape...  212 us

profile of v2, /device:TPU:0, one launch (start us, length us, event | category | flops | bytes accessed | tf_op | source)
XLA Modules:
  0.0 233.1 jit_solution(8840896374189182108)
XLA Ops:
  0.6 0.8 slice_bitcast_fusion.6
  1.5 1.4 pad_maximum_fusion.1
  2.9 0.5 multiply_exponential_fusion.slopes
  3.4 1.6 slice_bitcast_fusion.4
  5.0 0.7 pad_convert_fusion
  5.7 0.7 pad_convert_fusion.1
  6.3 1.3 fusion.1.small
  8.3 211.8 %layer.1 = (bf16[512,768]{1,0:T(8,128)(2,1)}, f32[512,768]{1,0:T(8,128)}, f32[48,768]{1,0:T(8,128)}, f32[48,768]{1,0:T(8,128)}, f32[2,48,1536]{2,1,0:T(8,128)}, ...) custom-call(bf16[512,768]{1,0:T(8,128)(2,1)} %tokens.1, ...), custom_call_target="tpu_custom_call" | custom-call | tf_op jit(solution)/shard_map/layer/pallas_call | solution.py:926
  220.0 0.0 copy-start.1
  220.1 1.6 slice_bitcast_fusion
  221.7 0.0 copy-start
  221.7 1.0 slice_bitcast_fusion.3
  222.7 0.7 pad_maximum_fusion
  223.5 0.7 slice.52
  224.2 0.6 constant_dynamic-slice_fusion.1
  224.9 0.7 slice.50
  225.6 0.6 constant_dynamic-slice_fusion.2
  226.2 0.7 slice.53
  227.0 0.1 constant_dynamic-slice_fusion
  227.0 0.6 slice.55
  227.6 0.6 slice.54
  228.2 1.7 maximum_bitcast_fusion
  229.9 0.0 copy-done.1
  229.9 0.9 copy.25
  230.8 0.0 copy-done
  230.8 0.0 copy-start.2
  230.8 1.1 copy.26
  231.9 0.3 copy-done.2
  232.3 0.8 copy.27
  (1 shorter events, 0.0 us)
Async XLA Ops:
  220.0 9.9 %copy-start.1 = (bf16[512,768]{1,0:T(8,128)(2,1)S(1)}, bf16[512,768]{1,0:T(8,128)(2,1)}, u32[]{:S(2)}) copy-start(bf16[512,768]{1,0:T(8,128)(2,1)} %get-tuple-element.47) | copy-start | bytes 2359300
  221.7 9.1 %copy-start = (f32[512,768]{1,0:T(8,128)S(1)}, f32[512,768]{1,0:T(8,128)}, u32[]{:S(2)}) copy-start(f32[512,768]{1,0:T(8,128)} %get-tuple-element.48) | copy-start | bytes 4718596
  230.8 1.5 copy-start.2

commit v3 on v2

--- a/solution.py
+++ b/solution.py
@@ -275,7 +275,7 @@
         for dz in self.far_first:
             self._arrive(number, self.line + dz)
             total = total + self.box(number, self.line + dz)[...].astype(jnp.float32)
-        self.chunks[number][1][...] = total
+        self.chunks[number][1](total)
 
     def drain(self):
         for args in self.sent:
@@ -287,7 +287,7 @@
     return 4 * grid.nz - 1
 bf16, f32 = jnp.bfloat16, jnp.float32
 NORM_EPSILON = 1e-06
-EARLY = 4
+EARLY = 12
 AFTER_PROJECTION = 4
 GATHER_STEPS = 4
 AFTER_OUT = 4
@@ -359,9 +359,9 @@
 
 def layer_body(
     grid, rows,
-    tokens, cotangent, length, slopes, qv_part, ko_part, in_part, low_part, high_part, small,
-    output, grad_tokens, to_qv, to_ko, to_in, to_low, to_high, small_grads, probs_far,
-    w_qv, w_ko, w_gate, w_up, w_low, w_high, small_pair, small_tiles, every_small, small_box,
+    tokens, cotangent, length, qv_part, ko_part, in_part, low_part, high_part, gains_part, offsets_part, qv_bias, in_bias,
+    output, grad_tokens, to_qkv, to_out, to_in, to_down, to_gains, to_offsets, to_qv_bias, to_in_bias, probs_far,
+    w_qv, w_ko, w_gate, w_up, w_low, w_high, small_mine, small_pair, small_tiles, every_small, small_box, small_grads,
     x, qkv, inverse, mixed, work, key_aug, value_aug, query_aug,
     rows_f32, attended_low, branch_rows, outgoing, incoming, cot, turned,
     grad_t, pair_b, grad_value_t, grad_key_t,
@@ -395,13 +395,32 @@
         (high_part, w_high, "zxy"),
         (small_pair, small_tiles, "zyx"),
     ], gather_send, gather_recv)
+    def sink_qv(total):
+        to_qkv[0], to_qkv[2] = total[:, :heads_wide], total[:, heads_wide:]
+
+    def sink_ko(total):
+        to_qkv[1] = total[:, :heads_wide]
+        to_out[...] = total[:, heads_wide:].T
+
+    def sink_gate(total):
+        to_in[0] = total
+
+    def sink_up(total):
+        to_in[1] = total
+
+    def sink_low(total):
+        to_down[: units // 2, :] = total.T
+
+    def sink_high(total):
+        to_down[units // 2 :, :] = total.T
+
     scatter = Scatter(grid, rows, [
-        (g_qv, to_qv, "x", box_qv),
-        (g_ko, to_ko, "y", box_ko),
-        (g_gate, to_in.at[0], "x", box_gate),
-        (g_up, to_in.at[1], "y", box_up),
-        (g_low, to_low, "x", box_low),
-        (g_high, to_high, "y", box_high),
+        (g_qv, sink_qv, "x", box_qv),
+        (g_ko, sink_ko, "y", box_ko),
+        (g_gate, sink_gate, "x", box_gate),
+        (g_up, sink_up, "y", box_up),
+        (g_low, sink_low, "x", box_low),
+        (g_high, sink_high, "y", box_high),
     ], scatter_send, scatter_recv)
     QV, KO, GATE, UP, LOW, HIGH, SMALL = range(7)
 
@@ -415,10 +434,14 @@
     token_copy.start()
     cot_copy = pltpu.make_async_copy(cotangent, cot, local_sem.at[1])
     cot_copy.start()
-    my_small = small_pair.at[:, pl.ds(pl.multiple_of(side * 128, 128), 128)]
-    small_copy = pltpu.make_async_copy(small, my_small, local_sem.at[4])
-    small_copy.start()
-    small_swap = swap(small, my_small, 8)
+    my_lanes = pl.ds(pl.multiple_of(side * 128, 128), 128)
+    small_mine[...] = jnp.zeros_like(small_mine)
+    small_mine[0:2, 0 : gains_part.shape[1]] = gains_part[...]
+    small_mine[2:6, 0 : offsets_part.shape[1]] = offsets_part[...]
+    small_mine[8:10, 0 : in_bias.shape[1]] = in_bias[...].astype(f32)
+    small_mine[10:12, 0 : qv_bias.shape[1]] = qv_bias[...].astype(f32)
+    small_pair[:, my_lanes] = small_mine[...]
+    small_swap = swap(small_mine, small_pair.at[:, my_lanes], 8)
     own_copies = []
     for n, (source, target, _) in enumerate(gather.chunks[:SMALL]):
         copy = pltpu.make_async_copy(source, target.at[aligned(grid.at(0, 0, 0) * rows, rows)], own_sem.at[n])
@@ -427,7 +450,6 @@
         for axis in gather.chunks[n][2]:
             gather.send(n, (0, 0, 0), axis)
         if n == KO:
-            small_copy.wait()
             small_swap.wait()
             for axis in gather.chunks[SMALL][2]:
                 gather.send(SMALL, (0, 0, 0), axis)
@@ -491,6 +513,7 @@
     zero, one = jnp.zeros((), bf16), jnp.ones((), bf16)
     block_lane = lax.broadcasted_iota(jnp.int32, (block, 128), 1)
     pairs = heads_wide // 128
+    slopes = [2.0 ** (-8.0 * (h + 1) / (4 * pairs)) for h in range(4 * pairs)]
 
     def prob_slot(upper):
         return work.at[:, pl.ds(upper * slots, slots)]
@@ -513,7 +536,11 @@
                 lax.broadcasted_iota(jnp.int32, (block, span), 0)
                 - (lax.broadcasted_iota(jnp.int32, (block, span), 1) - (span - slots))
             )
-            bias[...] = gap.astype(f32) * slopes[2 * pair + upper]
+            slope = sum(
+                jnp.where(pair == p, jnp.where(side == 0, slopes[2 * p + upper], slopes[2 * (pairs + p) + upper]), 0.0)
+                for p in range(pairs)
+            )
+            bias[...] = gap.astype(f32) * slope
             key_aug[...] = jnp.where(own, qkv[:, pair_cols(pair, 2 * heads_wide)], jnp.where(lane == spare, key_mask, zero))
             value_aug[...] = jnp.where(own, qkv[:, pair_cols(pair, heads_wide)], one)
             query_aug[...] = jnp.where(own, qkv[:, cols], jnp.where(lane == spare, one, zero))
@@ -849,13 +876,34 @@
     sums.stage(3)
     Pump(scatter.lasts(GATE, UP) + scatter.lines(QV, KO) + scatter.lasts(QV, KO)).run()
     sums.stage(4)
+    def turn_to(rows_block, start):
+        return pltpu.roll(rows_block, (width - start) % width, 1)
+
+    dp = lax.axis_index("dp")
+    piece = to_gains.shape[1]
+    low_rows, high_rows = small_grads[0:8, :], small_grads[8:16, :]
+    norm_part = turn_to(low_rows, (2 * dp + side) * piece)
+    to_gains[...] = norm_part[0:2, :piece]
+    to_offsets[...] = norm_part[2:6, :piece]
+    to_qv_bias[...] = turn_to(low_rows, side * heads_wide + dp * to_qv_bias.shape[1])[6:8, : to_qv_bias.shape[1]]
+    unit_piece = to_in_bias.shape[1]
+    first_lane = dp * unit_piece
+    unit_part = turn_to(high_rows, first_lane % width)
+    per_half = units // width
+    row = side * per_half + first_lane // width
+    for index in range(2):
+        chosen = sum(
+            jnp.where(row == r, unit_part[2 * per_half * index + r : 2 * per_half * index + r + 1, :], 0.0)
+            for r in range(2 * per_half)
+        )
+        to_in_bias[index : index + 1, :] = chosen[:, :unit_piece]
     output_copy.wait()
     tokens_copy.wait()
     gather.drain()
     scatter.drain()
 
 
-def layer_call(grid, tokens, cotangent, lengths, slopes, qv_part, ko_part, in_part, low_part, high_part, small):
+def layer_call(grid, tokens, cotangent, lengths, qv_part, ko_part, in_part, low_part, high_part, smalls_in):
     rows, wide = qv_part.shape
     width = rows * grid.nz * 4
     half = tokens.shape[0]
@@ -866,12 +914,11 @@
     shapes = [
         jax.ShapeDtypeStruct((half, width), bf16),
         jax.ShapeDtypeStruct((half, width), f32),
-        jax.ShapeDtypeStruct(qv_part.shape, f32),
-        jax.ShapeDtypeStruct(ko_part.shape, f32),
+        jax.ShapeDtypeStruct((3, rows, heads_wide), f32),
+        jax.ShapeDtypeStruct((heads_wide, rows), f32),
         jax.ShapeDtypeStruct(in_part.shape, f32),
-        jax.ShapeDtypeStruct(low_part.shape, f32),
-        jax.ShapeDtypeStruct(high_part.shape, f32),
-        jax.ShapeDtypeStruct((16, width), f32),
+        jax.ShapeDtypeStruct((units, rows), f32),
+        *(jax.ShapeDtypeStruct(part.shape, f32) for part in smalls_in),
         jax.ShapeDtypeStruct((heads, slots, slots), bf16),
     ]
     vmem = pl.BlockSpec(memory_space=pltpu.VMEM)
@@ -883,10 +930,12 @@
     scratch = (
         [pltpu.VMEM((width, w), bf16) for w in wides]
         + [
+            pltpu.VMEM((16, 128), f32),
             pltpu.VMEM((16, 256), f32),
             pltpu.VMEM((16 * grid.slots, 256), f32),
             pltpu.VMEM((16, width), f32),
             pltpu.VMEM((smalls, 16, width), f32),
+            pltpu.VMEM((16, width), f32),
             pltpu.VMEM((slots, width), bf16),
             pltpu.VMEM((slots, 3 * heads_wide), bf16),
             pltpu.VMEM((slots, 128), f32),
@@ -926,13 +975,13 @@
     results = pl.pallas_call(
         functools.partial(layer_body, grid, rows),
         out_shape=shapes,
-        in_specs=[anywhere, anywhere, smem, smem] + [anywhere] * 6,
-        out_specs=[anywhere] * 2 + [vmem] * 6 + [anywhere],
+        in_specs=[anywhere, anywhere, smem] + [anywhere] * 5 + [vmem] * 4,
+        out_specs=[anywhere] * 2 + [vmem] * 8 + [anywhere],
         scratch_shapes=scratch,
         compiler_params=pltpu.CompilerParams(collective_id=0, has_side_effects=True, vmem_limit_bytes=VMEM_LIMIT),
         name="layer",
-    )(tokens, cotangent, lengths, slopes, qv_part, ko_part, in_part, low_part, high_part, small)
-    return results[:8]
+    )(tokens, cotangent, lengths, qv_part, ko_part, in_part, low_part, high_part, *smalls_in)
+    return results[:10]
 
 
 norm_epsilon = 1e-06
@@ -1066,15 +1115,6 @@
     return jnp.pad(packed, ((0, -packed.shape[0] % 8), (0, 0)))
 
 
-def small_tile(norm_gains, offsets, qv_bias, in_bias):
-    def rows(part, count):
-        return jnp.pad(part.astype(f32), ((0, count - part.shape[0]), (0, 128 - part.shape[1])))
-
-    return jnp.concatenate(
-        [rows(norm_gains, 2), rows(offsets, 6), rows(in_bias, 2), rows(qv_bias, 6)], axis=0
-    )
-
-
 def unpack_small(packed, width_qv, width_in, piece, pieces):
     width = packed.shape[1]
     count_qv = 2 * width_qv * pieces // width
@@ -1105,6 +1145,21 @@
     dp_index = lax.axis_index("dp")
     flat_index = dp_index * pieces + piece_index
     grid = Grid3(dp)
+    if direct:
+        middle = down_weight.shape[0] // 2
+        output, grad_tokens, to_qkv, to_out, to_in, to_down, to_gains, to_offsets, to_qv_bias, to_in_bias = layer_call(
+            grid,
+            tokens,
+            cotangent,
+            lengths,
+            jnp.concatenate([qkv_weight[0], qkv_weight[2]], axis=1),
+            jnp.concatenate([qkv_weight[1], out_weight.T], axis=1),
+            in_weight,
+            down_weight[:middle].T,
+            down_weight[middle:].T,
+            (norm_gains, offsets, qv_bias, in_bias),
+        )
+        return output, grad_tokens, to_qkv, to_qv_bias, to_out, to_in, to_in_bias, to_down, to_gains, to_offsets
     slot_count = row_count * pieces
     length = lengths[0]
     heads_here = qkv_weight.shape[2] // HEAD
@@ -1116,38 +1171,6 @@
     )[:, None]
 
     width_qv, width_in = qkv_weight.shape[2], in_weight.shape[2]
-    if direct:
-        middle = down_weight.shape[0] // 2
-        output, grad_tokens, shard_qv, shard_ko, shard_in, shard_low, shard_high, small_grads = layer_call(
-            grid,
-            tokens,
-            cotangent,
-            lengths,
-            slopes,
-            jnp.concatenate([qkv_weight[0], qkv_weight[2]], axis=1),
-            jnp.concatenate([qkv_weight[1], out_weight.T], axis=1),
-            in_weight,
-            down_weight[:middle].T,
-            down_weight[middle:].T,
-            small_tile(norm_gains, offsets, qv_bias, in_bias),
-        )
-        shard_wqkv = jnp.stack([shard_qv[:, :width_qv], shard_ko[:, :width_qv], shard_qv[:, width_qv:]])
-        shard_out_t = shard_ko[:, width_qv:]
-        shard_down_t = jnp.concatenate([shard_low, shard_high], axis=1)
-        row_grads, bqv_grads, bin_grads = unpack_small(small_grads, width_qv, width_in, piece_index, pieces)
-        own_rows = pick(row_grads, flat_index, dp * pieces)
-        return (
-            output,
-            grad_tokens,
-            shard_wqkv,
-            pick(bqv_grads, dp_index, dp),
-            shard_out_t.T,
-            shard_in,
-            pick(bin_grads, dp_index, dp),
-            shard_down_t.T,
-            own_rows[:2],
-            own_rows[2:],
-        )
     parts = (qkv_weight, out_weight.T, in_weight, down_weight.T)
     small = pack_small(
         spread(qv_bias, dp_index, dp),

time: 234 us -> 228 us (0.974)
  other arithmetic: 6.99 us -> 1.44 us
    unnamed x9 -> x24, local copies, waits for them, and re-layouts: 3.17 us -> 10.9 us
    slice x5 -> x0, local copies, waits for them, and re-layouts: 3.36 us -> none  [the longest x1 0.74 us: unpack_small(): whole_qv = packed[6:6 + count_qv].reshape(2, -1)]
where the time goes in v3:
time: 228 us
  Pallas kernels  212 us (93%)
  local copies, waits for them, and re-layouts  13.3 us (6%)
    pallas_call x1, Pallas kernels, layer_call(): pl.pallas_call(functools.partial(layer_body, grid, rows), out_shape=shape...  212 us
    unnamed x24, local copies, waits for them, and re-layouts  10.9 us

profile of v3, /device:TPU:0, one launch (start us, length us, event | category | flops | bytes accessed | tf_op | source)
XLA Modules:
  0.0 227.6 jit_solution(14587627910550080628)
XLA Ops:
  1.3 0.8 slice_bitcast_fusion.2
  2.1 1.4 pad_maximum_fusion
  3.5 1.6 slice_bitcast_fusion
  5.1 211.5 %layer.1 = (bf16[512,768]{1,0:T(8,128)(2,1)}, f32[512,768]{1,0:T(8,128)}, f32[3,48,384]{2,1,0:T(8,128)}, f32[384,48]{1,0:T(8,128)}, f32[2,48,1536]{2,1,0:T(8,128...) custom-call(bf16[512,768]{1,0:T(8,128)(2,1)} %tokens.1, ...), custom_call_target="tpu_custom_call" | custom-call | tf_op jit(solution)/shard_map/layer/pallas_call | solution.py:975
  216.7 0.0 copy-start
  216.7 1.8 copy.21
  218.5 2.1 copy.22
  220.6 2.1 copy.32
  222.6 0.0 copy-done
  222.6 0.0 copy-start.2
  222.6 0.0 copy-start.6
  222.6 0.0 copy-start.1
  222.6 1.1 copy.33
  223.8 0.0 copy-done.2
  223.8 0.0 copy-start.5
  223.8 0.0 copy-start.4
  223.8 0.0 copy-start.3
  223.8 0.7 copy.34
  224.5 0.0 copy-done.6
  224.5 0.6 copy.35
  225.0 0.0 copy-done.1
  225.0 0.8 copy.36
  225.9 0.0 copy-done.5
  225.9 0.6 copy.37
  226.4 0.0 copy-done.4
  226.4 0.6 copy.38
  227.0 0.0 copy-done.3
  227.0 0.6 copy.39
Async XLA Ops:
  216.7 6.0 %copy-start = (f32[512,768]{1,0:T(8,128)S(1)}, f32[512,768]{1,0:T(8,128)}, u32[]{:S(2)}) copy-start(f32[512,768]{1,0:T(8,128)} %get-tuple-element.58) | copy-start | bytes 4718596
  222.6 1.2 copy-start.2
  222.6 1.9 copy-start.6
  222.6 2.4 %copy-start.1 = (f32[2,48,1536]{2,1,0:T(8,128)S(1)}, f32[2,48,1536]{2,1,0:T(8,128)}, u32[]{:S(2)}) copy-start(f32[2,48,1536]{2,1,0:T(8,128)} %get-tuple-element.62) | copy-start | bytes 1769476
  223.8 2.1 copy-start.5
  223.8 2.6 %copy-start.4 = (f32[2,24]{1,0:T(2,128)S(1)}, f32[2,24]{1,0:T(2,128)}, u32[]{:S(2)}) copy-start(f32[2,24]{1,0:T(2,128)} %get-tuple-element.65) | copy-start | bytes 580
  223.8 3.2 %copy-start.3 = (f32[4,24]{1,0:T(4,128)S(1)}, f32[4,24]{1,0:T(4,128)}, u32[]{:S(2)}) copy-start(f32[4,24]{1,0:T(4,128)} %get-tuple-element.66) | copy-start | bytes 1156

commit v4 on v3

--- a/solution.py
+++ b/solution.py
@@ -201,7 +201,7 @@
         self.send_sem, self.recv_sem = send, recv
         self.sent = []
         self.far_first = [2, 1, 3] if grid.nz == 4 else list(range(1, grid.nz))
-        self.second, self.line = 2 * grid.nz, 3 * grid.nz - 1
+        self.second, self.line, self.crossing = 2 * grid.nz, 3 * grid.nz - 1, 4 * grid.nz - 2
 
     def part(self, number, d):
         return self.chunks[number][0].at[pl.ds(pl.multiple_of(self.grid.at(*d) * self.rows, self.rows), self.rows)]
@@ -210,7 +210,7 @@
         return self.chunks[number][3].at[slot]
 
     def other(self, number):
-        return "y" if self.chunks[number][2] == "x" else "x"
+        return "y" if self.chunks[number][2][0] == "x" else "x"
 
     def place(self, number, dz, e):
         return (dz, e, 0) if self.other(number) == "y" else (dz, 0, e)
@@ -218,11 +218,17 @@
     def _copy(self, number, kind, dz, e=0):
         grid = self.grid
         if kind == "own":
-            move = grid.steps(self.chunks[number][2])[0]
+            move = grid.steps(self.chunks[number][2][0])[0]
             source, slot = self.part(number, joined(self.place(number, dz, e), move)), dz * 2 + e
         elif kind == "side":
             move = grid.steps(self.other(number))[0]
             source, slot = self.box(number, dz * 2 + 1), self.second + dz
+        elif kind == "cross":
+            move = grid.steps(self.other(number))[0]
+            source, slot = self.box(number, 1), self.crossing
+        elif kind == "middle":
+            move = (dz, 0, 0)
+            source, slot = self.box(number, dz * 2 + e), self.middle_slot(dz, e)
         else:
             move = (dz, 0, 0)
             source, slot = self.box(number, dz * 2), self.line + dz
@@ -261,20 +267,51 @@
         self.box(number, dz * 2)[...] = self.both(number, dz).astype(jnp.bfloat16)
         self._send(number, "line", dz)
 
+    def middle_slot(self, dz, e):
+        return self.second + e * (self.grid.nz - 1) + dz - 1
+
+    def middle(self, number, dz, e):
+        self.box(number, dz * 2 + e)[...] = self.held(number, dz, e).astype(jnp.bfloat16)
+        self._send(number, "middle", dz, e)
+
+    def line_total(self, number, e):
+        total = self.held(number, 0, e)
+        for dz in self.far_first:
+            slot = self.middle_slot(dz, e)
+            self._arrive(number, slot)
+            total = total + self.box(number, slot)[...].astype(jnp.float32)
+        return total
+
+    def cross(self, number):
+        self.box(number, 1)[...] = self.line_total(number, 1).astype(jnp.bfloat16)
+        self._send(number, "cross", 0)
+
+    def z_second(self, number):
+        return self.chunks[number][2][1] == "z"
+
     def sides(self, *numbers):
+        if self.z_second(numbers[0]):
+            return [(self.middle, n, dz, e) for e in (1, 0) for dz in self.far_first for n in numbers]
         return [(self.side, n, dz) for dz in self.far_first + [0] for n in numbers]
 
     def lines(self, *numbers):
+        if self.z_second(numbers[0]):
+            return [(self.cross, n) for n in numbers]
         return [(self.along, n, dz) for dz in self.far_first for n in numbers]
 
     def lasts(self, *numbers):
         return [(self.last, n) for n in numbers]
 
     def last(self, number):
-        total = self.both(number, 0)
-        for dz in self.far_first:
-            self._arrive(number, self.line + dz)
-            total = total + self.box(number, self.line + dz)[...].astype(jnp.float32)
+        if self.z_second(number):
+            total = self.line_total(number, 0)
+            self._arrive(number, self.crossing)
+            total = total + self.box(number, self.crossing)[...].astype(jnp.float32)
+        else:
+            total = self.both(number, 0)
+            for dz in self.far_first:
+                self._arrive(number, self.line + dz)
+                total = total + self.box(number, self.line + dz)[...].astype(jnp.float32)
         self.chunks[number][1](total)
 
     def drain(self):
@@ -359,7 +396,7 @@
 
 def layer_body(
     grid, rows,
-    tokens, cotangent, length, qv_part, ko_part, in_part, low_part, high_part, gains_part, offsets_part, qv_bias, in_bias,
+    tokens, cotangent, length, qkv_part, out_part, in_part, down_part, gains_part, offsets_part, qv_bias, in_bias,
     output, grad_tokens, to_qkv, to_out, to_in, to_down, to_gains, to_offsets, to_qv_bias, to_in_bias, probs_far,
     w_qv, w_ko, w_gate, w_up, w_low, w_high, small_mine, small_pair, small_tiles, every_small, small_box, small_grads,
     x, qkv, inverse, mixed, work, key_aug, value_aug, query_aug,
@@ -384,15 +421,35 @@
     span = 2 * slots - block
     bias = rows_f32.at[pl.ds(0, block), pl.ds(0, span)]
 
+    own_rows = aligned(grid.at(0, 0, 0) * rows, rows)
+    low, high = pl.ds(0, units // 2), pl.ds(units // 2, units // 2)
+    one_head, two_head = pl.ds(0, heads_wide), pl.ds(heads_wide, heads_wide)
+    own_copies = [
+        pltpu.make_async_copy(source, target, own_sem.at[n])
+        for n, (source, target) in enumerate(
+            [
+                (qkv_part.at[0], w_qv.at[own_rows, one_head]),
+                (qkv_part.at[2], w_qv.at[own_rows, two_head]),
+                (qkv_part.at[1], w_ko.at[own_rows, one_head]),
+                (out_part, w_ko.at[own_rows, two_head]),
+                (in_part.at[0], w_gate.at[own_rows]),
+                (in_part.at[1], w_up.at[own_rows]),
+                (down_part.at[:, low], w_low.at[own_rows]),
+                (down_part.at[:, high], w_high.at[own_rows]),
+            ]
+        )
+    ]
+    for copy in own_copies:
+        copy.start()
     greet(grid, other)
 
     gather = Gather(grid, [
-        (qv_part, w_qv, "zyx"),
-        (ko_part, w_ko, "zxy"),
-        (in_part.at[0], w_gate, "yzx"),
-        (in_part.at[1], w_up, "xzy"),
-        (low_part, w_low, "zyx"),
-        (high_part, w_high, "zxy"),
+        (w_qv.at[own_rows], w_qv, "zyx"),
+        (w_ko.at[own_rows], w_ko, "zxy"),
+        (w_gate.at[own_rows], w_gate, "yzx"),
+        (w_up.at[own_rows], w_up, "xzy"),
+        (w_low.at[own_rows], w_low, "zyx"),
+        (w_high.at[own_rows], w_high, "zxy"),
         (small_pair, small_tiles, "zyx"),
     ], gather_send, gather_recv)
     def sink_qv(total):
@@ -400,7 +457,7 @@
 
     def sink_ko(total):
         to_qkv[1] = total[:, :heads_wide]
-        to_out[...] = total[:, heads_wide:].T
+        to_out[...] = total[:, heads_wide:]
 
     def sink_gate(total):
         to_in[0] = total
@@ -409,18 +466,18 @@
         to_in[1] = total
 
     def sink_low(total):
-        to_down[: units // 2, :] = total.T
+        to_down[:, : units // 2] = total
 
     def sink_high(total):
-        to_down[units // 2 :, :] = total.T
+        to_down[:, units // 2 :] = total
 
     scatter = Scatter(grid, rows, [
-        (g_qv, sink_qv, "x", box_qv),
-        (g_ko, sink_ko, "y", box_ko),
-        (g_gate, sink_gate, "x", box_gate),
-        (g_up, sink_up, "y", box_up),
-        (g_low, sink_low, "x", box_low),
-        (g_high, sink_high, "y", box_high),
+        (g_qv, sink_qv, "xyz", box_qv),
+        (g_ko, sink_ko, "yxz", box_ko),
+        (g_gate, sink_gate, "xyz", box_gate),
+        (g_up, sink_up, "yxz", box_up),
+        (g_low, sink_low, "xzy", box_low),
+        (g_high, sink_high, "yzx", box_high),
     ], scatter_send, scatter_recv)
     QV, KO, GATE, UP, LOW, HIGH, SMALL = range(7)
 
@@ -442,11 +499,10 @@
     small_mine[10:12, 0 : qv_bias.shape[1]] = qv_bias[...].astype(f32)
     small_pair[:, my_lanes] = small_mine[...]
     small_swap = swap(small_mine, small_pair.at[:, my_lanes], 8)
-    own_copies = []
-    for n, (source, target, _) in enumerate(gather.chunks[:SMALL]):
-        copy = pltpu.make_async_copy(source, target.at[aligned(grid.at(0, 0, 0) * rows, rows)], own_sem.at[n])
-        copy.start()
-        own_copies.append(copy)
+    pieces = {QV: (0, 1), KO: (2, 3), GATE: (4,), UP: (5,), LOW: (6,), HIGH: (7,)}
+    for n in pieces:
+        for piece in pieces[n]:
+            own_copies[piece].wait()
         for axis in gather.chunks[n][2]:
             gather.send(n, (0, 0, 0), axis)
         if n == KO:
@@ -465,8 +521,6 @@
     pump = Pump(early)
     pump.run()
     pump = Pump(merged(near_units[EARLY:], ends_first) + ends_second)
-    for copy in own_copies:
-        copy.wait()
     token_copy.wait()
     token_swap.wait()
     for number in (SMALL, QV, KO):
@@ -718,13 +772,15 @@
         for j in range(units // width):
             small_grads[pl.ds(8 + 4 * index + 2 * side + j, 1), :] = total[:, j * width : (j + 1) * width]
 
-    Pump(scatter.sides(LOW, HIGH)).run()
+    sides_ends = Pump(scatter.sides(LOW, HIGH))
+    sides_ends.run(6)
     turn(attended_low)
     weight_grad(g_gate, work, 0, 512)
     scatter.begin(GATE, 1)
     weight_grad(g_up, work, units, 512)
     scatter.begin(UP, 1)
     scatter.begin(GATE, 0)
+    sides_ends.run()
 
     gate_cols, up_cols = pl.ds(0, units), pl.ds(units, units)
 
@@ -903,21 +959,21 @@
     scatter.drain()
 
 
-def layer_call(grid, tokens, cotangent, lengths, qv_part, ko_part, in_part, low_part, high_part, smalls_in):
-    rows, wide = qv_part.shape
+def layer_call(grid, tokens, cotangent, lengths, qkv_part, out_part, in_part, down_part, smalls_in):
+    rows, heads_wide = out_part.shape
+    wide = 2 * heads_wide
     width = rows * grid.nz * 4
     half = tokens.shape[0]
     slots = 2 * half
-    heads_wide = wide // 2
     units = in_part.shape[2]
     heads = heads_wide // HEAD
     shapes = [
         jax.ShapeDtypeStruct((half, width), bf16),
         jax.ShapeDtypeStruct((half, width), f32),
         jax.ShapeDtypeStruct((3, rows, heads_wide), f32),
-        jax.ShapeDtypeStruct((heads_wide, rows), f32),
+        jax.ShapeDtypeStruct((rows, heads_wide), f32),
         jax.ShapeDtypeStruct(in_part.shape, f32),
-        jax.ShapeDtypeStruct((units, rows), f32),
+        jax.ShapeDtypeStruct((rows, units), f32),
         *(jax.ShapeDtypeStruct(part.shape, f32) for part in smalls_in),
         jax.ShapeDtypeStruct((heads, slots, slots), bf16),
     ]
@@ -965,7 +1021,7 @@
             dma((6, scatter_slots(grid))),
             dma((smalls,)),
             dma((smalls,)),
-            dma((6,)),
+            dma((8,)),
             dma((9,)),
             dma((9,)),
             dma((5,)),
@@ -975,12 +1031,12 @@
     results = pl.pallas_call(
         functools.partial(layer_body, grid, rows),
         out_shape=shapes,
-        in_specs=[anywhere, anywhere, smem] + [anywhere] * 5 + [vmem] * 4,
+        in_specs=[anywhere, anywhere, smem] + [anywhere] * 4 + [vmem] * 4,
         out_specs=[anywhere] * 2 + [vmem] * 8 + [anywhere],
         scratch_shapes=scratch,
         compiler_params=pltpu.CompilerParams(collective_id=0, has_side_effects=True, vmem_limit_bytes=VMEM_LIMIT),
         name="layer",
-    )(tokens, cotangent, lengths, qv_part, ko_part, in_part, low_part, high_part, *smalls_in)
+    )(tokens, cotangent, lengths, qkv_part, out_part, in_part, down_part, *smalls_in)
     return results[:10]
 
 
@@ -1146,20 +1202,18 @@
     flat_index = dp_index * pieces + piece_index
     grid = Grid3(dp)
     if direct:
-        middle = down_weight.shape[0] // 2
         output, grad_tokens, to_qkv, to_out, to_in, to_down, to_gains, to_offsets, to_qv_bias, to_in_bias = layer_call(
             grid,
             tokens,
             cotangent,
             lengths,
-            jnp.concatenate([qkv_weight[0], qkv_weight[2]], axis=1),
-            jnp.concatenate([qkv_weight[1], out_weight.T], axis=1),
+            qkv_weight,
+            out_weight.T,
             in_weight,
-            down_weight[:middle].T,
-            down_weight[middle:].T,
+            down_weight.T,
             (norm_gains, offsets, qv_bias, in_bias),
         )
-        return output, grad_tokens, to_qkv, to_qv_bias, to_out, to_in, to_in_bias, to_down, to_gains, to_offsets
+        return output, grad_tokens, to_qkv, to_qv_bias, to_out.T, to_in, to_in_bias, to_down.T, to_gains, to_offsets
     slot_count = row_count * pieces
     length = lengths[0]
     heads_here = qkv_weight.shape[2] // HEAD

time: 228 us -> 216 us (0.947)
  Pallas kernels: 212 us -> 206 us
  local copies, waits for them, and re-layouts: 13.3 us -> 8.47 us
    pallas_call x1, Pallas kernels: 212 us -> 206 us  [layer_call(): pl.pallas_call(functools.partial(layer_body, grid, rows), out_shape=shape...]
    unnamed x24 -> x28, local copies, waits for them, and re-layouts: 10.9 us -> 8.47 us
where the time goes in v4:
time: 216 us
  Pallas kernels  206 us (95%)
  local copies, waits for them, and re-layouts  8.47 us (4%)
    pallas_call x1, Pallas kernels, layer_call(): pl.pallas_call(functools.partial(layer_body, grid, rows), out_shape=shape...  206 us
    unnamed x28, local copies, waits for them, and re-layouts  8.47 us

profile of v4, /device:TPU:0, one launch (start us, length us, event | category | flops | bytes accessed | tf_op | source)
XLA Modules:
  0.0 215.9 jit_solution(7018521080846555076)
XLA Ops:
  1.3 206.1 %layer.1 = (bf16[512,768]{1,0:T(8,128)(2,1)}, f32[512,768]{1,0:T(8,128)}, f32[3,48,384]{2,1,0:T(8,128)}, f32[48,384]{1,0:T(8,128)}, f32[2,48,1536]{2,1,0:T(8,128...) custom-call(bf16[512,768]{1,0:T(8,128)(2,1)} %tokens.1, ...), custom_call_target="tpu_custom_call" | custom-call | tf_op jit(solution)/shard_map/layer/pallas_call | solution.py:1031
  207.4 0.0 copy-start
  207.4 2.2 %copy.32 = bf16[512,768]{1,0:T(8,128)(2,1)} copy(bf16[512,768]{1,0:T(8,128)(2,1)} %get-tuple-element.40) | data formatting | bytes 1572864
  209.6 0.0 copy-done
  209.6 0.0 copy-start.3
  209.6 0.0 copy-start.8
  209.6 0.0 copy-start.4
  209.6 0.0 copy-start.1
  209.6 1.1 copy.33
  210.8 0.0 copy-done.3
  210.8 0.0 copy-start.7
  210.8 0.0 copy-start.2
  210.8 0.0 copy-start.6
  210.8 0.0 copy-start.5
  210.8 0.7 copy.34
  211.5 0.0 copy-done.8
  211.5 0.6 copy.35
  212.0 0.0 copy-done.4
  212.0 0.6 copy.36
  212.7 0.0 copy-done.1
  212.7 0.8 copy.37
  213.5 0.0 copy-done.7
  213.5 0.6 copy.38
  214.1 0.0 copy-done.2
  214.1 0.7 copy.39
  214.8 0.0 copy-done.6
  214.8 0.6 copy.40
  215.3 0.0 copy-done.5
  215.3 0.6 copy.41
Async XLA Ops:
  207.4 2.2 %copy-start = (f32[512,768]{1,0:T(8,128)S(1)}, f32[512,768]{1,0:T(8,128)}, u32[]{:S(2)}) copy-start(f32[512,768]{1,0:T(8,128)} %get-tuple-element.41) | copy-start | bytes 4718596
  209.6 1.2 copy-start.3
  209.6 1.9 copy-start.8
  209.6 2.4 %copy-start.4 = (f32[48,384]{1,0:T(8,128)S(1)}, f32[48,384]{1,0:T(8,128)}, u32[]{:S(2)}) copy-start(f32[48,384]{1,0:T(8,128)} %get-tuple-element.24) | copy-start | bytes 221188
  209.6 3.1 %copy-start.1 = (f32[2,48,1536]{2,1,0:T(8,128)S(1)}, f32[2,48,1536]{2,1,0:T(8,128)}, u32[]{:S(2)}) copy-start(f32[2,48,1536]{2,1,0:T(8,128)} %get-tuple-element.45) | copy-start | bytes 1769476
  210.8 2.7 %copy-start.7 = (f32[2,96]{1,0:T(2,128)S(1)}, f32[2,96]{1,0:T(2,128)}, u32[]{:S(2)}) copy-start(f32[2,96]{1,0:T(2,128)} %get-tuple-element.46) | copy-start | bytes 2308
  210.8 3.3 %copy-start.2 = (f32[48,1536]{1,0:T(8,128)S(1)}, f32[48,1536]{1,0:T(8,128)}, u32[]{:S(2)}) copy-start(f32[48,1536]{1,0:T(8,128)} %get-tuple-element.27) | copy-start | bytes 884740
  210.8 4.0 %copy-start.6 = (f32[2,24]{1,0:T(2,128)S(1)}, f32[2,24]{1,0:T(2,128)}, u32[]{:S(2)}) copy-start(f32[2,24]{1,0:T(2,128)} %get-tuple-element.48) | copy-start | bytes 580
  210.8 4.6 %copy-start.5 = (f32[4,24]{1,0:T(4,128)S(1)}, f32[4,24]{1,0:T(4,128)}, u32[]{:S(2)}) copy-start(f32[4,24]{1,0:T(4,128)} %get-tuple-element.49) | copy-start | bytes 1156

commit v5 on v4

--- a/solution.py
+++ b/solution.py
@@ -93,19 +93,19 @@
         self.copies = []
         if number == 1:
             self.out[...] = self.out[...] + self.box[0]
-            self._post(1, dp=grid.at(0, 0, 1))
-        elif number == 2:
-            self.out[...] = self.out[...] + self.box[1]
-            self._post(2, dp=grid.at(0, 1, 0))
-        elif number == 3:
-            self.out[...] = self.out[...] + self.box[2]
             for k in range(1, grid.nz):
                 self._post(2 + k, dp=grid.at(k, 0, 0))
-        else:
+        elif number == 2:
             total = self.out[...]
             for k in range(1, grid.nz):
                 total = total + self.box[2 + k]
             self.out[...] = total
+            self._post(1, dp=grid.at(0, 0, 1))
+        elif number == 3:
+            self.out[...] = self.out[...] + self.box[1]
+            self._post(2, dp=grid.at(0, 1, 0))
+        else:
+            self.out[...] = self.out[...] + self.box[2]
 
 
 def small_slots(grid):
@@ -400,7 +400,7 @@
     output, grad_tokens, to_qkv, to_out, to_in, to_down, to_gains, to_offsets, to_qv_bias, to_in_bias, probs_far,
     w_qv, w_ko, w_gate, w_up, w_low, w_high, small_mine, small_pair, small_tiles, every_small, small_box, small_grads,
     x, qkv, inverse, mixed, work, key_aug, value_aug, query_aug,
-    rows_f32, attended_low, branch_rows, outgoing, incoming, cot, turned,
+    rows_f32, attended_low, branch_rows, outgoing, incoming, turned,
     grad_t, pair_b, grad_value_t, grad_key_t,
     g_qv, g_ko, g_gate, g_up, g_low, g_high, box_qv, box_ko, box_gate, box_up, box_low, box_high,
     gather_send, gather_recv, scatter_send, scatter_recv, small_send, small_recv, own_sem, swap_send, swap_recv, local_sem, prob_sem,
@@ -489,7 +489,7 @@
     token_swap = swap(tokens, x.at[mine], 0)
     token_copy = pltpu.make_async_copy(tokens, x.at[mine], local_sem.at[0])
     token_copy.start()
-    cot_copy = pltpu.make_async_copy(cotangent, cot, local_sem.at[1])
+    cot_copy = pltpu.make_async_copy(cotangent, output, local_sem.at[1])
     cot_copy.start()
     my_lanes = pl.ds(pl.multiple_of(side * 128, 128), 128)
     small_mine[...] = jnp.zeros_like(small_mine)
@@ -715,8 +715,8 @@
         position = side * half + i * step + lax.broadcasted_iota(jnp.int32, (step, 1), 0)
         valid = jnp.where(position < count, 1.0, 0.0)
         unit, scale = unit_rows(attended[r, :] + incoming[1, r, :].astype(f32) + every_small[4:5, :])
-        grad = cot[r, :].astype(f32) * valid
-        cot[r, :] = ((unit * gain_two + every_small[5:6, :]) * valid).astype(bf16)
+        grad = output[r, :].astype(f32) * valid
+        output[r, :] = ((unit * gain_two + every_small[5:6, :]) * valid).astype(bf16)
         back = unit_back(grad * gain_two, unit, scale)
         attended[r, :] = back
         branch_rows[own, :] = back.astype(bf16)
@@ -724,8 +724,6 @@
 
     gain_two_sum, shift_two_sum, down_bias_sum = lax.fori_loop(0, half // step, second_norm, (nothing,) * 3)
     branch_swap = swap(branch_rows.at[mine], branch_rows.at[mine], 4)
-    output_copy = pltpu.make_async_copy(cot, output, local_sem.at[2])
-    output_copy.start()
     small_grads[...] = jnp.zeros_like(small_grads)
     small_grads[1:2, :] = jnp.sum(gain_two_sum, axis=0, keepdims=True)
     small_grads[5:6, :] = jnp.sum(shift_two_sum, axis=0, keepdims=True)
@@ -891,9 +889,11 @@
 
     turn(x)
     g_qv[...] = nn(grad_t[...], qkv[:, pl.ds(0, 2 * heads_wide)]).astype(bf16)
-    scatter.begin(QV)
+    scatter.begin(QV, 1)
     g_ko[:, pl.ds(0, heads_wide)] = nn(grad_t[...], qkv[:, k_cols]).astype(bf16)
-    scatter.begin(KO)
+    scatter.begin(KO, 1)
+    scatter.begin(QV, 0)
+    scatter.begin(KO, 0)
     def column_sum(cols):
         def add(i, carry):
             return carry + fold(qkv[aligned(i * 128, 128), cols].astype(f32))
@@ -918,6 +918,8 @@
     fourth_swap = swap(outgoing, incoming.at[1], 7)
     sums.stage(1)
     inputs_back(side, add_attended)
+    sums.stage(2)
+    Pump(scatter.lines(UP)).run()
     fourth_swap.wait()
 
     @pl.loop(0, half // step)
@@ -927,11 +929,11 @@
 
     tokens_copy = pltpu.make_async_copy(attended, grad_tokens, local_sem.at[3])
     tokens_copy.start()
-    sums.stage(2)
-    Pump(scatter.lines(UP) + scatter.sides(QV, KO)).run()
+    Pump(scatter.sides(QV, KO)).run()
     sums.stage(3)
-    Pump(scatter.lasts(GATE, UP) + scatter.lines(QV, KO) + scatter.lasts(QV, KO)).run()
+    Pump(scatter.lines(QV, KO) + scatter.lasts(GATE, UP) + scatter.lasts(QV, KO)).run()
     sums.stage(4)
+
     def turn_to(rows_block, start):
         return pltpu.roll(rows_block, (width - start) % width, 1)
 
@@ -953,7 +955,6 @@
             for r in range(2 * per_half)
         )
         to_in_bias[index : index + 1, :] = chosen[:, :unit_piece]
-    output_copy.wait()
     tokens_copy.wait()
     gather.drain()
     scatter.drain()
@@ -1005,7 +1006,6 @@
             pltpu.VMEM((slots, width), bf16),
             pltpu.VMEM((half, width), bf16),
             pltpu.VMEM((2, half, width), bf16),
-            pltpu.VMEM((half, width), bf16),
             pltpu.VMEM((24, units), f32),
             pltpu.VMEM((width, slots), bf16),
             pltpu.VMEM((2, 128, slots), bf16),
@@ -1032,7 +1032,7 @@
         functools.partial(layer_body, grid, rows),
         out_shape=shapes,
         in_specs=[anywhere, anywhere, smem] + [anywhere] * 4 + [vmem] * 4,
-        out_specs=[anywhere] * 2 + [vmem] * 8 + [anywhere],
+        out_specs=[vmem, anywhere] + [vmem] * 8 + [anywhere],
         scratch_shapes=scratch,
         compiler_params=pltpu.CompilerParams(collective_id=0, has_side_effects=True, vmem_limit_bytes=VMEM_LIMIT),
         name="layer",

time: 216 us -> 212 us (0.981); the launches traced: 216 us -> 209 us
  Pallas kernels: 206 us -> 199 us
    pallas_call x1, Pallas kernels: 206 us -> 199 us  [layer_call(): pl.pallas_call(functools.partial(layer_body, grid, rows), out_shape=shape...]
where the time goes in v5:
time: 212 us; the launch traced here: 209 us
  Pallas kernels  199 us (94%)
  local copies, waits for them, and re-layouts  8.47 us (4%)
    pallas_call x1, Pallas kernels, layer_call(): pl.pallas_call(functools.partial(layer_body, grid, rows), out_shape=shape...  199 us
    unnamed x28, local copies, waits for them, and re-layouts  8.47 us

profile of v5, /device:TPU:0, one launch (start us, length us, event | category | flops | bytes accessed | tf_op | source)
XLA Modules:
  0.0 208.6 jit_solution(17630410429570090832)
XLA Ops:
  1.3 198.7 %layer.1 = (bf16[512,768]{1,0:T(8,128)(2,1)}, f32[512,768]{1,0:T(8,128)}, f32[3,48,384]{2,1,0:T(8,128)}, f32[48,384]{1,0:T(8,128)}, f32[2,48,1536]{2,1,0:T(8,128...) custom-call(bf16[512,768]{1,0:T(8,128)(2,1)} %tokens.1, ...), custom_call_target="tpu_custom_call" | custom-call | tf_op jit(solution)/shard_map/layer/pallas_call | solution.py:1031
  200.0 0.0 copy-start
  200.0 2.2 %copy.32 = bf16[512,768]{1,0:T(8,128)(2,1)} copy(bf16[512,768]{1,0:T(8,128)(2,1)} %get-tuple-element.40) | data formatting | bytes 1572864
  202.2 0.0 copy-done
  202.2 0.0 copy-start.3
  202.2 0.0 copy-start.8
  202.2 0.0 copy-start.4
  202.2 0.0 copy-start.1
  202.2 1.1 copy.33
  203.4 0.0 copy-done.3
  203.4 0.0 copy-start.7
  203.4 0.0 copy-start.2
  203.4 0.0 copy-start.6
  203.4 0.0 copy-start.5
  203.4 0.7 copy.34
  204.1 0.0 copy-done.8
  204.1 0.6 copy.35
  204.7 0.0 copy-done.4
  204.7 0.6 copy.36
  205.3 0.0 copy-done.1
  205.3 0.8 copy.37
  206.1 0.0 copy-done.7
  206.1 0.6 copy.38
  206.7 0.0 copy-done.2
  206.7 0.7 copy.39
  207.4 0.0 copy-done.6
  207.4 0.6 copy.40
  208.0 0.0 copy-done.5
  208.0 0.6 copy.41
Async XLA Ops:
  200.0 2.2 %copy-start = (f32[512,768]{1,0:T(8,128)S(1)}, f32[512,768]{1,0:T(8,128)}, u32[]{:S(2)}) copy-start(f32[512,768]{1,0:T(8,128)} %get-tuple-element.41) | copy-start | bytes 4718596
  202.2 1.2 copy-start.3
  202.2 1.9 copy-start.8
  202.2 2.4 %copy-start.4 = (f32[48,384]{1,0:T(8,128)S(1)}, f32[48,384]{1,0:T(8,128)}, u32[]{:S(2)}) copy-start(f32[48,384]{1,0:T(8,128)} %get-tuple-element.24) | copy-start | bytes 221188
  202.2 3.1 %copy-start.1 = (f32[2,48,1536]{2,1,0:T(8,128)S(1)}, f32[2,48,1536]{2,1,0:T(8,128)}, u32[]{:S(2)}) copy-start(f32[2,48,1536]{2,1,0:T(8,128)} %get-tuple-element.45) | copy-start | bytes 1769476
  203.4 2.7 %copy-start.7 = (f32[2,96]{1,0:T(2,128)S(1)}, f32[2,96]{1,0:T(2,128)}, u32[]{:S(2)}) copy-start(f32[2,96]{1,0:T(2,128)} %get-tuple-element.46) | copy-start | bytes 2308
  203.4 3.3 %copy-start.2 = (f32[48,1536]{1,0:T(8,128)S(1)}, f32[48,1536]{1,0:T(8,128)}, u32[]{:S(2)}) copy-start(f32[48,1536]{1,0:T(8,128)} %get-tuple-element.27) | copy-start | bytes 884740
  203.4 4.0 %copy-start.6 = (f32[2,24]{1,0:T(2,128)S(1)}, f32[2,24]{1,0:T(2,128)}, u32[]{:S(2)}) copy-start(f32[2,24]{1,0:T(2,128)} %get-tuple-element.48) | copy-start | bytes 580
  203.4 4.6 %copy-start.5 = (f32[4,24]{1,0:T(4,128)S(1)}, f32[4,24]{1,0:T(4,128)}, u32[]{:S(2)}) copy-start(f32[4,24]{1,0:T(4,128)} %get-tuple-element.49) | copy-start | bytes 1156

commit v6 on v5

--- a/solution.py
+++ b/solution.py
@@ -643,7 +643,7 @@
     project(mixed, w_out, side, to_attended)
     first_swap.wait()
     gain_one, gain_two = every_small[0:1, :], every_small[1:2, :]
-    step = 64
+    step = 128
 
     @pl.loop(0, half // step)
     def _(i):
@@ -870,7 +870,7 @@
                 qkv[r, cols] = jnp.where(block_lane < 64, qkv[r, cols], result) if upper else result
                 return inner_carry
 
-            lax.fori_loop(0, slots // block, attend_back, 0, unroll=2)
+            lax.fori_loop(0, slots // block, attend_back, 0, unroll=4)
             for j in range(slots // 512):
                 c = pl.ds(j * 512, 512)
                 grad_key_t[part, c] = nn(query_t[part, :], work[:, pl.ds(base + j * 512, 512)]).astype(bf16)

time: 212 us -> 207 us (0.976); the launches traced: 209 us -> 206 us
  Pallas kernels: 199 us -> 196 us
    pallas_call x1, Pallas kernels: 199 us -> 196 us  [layer_call(): pl.pallas_call(functools.partial(layer_body, grid, rows), out_shape=shape...]
where the time goes in v6:
time: 207 us; the launch traced here: 206 us
  Pallas kernels  196 us (95%)
  local copies, waits for them, and re-layouts  8.47 us (4%)
    pallas_call x1, Pallas kernels, layer_call(): pl.pallas_call(functools.partial(layer_body, grid, rows), out_shape=shape...  196 us
    unnamed x28, local copies, waits for them, and re-layouts  8.47 us

profile of v6, /device:TPU:0, one launch (start us, length us, event | category | flops | bytes accessed | tf_op | source)
XLA Modules:
  0.0 206.2 jit_solution(6650906347851244192)
XLA Ops:
  1.3 196.4 %layer.1 = (bf16[512,768]{1,0:T(8,128)(2,1)}, f32[512,768]{1,0:T(8,128)}, f32[3,48,384]{2,1,0:T(8,128)}, f32[48,384]{1,0:T(8,128)}, f32[2,48,1536]{2,1,0:T(8,128...) custom-call(bf16[512,768]{1,0:T(8,128)(2,1)} %tokens.1, ...), custom_call_target="tpu_custom_call" | custom-call | tf_op jit(solution)/shard_map/layer/pallas_call | solution.py:1031
  197.7 0.0 copy-start
  197.7 2.2 %copy.32 = bf16[512,768]{1,0:T(8,128)(2,1)} copy(bf16[512,768]{1,0:T(8,128)(2,1)} %get-tuple-element.40) | data formatting | bytes 1572864
  199.9 0.0 copy-done
  199.9 0.0 copy-start.3
  199.9 0.0 copy-start.8
  199.9 0.0 copy-start.4
  199.9 0.0 copy-start.1
  199.9 1.1 copy.33
  201.0 0.0 copy-done.3
  201.1 0.0 copy-start.7
  201.1 0.0 copy-start.2
  201.1 0.0 copy-start.6
  201.1 0.0 copy-start.5
  201.1 0.7 copy.34
  201.8 0.0 copy-done.8
  201.8 0.6 copy.35
  202.3 0.0 copy-done.4
  202.3 0.6 copy.36
  203.0 0.0 copy-done.1
  203.0 0.8 copy.37
  203.8 0.0 copy-done.7
  203.8 0.6 copy.38
  204.3 0.0 copy-done.2
  204.3 0.7 copy.39
  205.1 0.0 copy-done.6
  205.1 0.6 copy.40
  205.6 0.0 copy-done.5
  205.6 0.6 copy.41
Async XLA Ops:
  197.7 2.2 %copy-start = (f32[512,768]{1,0:T(8,128)S(1)}, f32[512,768]{1,0:T(8,128)}, u32[]{:S(2)}) copy-start(f32[512,768]{1,0:T(8,128)} %get-tuple-element.41) | copy-start | bytes 4718596
  199.9 1.2 copy-start.3
  199.9 1.9 copy-start.8
  199.9 2.4 %copy-start.4 = (f32[48,384]{1,0:T(8,128)S(1)}, f32[48,384]{1,0:T(8,128)}, u32[]{:S(2)}) copy-start(f32[48,384]{1,0:T(8,128)} %get-tuple-element.24) | copy-start | bytes 221188
  199.9 3.1 %copy-start.1 = (f32[2,48,1536]{2,1,0:T(8,128)S(1)}, f32[2,48,1536]{2,1,0:T(8,128)}, u32[]{:S(2)}) copy-start(f32[2,48,1536]{2,1,0:T(8,128)} %get-tuple-element.45) | copy-start | bytes 1769476
  201.1 2.7 %copy-start.7 = (f32[2,96]{1,0:T(2,128)S(1)}, f32[2,96]{1,0:T(2,128)}, u32[]{:S(2)}) copy-start(f32[2,96]{1,0:T(2,128)} %get-tuple-element.46) | copy-start | bytes 2308
  201.1 3.3 %copy-start.2 = (f32[48,1536]{1,0:T(8,128)S(1)}, f32[48,1536]{1,0:T(8,128)}, u32[]{:S(2)}) copy-start(f32[48,1536]{1,0:T(8,128)} %get-tuple-element.27) | copy-start | bytes 884740
  201.1 4.0 %copy-start.6 = (f32[2,24]{1,0:T(2,128)S(1)}, f32[2,24]{1,0:T(2,128)}, u32[]{:S(2)}) copy-start(f32[2,24]{1,0:T(2,128)} %get-tuple-element.48) | copy-start | bytes 580
  201.1 4.6 %copy-start.5 = (f32[4,24]{1,0:T(4,128)S(1)}, f32[4,24]{1,0:T(4,128)}, u32[]{:S(2)}) copy-start(f32[4,24]{1,0:T(4,128)} %get-tuple-element.49) | copy-start | bytes 1156
